TPU v7x, 32 devices: a whole 2x2x4 slice. The times are simulated.
32 devices in a mesh: dp: 8 (over y, x, core), tensor: 4 (over z).
Axes of the slice: x: 2, y: 2, z: 4, core: 2. Of those that a mesh axis runs over, the one named last changes fastest.
Arguments:
- block_input: bfloat16 [8192, 2048], P(('dp', 'tensor')), may hold values from -60 to 60
- gain_attn: float32 [2048], P(('dp', 'tensor')), may hold values from 0.1 to 1.9
- gain_mlp: float32 [2048], P(('dp', 'tensor')), may hold values from 0.1 to 1.9
- w_query: bfloat16 [2048, 2048], P('dp', 'tensor'), may hold values from -4 to 4
- key_projection_weight: bfloat16 [2048, 256], P('dp', 'tensor'), may hold values from -0.125 to 0.125
- value_projection_weight: bfloat16 [2048, 256], P('dp', 'tensor'), may hold values from -0.125 to 0.125
- w_out: bfloat16 [2048, 2048], P('tensor', 'dp'), may hold values from -0.75 to 0.75
- w_gate: bfloat16 [2048, 5632], P('dp', 'tensor'), may hold values from -0.125 to 0.125
- w_up: bfloat16 [2048, 5632], P('dp', 'tensor'), may hold values from -0.125 to 0.125
- w_down: bfloat16 [5632, 2048], P('tensor', 'dp'), may hold values from -0.078125 to 0.078125
- cotangent: bfloat16 [8192, 2048], P(('dp', 'tensor')), may hold values from -6 to 6
Outputs:
- block_output: bfloat16 [8192, 2048], P(('dp', 'tensor'))
- input_grad: bfloat16 [8192, 2048], P(('dp', 'tensor'))
- grad_gain_attn: float32 [2048], P(('dp', 'tensor'))
- grad_gain_mlp: float32 [2048], P(('dp', 'tensor'))
- grad_query: float32 [2048, 2048], P('dp', 'tensor')
- grad_key: float32 [2048, 256], P('dp', 'tensor')
- grad_value: float32 [2048, 256], P('dp', 'tensor')
- grad_out: float32 [2048, 2048], P('tensor', 'dp')
- grad_gate: float32 [2048, 5632], P('dp', 'tensor')
- grad_up: float32 [2048, 5632], P('dp', 'tensor')
- grad_down: float32 [5632, 2048], P('tensor', 'dp')
All inputs are finite; a program needn't handle non-finite values.
Results may differ from a plain program's by a relative error of at most 0.025.
The roundings to bfloat16 on the way count: a program that leaves them out, or rounds other values in their place, can miss the bound.
Values may be sent and summed in bfloat16 or wider, within the bound.
A program may use at most 256 MiB of HBM per device.

v0:
```python
import math

import jax
import jax.numpy as jnp
from jax import lax
from jax.sharding import PartitionSpec as P

HEAD_SIZE = 64


EPS = 1e-05
ROPE_BASE = 10000.0
NEG_LARGE = -1e30


def rope_tables(sequence_length, head_dim):
    half_dim = head_dim // 2
    frequency = ROPE_BASE ** (-(jnp.arange(half_dim, dtype=jnp.float32) * 2.0) / head_dim)
    angles = jnp.arange(sequence_length, dtype=jnp.float32)[:, None] * frequency[None, :]
    return (jnp.cos(angles)[:, None, :], jnp.sin(angles)[:, None, :])


def apply_rotary(tensor, cosine_lookup, sine_lookup):
    half_dim = tensor.shape[-1] // 2
    lower_half = tensor[..., :half_dim]
    upper_half = tensor[..., half_dim:]
    return jnp.concatenate(
        [
            lower_half * cosine_lookup - upper_half * sine_lookup,
            upper_half * cosine_lookup + lower_half * sine_lookup,
        ],
        axis=-1,
    )


def invert_rotary(tensor, cosine_lookup, sine_lookup):
    half_dim = tensor.shape[-1] // 2
    lower_half = tensor[..., :half_dim]
    upper_half = tensor[..., half_dim:]
    return jnp.concatenate(
        [
            lower_half * cosine_lookup + upper_half * sine_lookup,
            upper_half * cosine_lookup - lower_half * sine_lookup,
        ],
        axis=-1,
    )


def causal_scores(query_block, keys_seen, first_row, score_scale):
    block_rows, q_heads, head_dim = query_block.shape
    kv_heads = keys_seen.shape[1]
    grouped = query_block.reshape(block_rows, kv_heads, q_heads // kv_heads, head_dim)
    scores = (
        jnp.einsum("qhgd,khd->hgqk", grouped, keys_seen, preferred_element_type=jnp.float32)
        * score_scale
    )
    row_pos = first_row + jnp.arange(block_rows)[:, None]
    col_pos = jnp.arange(keys_seen.shape[0])[None, :]
    return (jnp.where(col_pos <= row_pos, scores, NEG_LARGE), grouped)


def attend(queries, key_rows, value_rows):
    sequence_length, q_heads, head_dim = queries.shape
    block_rows = min(512, sequence_length)
    score_scale = 1.0 / math.sqrt(head_dim)
    outputs = []
    totals = []
    for first_row in range(0, sequence_length, block_rows):
        last_row = first_row + block_rows
        scores, grouped = causal_scores(
            queries[first_row:last_row], key_rows[:last_row], first_row, score_scale
        )
        peak = jnp.max(scores, axis=-1, keepdims=True)
        log_total = peak + jnp.log(jnp.sum(jnp.exp(scores - peak), axis=-1, keepdims=True))
        weights = jnp.exp(scores - log_total).astype(jnp.bfloat16)
        mixed = jnp.einsum(
            "hgqk,khd->qhgd", weights, value_rows[:last_row], preferred_element_type=jnp.float32
        )
        outputs.append(mixed.reshape(block_rows, q_heads, head_dim).astype(jnp.bfloat16))
        totals.append(log_total[..., 0])
    return (jnp.concatenate(outputs, axis=0), jnp.concatenate(totals, axis=2))


def attend_back(queries, key_rows, value_rows, outputs, log_totals, grad_outputs):
    sequence_length, q_heads, head_dim = queries.shape
    kv_heads = key_rows.shape[1]
    block_rows = min(512, sequence_length)
    score_scale = 1.0 / math.sqrt(head_dim)
    grad_keys = jnp.zeros(key_rows.shape, jnp.float32)
    grad_values = jnp.zeros(value_rows.shape, jnp.float32)
    query_parts = []
    for first_row in range(0, sequence_length, block_rows):
        last_row = first_row + block_rows
        scores, grouped = causal_scores(
            queries[first_row:last_row], key_rows[:last_row], first_row, score_scale
        )
        probs = jnp.exp(scores - log_totals[:, :, first_row:last_row, None])
        weights = probs.astype(jnp.bfloat16)
        grad_block = grad_outputs[first_row:last_row].reshape(
            block_rows, kv_heads, q_heads // kv_heads, head_dim
        )
        out_block = outputs[first_row:last_row].reshape(
            block_rows, kv_heads, q_heads // kv_heads, head_dim
        )
        grad_values = grad_values.at[:last_row].add(
            jnp.einsum("hgqk,qhgd->khd", weights, grad_block, preferred_element_type=jnp.float32)
        )
        grad_probs = jnp.einsum(
            "qhgd,khd->hgqk", grad_block, value_rows[:last_row], preferred_element_type=jnp.float32
        )
        delta = jnp.einsum(
            "qhgd,qhgd->hgq", grad_block, out_block, preferred_element_type=jnp.float32
        )
        grad_scores = (probs * (grad_probs - delta[..., None]) * score_scale).astype(jnp.bfloat16)
        query_parts.append(
            jnp.einsum(
                "hgqk,khd->qhgd",
                grad_scores,
                key_rows[:last_row],
                preferred_element_type=jnp.float32,
            ).reshape(block_rows, q_heads, head_dim)
        )
        grad_keys = grad_keys.at[:last_row].add(
            jnp.einsum("hgqk,qhgd->khd", grad_scores, grouped, preferred_element_type=jnp.float32)
        )
    return (jnp.concatenate(query_parts, axis=0), grad_keys, grad_values)


def fetch_attention(w_query, key_projection_weight, value_projection_weight, w_out):
    return (
        lax.all_gather(w_query, "dp", axis=0, tiled=True),
        lax.all_gather(key_projection_weight, "dp", axis=0, tiled=True),
        lax.all_gather(value_projection_weight, "dp", axis=0, tiled=True),
        lax.all_gather(w_out, "dp", axis=1, tiled=True),
    )


def fetch_mlp(w_gate, w_up, w_down):
    return (
        lax.all_gather(w_gate, "dp", axis=0, tiled=True),
        lax.all_gather(w_up, "dp", axis=0, tiled=True),
        lax.all_gather(w_down, "dp", axis=1, tiled=True),
    )


def gather_rows(normed):
    return lax.all_gather(normed, "tensor", axis=0, tiled=True)


def scatter_rows(partial_sums):
    return lax.psum_scatter(
        partial_sums.astype(jnp.bfloat16), "tensor", scatter_dimension=0, tiled=True
    ).astype(jnp.float32)


def gather_grads(grad_rows):
    return lax.all_gather(grad_rows, "tensor", axis=0, tiled=True)


def scatter_grads(partial_grads):
    return lax.psum_scatter(
        partial_grads.astype(jnp.bfloat16), "tensor", scatter_dimension=0, tiled=True
    ).astype(jnp.float32)


def dot_float(left, right):
    return jnp.dot(left, right, preferred_element_type=jnp.float32)


def local(
    block_input,
    gain_attn,
    gain_mlp,
    w_query,
    key_projection_weight,
    value_projection_weight,
    w_out,
    w_gate,
    w_up,
    w_down,
    cotangent,
):
    full_gain_attn, full_gain_mlp = (
        lax.all_gather(gain_attn, ("dp", "tensor"), axis=0, tiled=True),
        lax.all_gather(gain_mlp, ("dp", "tensor"), axis=0, tiled=True),
    )
    query_all, key_all, value_all, out_all = fetch_attention(
        w_query, key_projection_weight, value_projection_weight, w_out
    )
    xfloat = block_input.astype(jnp.float32)
    inv_rms_attn = lax.rsqrt(jnp.mean(xfloat * xfloat, axis=1, keepdims=True) + EPS)
    attention_norm = (xfloat * inv_rms_attn * full_gain_attn).astype(jnp.bfloat16)
    norm_attn_seq = gather_rows(attention_norm)
    sequence_length = norm_attn_seq.shape[0]
    q_heads = query_all.shape[1] // HEAD_SIZE
    kv_heads = key_all.shape[1] // HEAD_SIZE
    cosine_lookup, sine_lookup = rope_tables(sequence_length, HEAD_SIZE)
    queries = apply_rotary(
        dot_float(norm_attn_seq, query_all).reshape(sequence_length, q_heads, HEAD_SIZE),
        cosine_lookup,
        sine_lookup,
    ).astype(jnp.bfloat16)
    key_rows = apply_rotary(
        dot_float(norm_attn_seq, key_all).reshape(sequence_length, kv_heads, HEAD_SIZE),
        cosine_lookup,
        sine_lookup,
    ).astype(jnp.bfloat16)
    value_rows = (
        dot_float(norm_attn_seq, value_all)
        .astype(jnp.bfloat16)
        .reshape(sequence_length, kv_heads, HEAD_SIZE)
    )
    attended, log_totals = attend(queries, key_rows, value_rows)
    attended_flat = attended.reshape(sequence_length, q_heads * HEAD_SIZE)
    mid = xfloat + scatter_rows(dot_float(attended_flat, out_all))
    inv_rms_mlp = lax.rsqrt(jnp.mean(mid * mid, axis=1, keepdims=True) + EPS)
    norm_mlp = (mid * inv_rms_mlp * full_gain_mlp).astype(jnp.bfloat16)
    norm_mlp_seq = gather_rows(norm_mlp)
    gate_all, up_all, down_all = fetch_mlp(w_gate, w_up, w_down)
    gate_act = dot_float(norm_mlp_seq, gate_all)
    up_act = dot_float(norm_mlp_seq, up_all)
    sigmoid_gate = jax.nn.sigmoid(gate_act)
    hidden = (gate_act * sigmoid_gate * up_act).astype(jnp.bfloat16)
    block_output = (mid + scatter_rows(dot_float(hidden, down_all))).astype(jnp.bfloat16)
    gate_back, up_back, down_back = fetch_mlp(w_gate, w_up, w_down)
    query_back, key_back, value_back, out_back = fetch_attention(
        w_query, key_projection_weight, value_projection_weight, w_out
    )
    cotangent_seq = gather_grads(cotangent)
    grad_down = dot_float(hidden.T, cotangent_seq)
    grad_hidden = dot_float(cotangent_seq, down_back.T)
    grad_gate_act = (
        grad_hidden * up_act * sigmoid_gate * (1.0 + gate_act * (1.0 - sigmoid_gate))
    ).astype(jnp.bfloat16)
    grad_up_act = (grad_hidden * gate_act * sigmoid_gate).astype(jnp.bfloat16)
    grad_gate = dot_float(norm_mlp_seq.T, grad_gate_act)
    grad_up = dot_float(norm_mlp_seq.T, grad_up_act)
    grad_norm_mlp = scatter_grads(
        dot_float(grad_gate_act, gate_back.T) + dot_float(grad_up_act, up_back.T)
    )
    grad_gate, grad_up, grad_down = (
        lax.psum_scatter(
            grad_gate.astype(jnp.bfloat16), "dp", scatter_dimension=0, tiled=True
        ).astype(jnp.float32),
        lax.psum_scatter(
            grad_up.astype(jnp.bfloat16), "dp", scatter_dimension=0, tiled=True
        ).astype(jnp.float32),
        lax.psum_scatter(
            grad_down.astype(jnp.bfloat16), "dp", scatter_dimension=1, tiled=True
        ).astype(jnp.float32),
    )
    partial_gain_mlp = jnp.sum(grad_norm_mlp * mid * inv_rms_mlp, axis=0)
    scaled_mlp = grad_norm_mlp * full_gain_mlp
    grad_mid = cotangent.astype(jnp.float32) + inv_rms_mlp * (
        scaled_mlp
        - mid * inv_rms_mlp * inv_rms_mlp * jnp.mean(scaled_mlp * mid, axis=1, keepdims=True)
    )
    grad_mid_seq = gather_grads(grad_mid.astype(jnp.bfloat16))
    grad_out = dot_float(attended_flat.T, grad_mid_seq)
    grad_attended = (
        dot_float(grad_mid_seq, out_back.T)
        .astype(jnp.bfloat16)
        .reshape(sequence_length, q_heads, HEAD_SIZE)
    )
    grad_q, grad_key_rows, grad_value_rows = attend_back(
        queries, key_rows, value_rows, attended, log_totals, grad_attended
    )
    grad_queries_act = (
        invert_rotary(grad_q, cosine_lookup, sine_lookup)
        .astype(jnp.bfloat16)
        .reshape(sequence_length, q_heads * HEAD_SIZE)
    )
    grad_keys_rotated = (
        invert_rotary(grad_key_rows, cosine_lookup, sine_lookup)
        .astype(jnp.bfloat16)
        .reshape(sequence_length, kv_heads * HEAD_SIZE)
    )
    grad_values_projected = grad_value_rows.astype(jnp.bfloat16).reshape(
        sequence_length, kv_heads * HEAD_SIZE
    )
    grad_query = dot_float(norm_attn_seq.T, grad_queries_act)
    grad_key = dot_float(norm_attn_seq.T, grad_keys_rotated)
    grad_value = dot_float(norm_attn_seq.T, grad_values_projected)
    grad_norm_attn = scatter_grads(
        dot_float(grad_queries_act, query_back.T)
        + dot_float(grad_keys_rotated, key_back.T)
        + dot_float(grad_values_projected, value_back.T)
    )
    grad_query, grad_key, grad_value, grad_out = (
        lax.psum_scatter(
            grad_query.astype(jnp.bfloat16), "dp", scatter_dimension=0, tiled=True
        ).astype(jnp.float32),
        lax.psum_scatter(
            grad_key.astype(jnp.bfloat16), "dp", scatter_dimension=0, tiled=True
        ).astype(jnp.float32),
        lax.psum_scatter(
            grad_value.astype(jnp.bfloat16), "dp", scatter_dimension=0, tiled=True
        ).astype(jnp.float32),
        lax.psum_scatter(
            grad_out.astype(jnp.bfloat16), "dp", scatter_dimension=1, tiled=True
        ).astype(jnp.float32),
    )
    partial_gain_attn = jnp.sum(grad_norm_attn * xfloat * inv_rms_attn, axis=0)
    scaled_attn = grad_norm_attn * full_gain_attn
    input_grad = (
        grad_mid
        + inv_rms_attn
        * (
            scaled_attn
            - xfloat
            * inv_rms_attn
            * inv_rms_attn
            * jnp.mean(scaled_attn * xfloat, axis=1, keepdims=True)
        )
    ).astype(jnp.bfloat16)
    grad_gain_attn, grad_gain_mlp = (
        lax.psum_scatter(partial_gain_attn, ("dp", "tensor"), scatter_dimension=0, tiled=True),
        lax.psum_scatter(partial_gain_mlp, ("dp", "tensor"), scatter_dimension=0, tiled=True),
    )
    return (
        block_output,
        input_grad,
        grad_gain_attn,
        grad_gain_mlp,
        grad_query,
        grad_key,
        grad_value,
        grad_out,
        grad_gate,
        grad_up,
        grad_down,
    )


def solution(mesh):
    in_specs = (
        P(("dp", "tensor"), None),
        P(("dp", "tensor")),
        P(("dp", "tensor")),
        P("dp", "tensor"),
        P("dp", "tensor"),
        P("dp", "tensor"),
        P("tensor", "dp"),
        P("dp", "tensor"),
        P("dp", "tensor"),
        P("tensor", "dp"),
        P(("dp", "tensor"), None),
    )
    out_specs = (
        P(("dp", "tensor"), None),
        P(("dp", "tensor"), None),
        P(("dp", "tensor")),
        P(("dp", "tensor")),
        P("dp", "tensor"),
        P("dp", "tensor"),
        P("dp", "tensor"),
        P("tensor", "dp"),
        P("dp", "tensor"),
        P("dp", "tensor"),
        P("tensor", "dp"),
    )
    return jax.shard_map(local, mesh=mesh, in_specs=in_specs, out_specs=out_specs, check_vma=False)
```

profile of v0, /device:TPU:0, one launch (start us, length us, event | category | flops | bytes accessed | tf_op | source)
XLA Modules:
  0.0 1307.3 jit_solution(5801263813330568736)
XLA Ops:
  10.5 42.1 %all-reduce.7 = (f32[2048]{0:T(1024)S(1)}, f32[2048]{0:T(1024)S(1)}) all-reduce(f32[2048]{0:T(1024)S(1)} %dynamic-update-slice.10, f32[2048]{0:T(1024)S(1)} %dynamic-update-slice.11), channel_id=1, replica_groups=mesh['dp'=8,'tensor'=4] {'dp','tensor'}, use_global_device_ids=true, to_apply=%add.2 | all-reduce | flops 4096 | bytes 32768
  57.4 10.6 all_gather.49
  77.3 58.5 %all-gather.10.cloned.1.call-done = bf16[1024,2048]{1,0:T(8,128)(2,1)} async-done(((bf16[256,2048]{1,0:T(8,128)(2,1)}), bf16[1024,2048]{1,0:T(8,128)(2,1)}) %all-gather.10.cloned.1.call-update) | async-done | bytes 4194320 | tf_op jit(solution)/shard_map/all_gather | solution.py:147
  140.1 24.0 %all-gather.12.cloned.1.call-done = bf16[2048,512]{1,0:T(8,128)(2,1)} async-done(((bf16[256,512]{1,0:T(8,128)(2,1)}), bf16[2048,512]{1,0:T(8,128)(2,1)}) %all-gather.12.cloned.1.call-update) | async-done | bytes 2097168 | tf_op jit(solution)/shard_map/all_gather | solution.py:131
  177.6 9.2 exponential_reduce_fusion
  213.3 76.4 %reduce-scatter.12.cloned.1.call-done = bf16[256,2048]{1,0:T(8,128)(2,1)} async-done(((bf16[1024,2048]{1,0:T(8,128)(2,1)}), bf16[256,2048]{1,0:T(8,128)(2,1)}) %reduce-scatter.12.cloned.1.call-update) | async-done | bytes 1048592 | tf_op jit(solution)/shard_map/reduce_scatter | solution.py:151
  296.9 38.3 %all-gather.18.cloned.1.call-done = bf16[2048,1408]{1,0:T(8,128)(2,1)} async-done(((bf16[256,1408]{1,0:T(8,128)(2,1)}), bf16[2048,1408]{1,0:T(8,128)(2,1)}) %all-gather.18.cloned.1.call-update) | async-done | bytes 5767184 | tf_op jit(solution)/shard_map/all_gather | solution.py:140
  335.2 82.8 %all-gather.16.cloned.1.call-done = bf16[1024,2048]{1,0:T(8,128)(2,1)} async-done(((bf16[256,2048]{1,0:T(8,128)(2,1)}), bf16[1024,2048]{1,0:T(8,128)(2,1)}) %all-gather.16.cloned.1.call-update) | async-done | bytes 4194320 | tf_op jit(solution)/shard_map/all_gather | solution.py:147
  418.0 11.8 fusion.83
  429.8 31.8 %all-gather.20.cloned.1.call-done = bf16[2048,1408]{1,0:T(8,128)(2,1)} async-done(((bf16[256,1408]{1,0:T(8,128)(2,1)}), bf16[2048,1408]{1,0:T(8,128)(2,1)}) %all-gather.20.cloned.1.call-update) | async-done | bytes 5767184 | tf_op jit(solution)/shard_map/all_gather | solution.py:141
  461.6 11.7 fusion.84
  473.3 70.6 %all-gather.24.cloned.1.call-done = bf16[1024,2048]{1,0:T(8,128)(2,1)} async-done(((bf16[256,2048]{1,0:T(8,128)(2,1)}), bf16[1024,2048]{1,0:T(8,128)(2,1)}) %all-gather.24.cloned.1.call-update) | async-done | bytes 4194320 | tf_op jit(solution)/shard_map/all_gather | solution.py:157
  543.9 44.7 %all-gather.22.cloned.1.call-done = bf16[1408,2048]{1,0:T(8,128)(2,1)} async-done(((bf16[1408,256]{1,0:T(8,128)(2,1)}), bf16[1408,2048]{1,0:T(8,128)(2,1)}) %all-gather.22.cloned.1.call-update) | async-done | bytes 5767184 | tf_op jit(solution)/shard_map/all_gather | solution.py:142
  588.6 15.7 %multiply_convert_fusion = (bf16[1024,1408]{1,0:T(8,128)(2,1)S(1)}, bf16[1024,1408]{1,0:T(8,128)(2,1)S(1)}, bf16[1024,1408]{1,0:T(8,128)(2,1)}) fusion(f32[1024,1408]{1,0:T(8,128)} %fusion.83, f32[1024,1408]{1,0:T(8,128)} %fusion.84, bf16[1024,2048]{1,0:T(8,128)(2,1)} %all-gather.24.cloned.1.call-done, bf16[1408,2048]{1,0:T(8,128)(2,1)} %all-gather.22.cloned.1.call-done), kind=kOutput, calls=%fused_computation.27 | convolution fusion | flops 5928648704 | bytes 30146560 | tf_op jit(solution)/shard_map/dot_general | solution.py:167
  604.2 10.9 fusion.85
  623.8 76.7 %reduce-scatter.16.cloned.1.call-done = bf16[256,2048]{1,0:T(8,128)(2,1)} async-done(((bf16[1024,2048]{1,0:T(8,128)(2,1)}), bf16[256,2048]{1,0:T(8,128)(2,1)}) %reduce-scatter.16.cloned.1.call-update) | async-done | bytes 1048592 | tf_op jit(solution)/shard_map/reduce_scatter | solution.py:161
  706.3 11.0 convolution_convert_fusion.2
  717.4 11.0 convolution_convert_fusion.1
  728.4 10.5 convolution_convert_fusion
  739.4 48.2 %all-gather.26.cloned.1.call-done = bf16[1024,2048]{1,0:T(8,128)(2,1)} async-done(((bf16[256,2048]{1,0:T(8,128)(2,1)}), bf16[1024,2048]{1,0:T(8,128)(2,1)}) %all-gather.26.cloned.1.call-update) | async-done | bytes 4194320 | tf_op jit(solution)/shard_map/all_gather | solution.py:157
  804.0 9.6 fusion.2
  828.5 10.4 fusion.47
  869.9 10.9 convolution_convert_fusion.3
  883.2 27.8 %reduce-scatter.30.cloned.1.call-done = bf16[256,1408]{1,0:T(8,128)(2,1)} async-done(((bf16[2048,1408]{1,0:T(8,128)(2,1)}), bf16[256,1408]{1,0:T(8,128)(2,1)}) %reduce-scatter.30.cloned.1.call-update) | async-done | bytes 720912 | tf_op jit(solution)/shard_map/reduce_scatter | solution.py:245
  913.3 59.9 %reduce-scatter.32.cloned.1.call-done = bf16[1408,256]{1,0:T(8,128)(2,1)} async-done(((bf16[1408,2048]{1,0:T(8,128)(2,1)}), bf16[1408,256]{1,0:T(8,128)(2,1)}) %reduce-scatter.32.cloned.1.call-update) | async-done | bytes 720912 | tf_op jit(solution)/shard_map/reduce_scatter | solution.py:248
  975.6 34.3 %reduce-scatter.22.cloned.1.call-done = bf16[256,64]{0,1:T(8,128)(2,1)} async-done(((bf16[2048,64]{0,1:T(8,128)(2,1)}), bf16[256,64]{0,1:T(8,128)(2,1)}) %reduce-scatter.22.cloned.1.call-update) | async-done | bytes 32784 | tf_op jit(solution)/shard_map/reduce_scatter | solution.py:293
  1011.2 35.8 %reduce-scatter.24.cloned.1.call-done = bf16[256,64]{0,1:T(8,128)(2,1)} async-done(((bf16[2048,64]{0,1:T(8,128)(2,1)}), bf16[256,64]{0,1:T(8,128)(2,1)}) %reduce-scatter.24.cloned.1.call-update) | async-done | bytes 32784 | tf_op jit(solution)/shard_map/reduce_scatter | solution.py:296
  1048.4 42.9 %reduce-scatter.26.cloned.1.call-done = bf16[512,256]{1,0:T(8,128)(2,1)} async-done(((bf16[512,2048]{1,0:T(8,128)(2,1)}), bf16[512,256]{1,0:T(8,128)(2,1)}) %reduce-scatter.26.cloned.1.call-update) | async-done | bytes 262160 | tf_op jit(solution)/shard_map/reduce_scatter | solution.py:299
  1093.1 42.5 %reduce-scatter.20.cloned.1.call-done = bf16[256,512]{1,0:T(8,128)(2,1)} async-done(((bf16[2048,512]{1,0:T(8,128)(2,1)}), bf16[256,512]{1,0:T(8,128)(2,1)}) %reduce-scatter.20.cloned.1.call-update) | async-done | bytes 262160 | tf_op jit(solution)/shard_map/reduce_scatter | solution.py:290
  1137.4 77.3 %reduce-scatter.18.cloned.1.call-done = bf16[256,2048]{1,0:T(8,128)(2,1)} async-done(((bf16[1024,2048]{1,0:T(8,128)(2,1)}), bf16[256,2048]{1,0:T(8,128)(2,1)}) %reduce-scatter.18.cloned.1.call-update) | async-done | bytes 1048592 | tf_op jit(solution)/shard_map/reduce_scatter | solution.py:161
  1216.6 43.1 %all-reduce.6 = (f32[2048]{0:T(1024)S(1)}, f32[2048]{0:T(1024)S(1)}) all-reduce(f32[2048]{0:T(1024)S(1)} %get-tuple-element.77, f32[2048]{0:T(1024)S(1)} %get-tuple-element.75), channel_id=6, replica_groups=mesh['dp'=8,'tensor'=4] {'dp','tensor'}, use_global_device_ids=true, to_apply=%region_13.14.clone | all-reduce | flops 4096 | bytes 32768
  1260.9 34.4 %reduce-scatter.14.cloned.1.call-done = bf16[256,2048]{1,0:T(8,128)(2,1)} async-done(((bf16[1024,2048]{1,0:T(8,128)(2,1)}), bf16[256,2048]{1,0:T(8,128)(2,1)}) %reduce-scatter.14.cloned.1.call-update) | async-done | bytes 1048592 | tf_op jit(solution)/shard_map/reduce_scatter | solution.py:151
  (224 shorter events, 166.5 us)
Async XLA Ops:
  7.2 128.7 %all-gather.10.cloned.1.call-start = ((), (), s32[]{:S(2)}) async-start(), calls=%async_computation.11 | async-start | bytes 5242880 | tf_op jit(solution)/shard_map/all_gather | solution.py:147
  8.8 130.7 %copy-start.45 = (f32[256]{0:T(256)}, f32[256]{0:T(256)S(1)}, u32[]{:S(2)}) copy-start(f32[256]{0:T(256)S(1)} %add_rsqrt_fusion.1) | copy-start | bytes 3076
  55.2 108.9 %all-gather.12.cloned.1.call-start = ((), (), s32[]{:S(2)}) async-start(), calls=%async_computation.12 | async-start | bytes 2359296 | tf_op jit(solution)/shard_map/all_gather | solution.py:131
  55.9 149.9 %all-gather.14.cloned.1.call-start = ((), (), s32[]{:S(2)}) async-start(), calls=%async_computation.13 | async-start | bytes 2359296 | tf_op jit(solution)/shard_map/all_gather | solution.py:134
  56.6 233.1 %reduce-scatter.12.cloned.1.call-start = ((), (), s32[]{:S(2)}) async-start(), calls=%async_computation.14 | async-start | bytes 5242880 | tf_op jit(solution)/shard_map/reduce_scatter | solution.py:151
  56.7 112.6 %copy-start.49 = (f32[32]{0:T(128)}, f32[32]{0:T(128)S(1)}, u32[]{:S(2)}) copy-start(f32[32]{0:T(128)S(1)} %multiply_power_fusion) | copy-start | bytes 388
  57.4 112.0 %copy-start.19 = (f32[1024,32]{0,1:T(8,128)}, f32[1024,32]{0,1:T(8,128)S(1)}, u32[]{:S(2)}) copy-start(f32[1024,32]{0,1:T(8,128)S(1)} %get-tuple-element.102) | copy-start | bytes 393220
  57.4 112.0 %copy-start.21 = (f32[1024,32]{0,1:T(8,128)}, f32[1024,32]{0,1:T(8,128)S(1)}, u32[]{:S(2)}) copy-start(f32[1024,32]{0,1:T(8,128)S(1)} %get-tuple-element.103) | copy-start | bytes 393220
  68.0 101.3 %copy-start.15 = (bf16[2048,64]{0,1:T(8,128)(2,1)}, bf16[2048,64]{0,1:T(8,128)(2,1)S(1)}, u32[]{:S(2)}) copy-start(bf16[2048,64]{0,1:T(8,128)(2,1)S(1)} %all_gather.49) | copy-start | bytes 786436
  68.4 132.6 %copy-start.14 = (pred[512,1024]{0,1:T(8,128)(4,1)}, pred[512,1024]{0,1:T(8,128)(4,1)S(1)}, u32[]{:S(2)}) copy-start(pred[512,1024]{0,1:T(8,128)(4,1)S(1)} %iota_compare_fusion) | copy-start | bytes 1572868
  77.3 115.2 %copy-start.17 = (bf16[2048,64]{0,1:T(8,128)(2,1)}, bf16[2048,64]{0,1:T(8,128)(2,1)S(1)}, u32[]{:S(2)}) copy-start(bf16[2048,64]{0,1:T(8,128)(2,1)S(1)} %all_gather.48) | copy-start | bytes 786436
  212.7 122.5 %all-gather.18.cloned.1.call-start = ((), (), s32[]{:S(2)}) async-start(), calls=%async_computation.16 | async-start | bytes 6488064 | tf_op jit(solution)/shard_map/all_gather | solution.py:140
  213.3 204.7 %all-gather.16.cloned.1.call-start = ((), (), s32[]{:S(2)}) async-start(), calls=%async_computation.15 | async-start | bytes 5242880 | tf_op jit(solution)/shard_map/all_gather | solution.py:147
  294.6 167.0 %all-gather.20.cloned.1.call-start = ((), (), s32[]{:S(2)}) async-start(), calls=%async_computation.17 | async-start | bytes 6488064 | tf_op jit(solution)/shard_map/all_gather | solution.py:141
  295.4 248.6 %all-gather.24.cloned.1.call-start = ((), (), s32[]{:S(2)}) async-start(), calls=%async_computation.20 | async-start | bytes 5242880 | tf_op jit(solution)/shard_map/all_gather | solution.py:157
  296.1 292.5 %all-gather.22.cloned.1.call-start = ((), (), s32[]{:S(2)}) async-start(), calls=%async_computation.18 | async-start | bytes 6488064 | tf_op jit(solution)/shard_map/all_gather | solution.py:142
  296.8 403.7 %reduce-scatter.16.cloned.1.call-start = ((), (), s32[]{:S(2)}) async-start(), calls=%async_computation.21 | async-start | bytes 5242880 | tf_op jit(solution)/shard_map/reduce_scatter | solution.py:161
  623.5 79.5 %copy-start.8 = (bf16[256,2048]{1,0:T(8,128)(2,1)S(1)}, bf16[256,2048]{1,0:T(8,128)(2,1)}, u32[]{:S(2)}) copy-start(bf16[256,2048]{1,0:T(8,128)(2,1)} %param.33) | copy-start | bytes 3145732
  623.5 164.1 %all-gather.26.cloned.1.call-start = ((), (), s32[]{:S(2)}) async-start(), calls=%async_computation.22 | async-start | bytes 5242880 | tf_op jit(solution)/shard_map/all_gather | solution.py:157
  706.2 174.6 %reduce-scatter.28.cloned.1.call-start = ((), (), s32[]{:S(2)}) async-start(), calls=%async_computation.28 | async-start | bytes 6488064 | tf_op jit(solution)/shard_map/reduce_scatter | solution.py:242
  717.3 193.7 %reduce-scatter.30.cloned.1.call-start = ((), (), s32[]{:S(2)}) async-start(), calls=%async_computation.29 | async-start | bytes 6488064 | tf_op jit(solution)/shard_map/reduce_scatter | solution.py:245
  728.4 244.9 %reduce-scatter.32.cloned.1.call-start = ((), (), s32[]{:S(2)}) async-start(), calls=%async_computation.30 | async-start | bytes 6488064 | tf_op jit(solution)/shard_map/reduce_scatter | solution.py:248
  738.9 270.9 %reduce-scatter.22.cloned.1.call-start = ((), (), s32[]{:S(2)}) async-start(), calls=%async_computation.25 | async-start | bytes 294912 | tf_op jit(solution)/shard_map/reduce_scatter | solution.py:293
  828.3 218.7 %reduce-scatter.24.cloned.1.call-start = ((), (), s32[]{:S(2)}) async-start(), calls=%async_computation.26 | async-start | bytes 294912 | tf_op jit(solution)/shard_map/reduce_scatter | solution.py:296
  840.5 250.8 %reduce-scatter.26.cloned.1.call-start = ((), (), s32[]{:S(2)}) async-start(), calls=%async_computation.27 | async-start | bytes 2359296 | tf_op jit(solution)/shard_map/reduce_scatter | solution.py:299
  846.8 288.8 %reduce-scatter.20.cloned.1.call-start = ((), (), s32[]{:S(2)}) async-start(), calls=%async_computation.24 | async-start | bytes 2359296 | tf_op jit(solution)/shard_map/reduce_scatter | solution.py:290
  861.5 353.2 %reduce-scatter.18.cloned.1.call-start = ((), (), s32[]{:S(2)}) async-start(), calls=%async_computation.23 | async-start | bytes 5242880 | tf_op jit(solution)/shard_map/reduce_scatter | solution.py:161
  869.8 425.5 %reduce-scatter.14.cloned.1.call-start = ((), (), s32[]{:S(2)}) async-start(), calls=%async_computation.19 | async-start | bytes 5242880 | tf_op jit(solution)/shard_map/reduce_scatter | solution.py:151
  880.8 333.9 %copy-start.37 = (f32[2048]{0:T(1024)S(1)}, f32[2048]{0:T(1024)}, u32[]{:S(2)}) copy-start(f32[2048]{0:T(1024)} %copy-done.36) | copy-start | bytes 24580
  880.8 333.9 %copy-start.46 = (f32[256]{0:T(256)S(1)}, f32[256]{0:T(256)}, u32[]{:S(2)}) copy-start(f32[256]{0:T(256)} %copy-done.45) | copy-start | bytes 3076
  883.2 412.1 %copy-start.41 = (f32[256]{0:T(256)S(1)}, f32[256]{0:T(256)}, u32[]{:S(2)}) copy-start(f32[256]{0:T(256)} %copy-done.40) | copy-start | bytes 3076
  883.2 412.1 %copy-start.48 = (f32[256]{0:T(256)S(1)}, f32[256]{0:T(256)}, u32[]{:S(2)}) copy-start(f32[256]{0:T(256)} %copy-done.47) | copy-start | bytes 3076
  (47 other events, 633.0 us)
Sparse Core Ops, SparseCore 0:
  55.3 80.5 all-gather.9
  137.8 26.2 all-gather.11
  166.0 28.0 all-gather.13
  212.8 76.8 reduce-scatter.11
  291.5 43.6 all-gather.17
  337.2 80.7 all-gather.15
  419.9 41.6 all-gather.19
  463.1 80.7 all-gather.23
  545.8 42.7 all-gather.21
  623.7 76.7 reduce-scatter.15
  706.4 81.2 all-gather.25
  790.9 57.4 reduce-scatter.27
  851.9 59.0 reduce-scatter.29
  914.3 58.8 reduce-scatter.31
  976.1 33.6 reduce-scatter.21
  1013.3 33.6 reduce-scatter.23
  1050.2 41.1 reduce-scatter.25
  1094.5 41.1 reduce-scatter.19
  1137.9 76.7 reduce-scatter.17
  1216.9 78.3 reduce-scatter.13
where the time goes:
time: 1310 us
  waiting for transfers between devices  911 us (70%)
  matrix products  211 us (16%)
  blocking collectives  105 us (8%)
  other arithmetic  48.6 us (4%)
  between operations  15.3 us (1%)
  local copies, waits for them, and re-layouts  14.9 us (1%)
    reduce_scatter x2, waiting for transfers between devices, scatter_grads(): lax.psum_scatter(partial_grads.astype(jnp.bfloat16), 'tensor', scatter_di...  154 us
    dot_general x21, matrix products, dot_float(): return jnp.dot(left, right, preferred_element_type=jnp.float32)  143 us
    all_gather x2, waiting for transfers between devices, gather_rows(): return lax.all_gather(normed, 'tensor', axis=0, tiled=True)  141 us
    all_gather x2, waiting for transfers between devices, gather_grads(): return lax.all_gather(grad_rows, 'tensor', axis=0, tiled=True)  119 us
    reduce_scatter x2, waiting for transfers between devices, scatter_rows(): lax.psum_scatter(partial_sums.astype(jnp.bfloat16), 'tensor', scatter_dim...  111 us
    unnamed x2, blocking collectives  85.2 us
    reduce_scatter x1, waiting for transfers between devices, local(): lax.psum_scatter(grad_down.astype(jnp.bfloat16), 'dp', scatter_dimension=...  59.9 us
    all_gather x1, waiting for transfers between devices, fetch_mlp(): lax.all_gather(w_down, 'dp', axis=1, tiled=True)  44.7 us
  transfers between devices with their start and end apart: 20, of which 18 were waited for; matrix products, arithmetic and copies ran while one was open for 16% of the time, Pallas kernels for 0%

commit v1 on v0

v1 whole, which is shorter than its diff:
```python
import functools
import math

import jax
import jax.numpy as jnp
from jax import lax
from jax.experimental import pallas as pl
from jax.experimental.pallas import tpu as pltpu
from jax.sharding import PartitionSpec as P

HEAD_SIZE = 64
EPS = 1e-05
ROPE_BASE = 10000.0
NEG_LARGE = -1e30
LANES = 128
MESH = pl.DeviceIdType.MESH
F32 = jnp.float32
BF16 = jnp.bfloat16
VMEM_SPEC = pl.BlockSpec(memory_space=pltpu.VMEM)


def tables(sequence_length):
    half = HEAD_SIZE // 2
    frequency = ROPE_BASE ** (-(jnp.arange(half, dtype=F32) * 2.0) / HEAD_SIZE)
    angles = frequency[:, None] * jnp.arange(sequence_length, dtype=F32)[None, :]
    return jnp.cos(angles), jnp.sin(angles)


def dims(contract_left, contract_right):
    return (((contract_left,), (contract_right,)), ((), ()))


def mm(left, right, contract_left=1, contract_right=0):
    return lax.dot_general(
        left, right, dims(contract_left, contract_right), preferred_element_type=F32
    )


class Line:
    def __init__(self, n):
        self.n = n
        self.me = lax.axis_index("tensor")
        self.waits = []

    def barrier(self):
        barrier = pltpu.get_barrier_semaphore()
        n, me = self.n, self.me

        @pl.when(me > 0)
        def _():
            pl.semaphore_signal(barrier, inc=1, device_id={"tensor": me - 1}, device_id_type=MESH)

        @pl.when(me < n - 1)
        def _():
            pl.semaphore_signal(barrier, inc=1, device_id={"tensor": me + 1}, device_id_type=MESH)

        inner = (me > 0) & (me < n - 1)

        @pl.when(inner)
        def _():
            pl.semaphore_wait(barrier, 2)

        @pl.when(jnp.logical_not(inner))
        def _():
            pl.semaphore_wait(barrier, 1)

    def copy(self, src, dst, send, recv, step):
        return pltpu.make_async_remote_copy(
            src_ref=src,
            dst_ref=dst,
            send_sem=send,
            recv_sem=recv,
            device_id={"tensor": self.me + step},
            device_id_type=MESH,
        )


class Gather:
    def __init__(self, line, buf, send, recv, pieces):
        self.line, self.buf, self.send, self.recv, self.pieces = line, buf, send, recv, pieces
        self.size = buf.shape[1] // pieces

    def message(self, right, hop, piece, shard):
        d = 0 if right else 1
        part = self.buf.at[shard, pl.ds(piece * self.size, self.size)]
        return self.line.copy(
            part, part, self.send.at[d, hop - 1, piece], self.recv.at[d, hop - 1, piece], 1 if right else -1
        )

    def start_own(self, piece):
        line = self.line
        me, n = line.me, line.n

        @pl.when(me < n - 1)
        def _():
            self.message(True, 1, piece, me).start()

        @pl.when(me > 0)
        def _():
            self.message(False, 1, piece, me).start()

    def receive(self, hop, piece, use=None):
        line = self.line
        me, n = line.me, line.n

        @pl.when(me - hop >= 0)
        def _():
            shard = me - hop
            self.message(True, hop, piece, shard).wait_recv()
            if hop < n - 1:

                @pl.when(me < n - 1)
                def _():
                    self.message(True, hop + 1, piece, shard).start()

            if use is not None:
                use(shard, piece)

        @pl.when(me + hop <= n - 1)
        def _():
            shard = me + hop
            self.message(False, hop, piece, shard).wait_recv()
            if hop < n - 1:

                @pl.when(me > 0)
                def _():
                    self.message(False, hop + 1, piece, shard).start()

            if use is not None:
                use(shard, piece)

    def finish(self):
        line = self.line
        me, n = line.me, line.n
        for piece in range(self.pieces):
            for hop in range(1, n):

                @pl.when((me - (hop - 1) >= 0) & (me < n - 1))
                def _():
                    self.message(True, hop, piece, me - (hop - 1)).wait_send()

                @pl.when((me + (hop - 1) <= n - 1) & (me > 0))
                def _():
                    self.message(False, hop, piece, me + (hop - 1)).wait_send()


class Scatter:
    def __init__(self, line, part, buf, send, recv, pieces):
        self.line, self.part, self.buf, self.pieces = line, part, buf, pieces
        self.send, self.recv = send, recv
        self.size = part.shape[1] // pieces

    def rows(self, piece):
        return pl.ds(piece * self.size, self.size)

    def outgoing(self, d, target, piece, from_part=False):
        rows, line = self.rows(piece), self.line
        src = (self.part if from_part else self.buf).at[target, rows]
        slot = target
        if d == 1:
            slot = jnp.where(target == line.me - 1, line.n, target)
        return line.copy(
            src,
            self.buf.at[slot, rows],
            self.send.at[d, target, piece],
            self.recv.at[d, target, piece],
            1 if d == 0 else -1,
        )

    def incoming(self, d, target, slot, piece):
        part = self.buf.at[slot, self.rows(piece)]
        return self.line.copy(
            part, part, self.send.at[d, target, piece], self.recv.at[d, target, piece], 1 if d == 0 else -1
        )

    def start_ends(self, piece):
        line = self.line
        me, n = line.me, line.n

        @pl.when(me == 0)
        def _():
            for target in range(n - 1, 0, -1):
                self.outgoing(0, target, piece, True).start()

        @pl.when(me == n - 1)
        def _():
            for target in range(0, n - 1):
                self.outgoing(1, target, piece, True).start()

    def pass_on(self, d, target, piece):
        buf = self.buf
        self.incoming(d, target, target, piece).wait_recv()
        rows = self.rows(piece)
        total = buf[target, rows].astype(F32) + self.part[target, rows].astype(F32)
        buf[target, rows] = total.astype(BF16)
        self.outgoing(d, target, piece).start()

    def middle(self, piece):
        line = self.line
        me, n = line.me, line.n

        def rightward(near):
            for target in range(n - 1, 0, -1):

                @pl.when(near & (me > 0) & (me < target))
                def _():
                    self.pass_on(0, target, piece)

        def leftward(near):
            for target in range(0, n - 1):

                @pl.when(near & (me < n - 1) & (me > target))
                def _():
                    self.pass_on(1, target, piece)

        rightward(me < n // 2)
        leftward(me >= 0)
        rightward(me >= n // 2)

    def result(self, piece, store):
        line = self.line
        me, n = line.me, line.n
        rows = self.rows(piece)

        @pl.when(me > 0)
        def _():
            self.incoming(0, me, me, piece).wait_recv()

        @pl.when(me < n - 1)
        def _():
            self.incoming(1, me, n, piece).wait_recv()

        own = self.part[me, rows].astype(F32)

        @pl.when(me == 0)
        def _():
            store(own + self.buf[n, rows].astype(F32))

        @pl.when(me == n - 1)
        def _():
            store(own + self.buf[me, rows].astype(F32))

        @pl.when((me > 0) & (me < n - 1))
        def _():
            store(own + self.buf[me, rows].astype(F32) + self.buf[n, rows].astype(F32))

    def finish(self):
        line = self.line
        me, n = line.me, line.n
        for piece in range(self.pieces):
            for target in range(1, n):

                @pl.when(me < target)
                def _():
                    self.outgoing(0, target, piece).wait_send()

            for target in range(0, n - 1):

                @pl.when(me > target)
                def _():
                    self.outgoing(1, target, piece).wait_send()


def sems(n, pieces):
    return [pltpu.SemaphoreType.DMA((2, n, pieces)), pltpu.SemaphoreType.DMA((2, n, pieces))]


def comm_params(collective_id):
    return pltpu.CompilerParams(
        collective_id=collective_id, has_side_effects=True, vmem_limit_bytes=56 * 1024 * 1024
    )


def exchange_all(n, dp, send_row, recv_row, send, recv, start_only=False, wait_only=False):
    devices = n * dp
    me = lax.axis_index("dp") * n + lax.axis_index("tensor")

    def message(offset, peer, source):
        return pltpu.make_async_remote_copy(
            src_ref=send_row(peer),
            dst_ref=recv_row(source),
            send_sem=send.at[offset],
            recv_sem=recv.at[offset],
            device_id={"dp": peer // n, "tensor": peer % n},
            device_id_type=MESH,
        )

    if not wait_only:

        @pl.loop(1, devices)
        def _(offset):
            message(offset, lax.rem(me + offset, devices), me).start()

    if not start_only:

        @pl.loop(1, devices)
        def _(offset):
            copy = message(offset, lax.rem(me + offset, devices), me)
            copy.wait_send()
            copy.wait_recv()


def barrier_all(n, dp):
    devices = n * dp
    me = lax.axis_index("dp") * n + lax.axis_index("tensor")
    barrier = pltpu.get_barrier_semaphore()

    @pl.loop(1, devices)
    def _(offset):
        peer = lax.rem(me + offset, devices)
        pl.semaphore_signal(
            barrier, inc=1, device_id={"dp": peer // n, "tensor": peer % n}, device_id_type=MESH
        )

    pl.semaphore_wait(barrier, devices - 1)


def gather_kernel(n, dp, pieces, x_ref, gain_ref, seq_ref, gains_ref, send, recv, gsend, grecv):
    line = Line(n)
    me = line.me
    all_me = lax.axis_index("dp") * n + me
    barrier_all(n, dp)
    seq_ref[me] = x_ref[...]
    gains_ref[all_me] = gain_ref[...]
    gather = Gather(line, seq_ref, send, recv, pieces)
    exchange_all(
        n, dp, lambda peer: gain_ref, lambda source: gains_ref.at[source], gsend, grecv, start_only=True
    )
    for piece in range(pieces):
        gather.start_own(piece)
    for hop in range(1, n):
        for piece in range(pieces):
            gather.receive(hop, piece)
    gather.finish()
    exchange_all(
        n, dp, lambda peer: gain_ref, lambda source: gains_ref.at[source], gsend, grecv, wait_only=True
    )


def gather_rows_and_gains(n, dp, x, gains, pieces=2):
    rows, width = x.shape
    seq, all_gains = pl.pallas_call(
        functools.partial(gather_kernel, n, dp, pieces),
        out_shape=(
            jax.ShapeDtypeStruct((n, rows, width), BF16),
            jax.ShapeDtypeStruct((n * dp, 1, gains.shape[1]), F32),
        ),
        in_specs=[VMEM_SPEC] * 2,
        out_specs=(VMEM_SPEC,) * 2,
        scratch_shapes=sems(n, pieces)
        + [pltpu.SemaphoreType.DMA((n * dp,)), pltpu.SemaphoreType.DMA((n * dp,))],
        compiler_params=comm_params(1),
        name="gather_rows",
    )(x, gains)
    return seq.reshape(n * rows, width), all_gains


def tiles(extent, size):
    return [(start, min(size, extent - start)) for start in range(0, extent, size)]


def mlp_kernel(n, pieces, *refs):
    part_ref, x_ref, gain_ref, w_hbm = refs[:4]
    cot_hbm = refs[4 : 4 + n]
    npart_ref, mid_ref, inv_ref, down_ref, grad_hbm = refs[4 + n : 9 + n]
    (w, cot, seq, buf, hid, dgate, dup, stage) = refs[9 + n : 17 + n]
    ssend, srecv, gsend, grecv, local_sem, stage_sem = refs[17 + n :]
    line = Line(n)
    me = line.me
    rows_all, width = part_ref.shape[1:]
    units = hid.shape[2]
    loads = [pltpu.make_async_copy(w_hbm, w, local_sem.at[n])]
    for d in range(n):
        loads.append(
            pltpu.make_async_copy(cot_hbm[d], cot.at[lax.rem(me - d + n, n)], local_sem.at[d])
        )
    for load in loads:
        load.start()
    line.barrier()
    scatter = Scatter(line, part_ref, buf, ssend, srecv, pieces)
    gather = Gather(line, seq, gsend, grecv, pieces)
    size = scatter.size
    scatter.start_ends(0)

    def norm(piece):
        rows = scatter.rows(piece)

        def store(total):
            mid_ref[rows, :] = x_ref[rows, :].astype(F32) + total

        scatter.result(piece, store)
        mid = mid_ref[rows, :]
        inv = lax.rsqrt(jnp.mean(mid * mid, axis=1, keepdims=True) + EPS)
        inv_ref[rows, :] = jnp.broadcast_to(inv, (size, LANES))
        seq[me, rows, :] = (mid * inv * gain_ref[...]).astype(BF16)

    def flat(ref, piece):
        value = ref[:, scatter.rows(piece), :]
        return value.reshape(n * size, value.shape[2])

    def feed(piece):
        rows = scatter.rows(piece)
        tasks = []

        def unit_tile(start, count):
            def run():
                x = flat(seq, piece)
                gate = mm(x, w[:, start : start + count])
                up = mm(x, w[:, units + start : units + start + count])
                dhidden = mm(flat(cot, piece), w[:, 2 * units + start : 2 * units + start + count])
                sigmoid = jax.nn.sigmoid(gate)
                act = gate * sigmoid
                cols = slice(start, start + count)
                shape = (n, size, count)
                hid[:, rows, cols] = (act * up).astype(BF16).reshape(shape)
                dup[:, rows, cols] = (dhidden * act).astype(BF16).reshape(shape)
                dgate[:, rows, cols] = (
                    (dhidden * up * sigmoid * (1.0 + gate * (1.0 - sigmoid))).astype(BF16).reshape(shape)
                )

            return run

        def width_tile(start, count):
            def run():
                cols = slice(start, start + count)
                shape = (n, size, count)
                total = mm(flat(dgate, piece), w[cols, :units], 1, 1)
                total += mm(flat(dup, piece), w[cols, units : 2 * units], 1, 1)
                npart_ref[:, rows, cols] = total.astype(BF16).reshape(shape)
                down = mm(flat(hid, piece), w[cols, 2 * units :], 1, 1).astype(BF16).reshape(shape)
                for shard in range(n):
                    down_ref[lax.rem(shard - me + n, n), rows, cols] = down[shard]

            return run

        tasks += [unit_tile(*t) for t in tiles(units, 512)]
        tasks += [width_tile(*t) for t in tiles(width, 512)]
        return tasks

    for step in range(pieces + n - 1):
        if step < pieces:
            if step + 1 < pieces:
                scatter.start_ends(step + 1)
            scatter.middle(step)
            norm(step)
            gather.start_own(step)
        tasks = []
        ready = step - (n - 1)
        for hop in range(1, n):
            if 0 <= step - hop < pieces:
                gather.receive(hop, step - hop)
        if ready >= 0:
            if ready == 0:
                for load in loads:
                    load.wait()
            for task in feed(ready):
                task()

    scatter.finish()
    gather.finish()

    step_rows = min(256, width)
    count = width // step_rows

    def save(index, slot):
        return pltpu.make_async_copy(
            stage.at[slot],
            grad_hbm.at[pl.ds(pl.multiple_of(index * step_rows, step_rows), step_rows), :],
            stage_sem.at[slot],
        )

    @pl.loop(0, count)
    def _(index):
        slot = lax.rem(index, 2)
        cols = pl.ds(pl.multiple_of(index * step_rows, step_rows), step_rows)

        @pl.when(index >= 2)
        def _():
            save(index - 2, slot).wait()

        x = seq[:, :, cols].reshape(n * rows_all, step_rows)
        g = cot[:, :, cols].reshape(n * rows_all, step_rows)
        for at, left, right in ((0, x, dgate), (1, x, dup), (2, g, hid)):
            value = right[...].reshape(n * rows_all, units)
            stage[slot, :, at * units : (at + 1) * units] = mm(left, value, 0, 0).astype(BF16)
        save(index, slot).start()

    for index in range(max(count - 2, 0), count):
        save(index, index % 2).wait()


def mlp(n, part, x, gain, weights, cots, pieces=4):
    rows, width = x.shape
    units = weights.shape[1] // 3
    any_spec = pl.BlockSpec(memory_space=pl.ANY)
    return pl.pallas_call(
        functools.partial(mlp_kernel, n, pieces),
        out_shape=(
            jax.ShapeDtypeStruct((n, rows, width), BF16),
            jax.ShapeDtypeStruct((rows, width), F32),
            jax.ShapeDtypeStruct((rows, LANES), F32),
            jax.ShapeDtypeStruct((n, rows, width), BF16),
            jax.ShapeDtypeStruct((width, 3 * units), BF16),
        ),
        in_specs=[VMEM_SPEC] * 3 + [any_spec] * (1 + n),
        out_specs=(VMEM_SPEC,) * 4 + (any_spec,),
        scratch_shapes=[
            pltpu.VMEM((width, 3 * units), BF16),
            pltpu.VMEM((n, rows, width), BF16),
            pltpu.VMEM((n, rows, width), BF16),
            pltpu.VMEM((n + 1, rows, width), BF16),
            pltpu.VMEM((n, rows, units), BF16),
            pltpu.VMEM((n, rows, units), BF16),
            pltpu.VMEM((n, rows, units), BF16),
            pltpu.VMEM((2, min(256, width), 3 * units), BF16),
        ]
        + sems(n, pieces) * 2
        + [pltpu.SemaphoreType.DMA((n + 1,)), pltpu.SemaphoreType.DMA((2,))],
        compiler_params=pltpu.CompilerParams(
            collective_id=2, has_side_effects=True, vmem_limit_bytes=67043328
        ),
        cost_estimate=pl.CostEstimate(
            flops=18 * n * rows * width * units, bytes_accessed=400 * 1024 * 1024, transcendentals=0
        ),
        name="mlp",
    )(part.reshape(n, rows, width), x, gain, weights, *cots)


def back_kernel(
    n, pieces, part_ref, mid_ref, inv_ref, gain_ref, cot_ref, seq_ref, grad_ref, dgain_ref,
    buf, ssend, srecv, gsend, grecv,
):
    line = Line(n)
    me = line.me
    line.barrier()
    scatter = Scatter(line, part_ref, buf, ssend, srecv, pieces)
    gather = Gather(line, seq_ref, gsend, grecv, pieces)
    scatter.start_ends(0)
    dgain_ref[...] = jnp.zeros_like(dgain_ref)

    def back(piece):
        rows = scatter.rows(piece)

        def store(total):
            grad_ref[rows, :] = total

        scatter.result(piece, store)
        grad = grad_ref[rows, :]
        mid = mid_ref[rows, :]
        inv = inv_ref[rows, 0:1]
        dgain_ref[...] += jnp.sum(grad * mid * inv, axis=0, keepdims=True)
        scaled = grad * gain_ref[...]
        mean = jnp.mean(scaled * mid, axis=1, keepdims=True)
        out = cot_ref[rows, :].astype(F32) + inv * (scaled - mid * (inv * inv * mean))
        grad_ref[rows, :] = out
        seq_ref[me, rows, :] = out.astype(BF16)

    for piece in range(pieces):
        if piece + 1 < pieces:
            scatter.start_ends(piece + 1)
        scatter.middle(piece)
        back(piece)
        gather.start_own(piece)
        for hop in range(1, n):
            if piece - hop >= 0:
                gather.receive(hop, piece - hop)
    for late in range(1, n):
        for hop in range(late, n):
            piece = pieces - 1 - (hop - late)
            if piece >= 0:
                gather.receive(hop, piece)
    scatter.finish()
    gather.finish()


def sum_back_gather(n, part, mid, inv, gain, cotangent, pieces=4):
    rows, width = cotangent.shape
    return pl.pallas_call(
        functools.partial(back_kernel, n, pieces),
        out_shape=(
            jax.ShapeDtypeStruct((n, rows, width), BF16),
            jax.ShapeDtypeStruct((rows, width), F32),
            jax.ShapeDtypeStruct((1, width), F32),
        ),
        in_specs=[VMEM_SPEC] * 5,
        out_specs=(VMEM_SPEC,) * 3,
        scratch_shapes=[pltpu.VMEM((n + 1, rows, width), BF16)] + sems(n, pieces) * 2,
        compiler_params=comm_params(3),
        cost_estimate=pl.CostEstimate(flops=0, bytes_accessed=350 * 1024 * 1024, transcendentals=0),
        name="sum_back_gather",
    )(part.reshape(n, rows, width), mid, inv, gain, cotangent)


def last_kernel(
    n, pieces, part_ref, x_ref, gain_ref, grad_mid_ref, out_ref, dgain_ref, total_ref,
    buf, ssend, srecv,
):
    line = Line(n)
    line.barrier()
    scatter = Scatter(line, part_ref, buf, ssend, srecv, pieces)
    for piece in range(pieces):
        scatter.start_ends(piece)
    dgain_ref[...] = jnp.zeros_like(dgain_ref)
    for piece in range(pieces):
        scatter.middle(piece)
        rows = scatter.rows(piece)

        def store(total):
            total_ref[...] = total

        scatter.result(piece, store)
        grad = total_ref[...]
        x = x_ref[rows, :].astype(F32)
        inv = lax.rsqrt(jnp.mean(x * x, axis=1, keepdims=True) + EPS)
        dgain_ref[...] += jnp.sum(grad * x * inv, axis=0, keepdims=True)
        scaled = grad * gain_ref[...]
        mean = jnp.mean(scaled * x, axis=1, keepdims=True)
        out = grad_mid_ref[rows, :] + inv * (scaled - x * (inv * inv * mean))
        out_ref[rows, :] = out.astype(BF16)
    scatter.finish()


def sum_input_grad(n, part, x, gain, grad_mid, pieces=4):
    rows, width = x.shape
    return pl.pallas_call(
        functools.partial(last_kernel, n, pieces),
        out_shape=(
            jax.ShapeDtypeStruct((rows, width), BF16),
            jax.ShapeDtypeStruct((1, width), F32),
        ),
        in_specs=[VMEM_SPEC] * 4,
        out_specs=(VMEM_SPEC,) * 2,
        scratch_shapes=[pltpu.VMEM((rows // pieces, width), F32)]
        + [pltpu.VMEM((n + 1, rows, width), BF16)]
        + sems(n, pieces),
        compiler_params=comm_params(4),
        cost_estimate=pl.CostEstimate(flops=0, bytes_accessed=250 * 1024 * 1024, transcendentals=0),
        name="sum_input_grad",
    )(part.reshape(n, rows, width), x, gain, grad_mid)


def gains_kernel(n, dp, part_ref, out_ref, held, send, recv):
    me = lax.axis_index("dp") * n + lax.axis_index("tensor")
    barrier_all(n, dp)
    held[me] = part_ref[me]
    exchange_all(n, dp, lambda peer: part_ref.at[peer], lambda source: held.at[source], send, recv)
    out_ref[...] = jnp.sum(held[...], axis=0)


def sum_gains(n, dp, part):
    return pl.pallas_call(
        functools.partial(gains_kernel, n, dp),
        out_shape=jax.ShapeDtypeStruct((1, part.shape[2]), F32),
        in_specs=[VMEM_SPEC],
        out_specs=VMEM_SPEC,
        scratch_shapes=[
            pltpu.VMEM(part.shape, F32),
            pltpu.SemaphoreType.DMA((n * dp,)),
            pltpu.SemaphoreType.DMA((n * dp,)),
        ],
        compiler_params=comm_params(5),
        name="sum_gains",
    )(part)


def rotate(half_a, half_b, cos, sin):
    return half_a * cos - half_b * sin, half_b * cos + half_a * sin


def unrotate(half_a, half_b, cos, sin):
    return half_a * cos + half_b * sin, half_b * cos - half_a * sin


def mask_block(size, scores):
    key = lax.broadcasted_iota(jnp.int32, (size, size), 0)
    row = lax.broadcasted_iota(jnp.int32, (size, size), 1)
    return jnp.where(key <= row, scores, NEG_LARGE)


def attend_kernel(heads, block, act_ref, cos_ref, sin_ref, qkv_ref, kv_ref, out_ref, log_ref):
    half = HEAD_SIZE // 2
    cos, sin = cos_ref[...], sin_ref[...]

    @pl.loop(0, heads + 1)
    def _(h):
        base = pl.multiple_of(h * HEAD_SIZE, HEAD_SIZE)
        a, b = rotate(act_ref[pl.ds(base, half), :], act_ref[pl.ds(base + half, half), :], cos, sin)
        qkv_ref[pl.ds(base, half), :] = a.astype(BF16)
        qkv_ref[pl.ds(base + half, half), :] = b.astype(BF16)

    values = pl.ds((heads + 1) * HEAD_SIZE, HEAD_SIZE)
    qkv_ref[values, :] = act_ref[values, :].astype(BF16)
    length = qkv_ref.shape[1]
    scale = 1.0 / math.sqrt(HEAD_SIZE)
    kv_ref[...] = qkv_ref[pl.ds(heads * HEAD_SIZE, 2 * HEAD_SIZE), :].T

    @pl.loop(0, heads)
    def _(h):
        base = pl.multiple_of(h * HEAD_SIZE, HEAD_SIZE)
        for i in range(length // block):
            cols = pl.ds(i * block, block)
            query = qkv_ref[pl.ds(base, HEAD_SIZE), cols]
            scores = []
            peak = None
            for j in range(i + 1):
                s = mm(kv_ref[pl.ds(j * block, block), :HEAD_SIZE], query) * scale
                if i == j:
                    s = mask_block(block, s)
                top = jnp.max(s, axis=0, keepdims=True)
                peak = top if peak is None else jnp.maximum(peak, top)
                scores.append(s)
            weights = [jnp.exp(s - peak) for s in scores]
            total = sum(jnp.sum(w, axis=0, keepdims=True) for w in weights)
            log_ref[pl.ds(h, 1), cols] = peak + jnp.log(total)
            inverse = 1.0 / total
            mixed = None
            for j in range(i + 1):
                w = (weights[j] * inverse).astype(BF16)
                v = qkv_ref[values, pl.ds(j * block, block)]
                term = mm(v, w)
                mixed = term if mixed is None else mixed + term
            out_ref[pl.ds(base, HEAD_SIZE), cols] = mixed.astype(BF16)


def attend(act, cos, sin, block=256):
    width, length = act.shape
    heads = width // HEAD_SIZE - 2
    return pl.pallas_call(
        functools.partial(attend_kernel, heads, block),
        out_shape=(
            jax.ShapeDtypeStruct((width, length), BF16),
            jax.ShapeDtypeStruct((length, 2 * HEAD_SIZE), BF16),
            jax.ShapeDtypeStruct((heads * HEAD_SIZE, length), BF16),
            jax.ShapeDtypeStruct((heads, length), F32),
        ),
        in_specs=[VMEM_SPEC] * 3,
        out_specs=(VMEM_SPEC,) * 4,
        compiler_params=pltpu.CompilerParams(vmem_limit_bytes=56 * 1024 * 1024),
        cost_estimate=pl.CostEstimate(
            flops=4 * heads * HEAD_SIZE * length * length,
            bytes_accessed=12 * width * length,
            transcendentals=heads * length * length,
        ),
        name="attend",
    )(act, cos, sin)


def attend_back_kernel(
    heads, block, qkv_ref, kv_ref, out_ref, log_ref, grad_ref, cos_ref, sin_ref, dqkv_ref, dkv
):
    half = HEAD_SIZE // 2
    length = qkv_ref.shape[1]
    scale = 1.0 / math.sqrt(HEAD_SIZE)
    dkv[...] = jnp.zeros_like(dkv)
    keys = pl.ds(heads * HEAD_SIZE, HEAD_SIZE)

    @pl.loop(0, heads)
    def _(h):
        base = pl.multiple_of(h * HEAD_SIZE, HEAD_SIZE)
        mine = pl.ds(base, HEAD_SIZE)
        for i in range(length // block):
            cols = pl.ds(i * block, block)
            query = qkv_ref[mine, cols]
            grad = grad_ref[mine, cols]
            delta = jnp.sum(
                grad.astype(F32) * out_ref[mine, cols].astype(F32), axis=0, keepdims=True
            )
            log_total = log_ref[pl.ds(h, 1), cols]
            dquery = None
            for j in range(i + 1):
                rows = pl.ds(j * block, block)
                s = mm(kv_ref[rows, :HEAD_SIZE], query) * scale
                if i == j:
                    s = mask_block(block, s)
                probs = jnp.exp(s - log_total)
                dprobs = mm(kv_ref[rows, HEAD_SIZE:], grad)
                dscores = (probs * (dprobs - delta) * scale).astype(BF16)
                dkv[0, rows, :] += mm(dscores, query, 1, 1)
                dkv[1, rows, :] += mm(probs.astype(BF16), grad, 1, 1)
                term = mm(qkv_ref[keys, rows], dscores)
                dquery = term if dquery is None else dquery + term
            cos, sin = cos_ref[:, cols], sin_ref[:, cols]
            a, b = unrotate(dquery[:half], dquery[half:], cos, sin)
            dqkv_ref[pl.ds(base, half), cols] = a.astype(BF16)
            dqkv_ref[pl.ds(base + half, half), cols] = b.astype(BF16)

    dkeys = dkv[0].T
    a, b = unrotate(dkeys[:half], dkeys[half:], cos_ref[...], sin_ref[...])
    dqkv_ref[pl.ds(heads * HEAD_SIZE, half), :] = a.astype(BF16)
    dqkv_ref[pl.ds(heads * HEAD_SIZE + half, half), :] = b.astype(BF16)
    dqkv_ref[pl.ds((heads + 1) * HEAD_SIZE, HEAD_SIZE), :] = dkv[1].T.astype(BF16)


def attend_back(qkv, kv, out, log_total, grad, cos, sin, block=256):
    width, length = qkv.shape
    heads = width // HEAD_SIZE - 2
    return pl.pallas_call(
        functools.partial(attend_back_kernel, heads, block),
        out_shape=jax.ShapeDtypeStruct((width, length), BF16),
        in_specs=[VMEM_SPEC] * 7,
        out_specs=VMEM_SPEC,
        scratch_shapes=[pltpu.VMEM((2, length, HEAD_SIZE), F32)],
        compiler_params=pltpu.CompilerParams(vmem_limit_bytes=56 * 1024 * 1024),
        cost_estimate=pl.CostEstimate(
            flops=10 * heads * HEAD_SIZE * length * length,
            bytes_accessed=12 * width * length,
            transcendentals=heads * length * length,
        ),
        name="attend_back",
    )(qkv, kv, out, log_total, grad, cos, sin)


def local(
    n, dp, x, gain_attn, gain_mlp, w_query, w_key, w_value, w_out, w_gate, w_up, w_down, cotangent
):
    rows, width = x.shape
    length = n * rows
    per = gain_attn.shape[0]
    q_cols, k_cols = w_query.shape[1], w_key.shape[1]

    attn_cols = q_cols + 2 * k_cols
    attn_all = lax.all_gather(
        jnp.concatenate([w_query, w_key, w_value, w_out.T], axis=1), "dp", axis=0, tiled=True
    )
    w_qkv, w_out_t = attn_all[:, :attn_cols], attn_all[:, attn_cols:]
    mlp_all = lax.all_gather(
        jnp.concatenate([w_gate, w_up, w_down.T], axis=1), "dp", axis=0, tiled=True
    )
    units = w_gate.shape[1]

    packed = 2 * per + (-2 * per) % LANES
    gains = jnp.zeros((1, packed), F32)
    gains = gains.at[0, :per].set(gain_attn).at[0, per : 2 * per].set(gain_mlp)
    x_seq, all_gains = gather_rows_and_gains(n, dp, x, gains)
    full_attn = all_gains[:, 0, :per].reshape(1, width)
    full_mlp = all_gains[:, 0, per : 2 * per].reshape(1, width)

    def shift(value, distance):
        pairs = [(i, (i + distance) % n) for i in range(n)]
        return lax.ppermute(value, "tensor", pairs)

    cot_own, x_seq = lax.optimization_barrier((cotangent, x_seq))
    cots = [cot_own] + [shift(cot_own, d) for d in range(1, n)]

    x_float = x_seq.astype(F32)
    inv_attn = lax.rsqrt(jnp.mean(x_float * x_float, axis=1, keepdims=True) + EPS)
    norm_attn = (x_float * inv_attn * full_attn).astype(BF16)
    cos, sin = tables(length)
    act = mm(w_qkv, norm_attn, 0, 1)
    qkv, kv, attended, log_total = attend(act, cos, sin)
    out_part = mm(attended, w_out_t, 0, 1).astype(BF16)
    norm_part, mid, inv_mlp, down_parts, mlp_grad = mlp(n, out_part, x, full_mlp, mlp_all, cots)
    mlp_grad = lax.psum_scatter(mlp_grad, "dp", scatter_dimension=0, tiled=True)

    grad_mid_seq, grad_mid, dgain_mlp = sum_back_gather(n, norm_part, mid, inv_mlp, full_mlp, cotangent)
    down_parts, grad_mid_seq = lax.optimization_barrier((down_parts, grad_mid_seq))
    block_output = mid + down_parts[0].astype(F32)
    for d in range(1, n):
        block_output += shift(down_parts[d], d).astype(F32)
    block_output = block_output.astype(BF16)

    grad_mid_seq = grad_mid_seq.reshape(length, width)
    grad_out_t = mm(grad_mid_seq, attended, 0, 1).astype(BF16)
    dattended = mm(w_out_t, grad_mid_seq, 0, 1).astype(BF16)
    dqkv = attend_back(qkv, kv, attended, log_total, dattended, cos, sin)
    attn_part = mm(dqkv, w_qkv, 0, 1).astype(BF16)
    grad_qkv = mm(norm_attn, dqkv, 0, 1).astype(BF16)
    attn_grad = lax.psum_scatter(
        jnp.concatenate([grad_qkv, grad_out_t], axis=1), "dp", scatter_dimension=0, tiled=True
    ).astype(F32)
    input_grad, dgain_attn = sum_input_grad(n, attn_part, x, full_attn, grad_mid)
    mlp_grad = mlp_grad.astype(F32)

    dgains = jnp.concatenate(
        [dgain_attn.reshape(-1, per), dgain_mlp.reshape(-1, per)]
        + ([jnp.zeros((n * dp, packed - 2 * per), F32)] if packed > 2 * per else []),
        axis=1,
    )
    dgains = sum_gains(n, dp, dgains.reshape(n * dp, 1, packed))

    return (
        block_output,
        input_grad,
        dgains[0, :per],
        dgains[0, per : 2 * per],
        attn_grad[:, :q_cols],
        attn_grad[:, q_cols : q_cols + k_cols],
        attn_grad[:, q_cols + k_cols : attn_cols],
        attn_grad[:, attn_cols:].T,
        mlp_grad[:, :units],
        mlp_grad[:, units : 2 * units],
        mlp_grad[:, 2 * units :].T,
    )


def solution(mesh):
    rows = P(("dp", "tensor"), None)
    gain = P(("dp", "tensor"))
    into = P("dp", "tensor")
    back = P("tensor", "dp")
    in_specs = (rows, gain, gain, into, into, into, back, into, into, back, rows)
    out_specs = (rows, rows, gain, gain, into, into, into, back, into, into, back)
    body = functools.partial(local, mesh.shape["tensor"], mesh.shape["dp"])
    return jax.shard_map(body, mesh=mesh, in_specs=in_specs, out_specs=out_specs, check_vma=False)
```

time: 1310 us -> 720 us (0.55)
  waiting for transfers between devices: 911 us -> 58.9 us
  Pallas kernels: 0 us -> 546 us
  matrix products: 211 us -> 35.3 us
  blocking collectives: 105 us -> 0 us
  other arithmetic: 48.6 us -> 23.5 us
    pallas_call x0 -> x7, Pallas kernels: none -> 546 us  [the longest x1 167 us: mlp(): pl.pallas_call(functools.partial(mlp_kernel, n, pieces), out_shape=(jax.S...]
    reduce_scatter x11 -> x2, waiting for transfers between devices: 508 us -> 8.47 us  [the longest x1 8.47 us: local(): mlp_grad = lax.psum_scatter(mlp_grad, 'dp', scatter_dimension=0, tiled=True)]
    all_gather x9 -> x2, waiting for transfers between devices: 399 us -> 0.01 us  [the longest x1 0.01 us: local(): lax.all_gather(jnp.concatenate([w_query, w_key, w_value, w_out.T], axis=1...]
    dot_general x33 -> x6, matrix products: 211 us -> 35.3 us  [mm(): lax.dot_general(left, right, dims(contract_left, contract_right), preferr...]
    unnamed x2 -> x0, blocking collectives: 85.2 us -> none
    ppermute x0 -> x6, waiting for transfers between devices: none -> 49.8 us  [shift(): return lax.ppermute(value, 'tensor', pairs)]
    convert_element_type x11 -> x3, other arithmetic: 26.6 us -> 7.01 us  [the longest x1 3.89 us: local(): block_output = block_output.astype(BF16)]
    all_gather x2 -> x0, blocking collectives: 19.5 us -> none  [the longest x1 10.6 us: fetch_attention(): lax.all_gather(key_projection_weight, 'dp', axis=0, tiled=True)]
  transfers between devices with their start and end apart: 20 -> 10, of which waited for: 18 -> 2; matrix products, arithmetic and copies ran while one was open for 16% -> 8% of each run, Pallas kernels for 0% -> 33%
where the time goes in v1:
time: 720 us; the launch traced here: 709 us
  Pallas kernels  546 us (76%)
  waiting for transfers between devices  58.9 us (8%)
  matrix products  35.3 us (5%)
  local copies, waits for them, and re-layouts  24.9 us (3%)
  other arithmetic  23.5 us (3%)
  between operations  14.3 us (2%)
    pallas_call x1, Pallas kernels, mlp(): pl.pallas_call(functools.partial(mlp_kernel, n, pieces), out_shape=(jax.S...  167 us
    pallas_call x1, Pallas kernels, sum_input_grad(): pl.pallas_call(functools.partial(last_kernel, n, pieces), out_shape=(jax....  125 us
    pallas_call x1, Pallas kernels, sum_back_gather(): pl.pallas_call(functools.partial(back_kernel, n, pieces), out_shape=(jax....  122 us
    pallas_call x1, Pallas kernels, gather_rows_and_gains(): pl.pallas_call(functools.partial(gather_kernel, n, dp, pieces), out_shape...  81.5 us
    ppermute x6, waiting for transfers between devices, shift(): return lax.ppermute(value, 'tensor', pairs)  49.8 us
    dot_general x6, matrix products, mm(): lax.dot_general(left, right, dims(contract_left, contract_right), preferr...  35.3 us
    pallas_call x1, Pallas kernels, attend_back(): pl.pallas_call(functools.partial(attend_back_kernel, heads, block), out_s...  23.4 us
    pallas_call x1, Pallas kernels, attend(): pl.pallas_call(functools.partial(attend_kernel, heads, block), out_shape=...  18.1 us
  transfers between devices with their start and end apart: 10, of which 2 were waited for; matrix products, arithmetic and copies ran while one was open for 8% of the time, Pallas kernels for 33%

profile of v1, /device:TPU:0, one launch (start us, length us, event | category | flops | bytes accessed | tf_op | source)
XLA Modules:
  0.0 709.2 jit_solution(748002479253860682)
XLA Ops:
  8.4 1.8 pad_maximum_fusion.2
  10.3 1.5 copy.23
  11.9 1.5 pad_maximum_fusion.1
  16.0 1.4 broadcast_select_fusion
  18.8 81.5 %gather_rows.1 = (bf16[4,256,2048]{2,1,0:T(8,128)(2,1)}, f32[32,1,128]{2,1,0:T(1,128)}) custom-call(bf16[256,2048]{1,0:T(8,128)(2,1)} %x_ref.3, f32[1,128]{1,0:T(1,128)} %copy-done.13), custom_call_target="tpu_custom_call" | custom-call | tf_op jit(solution)/shard_map/gather_rows/pallas_call | solution.py:342
  100.2 1.8 collective-permute-start.2
  102.7 1.4 slice_reduce_fusion
  104.9 3.1 fusion
  109.3 7.7 %fusion.4.act_ref = f32[640,1024]{1,0:T(8,128)} fusion(bf16[2048,1152]{0,1:T(8,128)(2,1)} %all-gather.3.cloned.1.call-done, bf16[1024,2048]{1,0:T(8,128)(2,1)} %bitcast.37, f32[2048]{0:T(1024)S(1)} %mul.71, f32[1024]{0:T(1024)S(1)} %add_rsqrt_fusion), kind=kOutput, calls=%fused_computation.11 | convolution fusion | flops 2692743168 | bytes 9449472 | tf_op jit(solution)/shard_map/dot_general | solution.py:34
  117.0 18.1 %attend.1 = (bf16[640,1024]{1,0:T(8,128)(2,1)}, bf16[1024,128]{1,0:T(8,128)(2,1)}, bf16[512,1024]{1,0:T(8,128)(2,1)}, f32[8,1024]{1,0:T(8,128)}) custom-call(f32[640,1024]{1,0:T(8,128)} %fusion.4.act_ref, f32[32,1024]{1,0:T(8,128)} %get-tuple-element.99.cos_ref, f32[32,1024]{1,0:T(8,128)} %get-tuple-element.98.sin_ref), custom_call_target="tpu_custom_call" | custom-call | flops 2147483648 | bytes 7864320 | tf_op jit(solution)/shard_map/attend/pallas_call | solution.py:728
  135.2 6.3 convolution_convert_fusion.1
  141.4 49.8 %collective-permute-done.1.refs_6_ = bf16[256,2048]{1,0:T(8,128)(2,1)} collective-permute-done((bf16[256,2048]{1,0:T(8,128)(2,1)S(1)}, bf16[256,2048]{1,0:T(8,128)(2,1)}, u32[]{:S(2)}, u32[]{:S(2)}) %collective-permute-start.1) | collective-permute-done | bytes 1048608 | tf_op jit(solution)/shard_map/ppermute | solution.py:840
  191.3 166.9 %mlp.1 = (bf16[4,256,2048]{2,1,0:T(8,128)(2,1)}, f32[256,2048]{1,0:T(8,128)}, f32[256,128]{1,0:T(8,128)}, bf16[4,256,2048]{2,1,0:T(8,128)(2,1)}, bf16[2048,4224]{1,0:T(8,128)(2,1)}) custom-call(bf16[4,256,2048]{2,1,0:T(8,128)(2,1)} %bitcast.46, bf16[256,2048]{1,0:T(8,128)(2,1)} %x_ref.3, f32[1,2048]{1,0:T(1,128)} %reshape_squeeze.6.refs_2_.gain_ref, ...), custom_call_target="tpu_custom_call" | custom-call | flops 53150220288 | bytes 419430400 | tf_op jit(solution)/shard_map/mlp/pallas_call | solution.py:496
  358.2 121.8 %sum_back_gather.1 = (bf16[4,256,2048]{2,1,0:T(8,128)(2,1)}, f32[256,2048]{1,0:T(8,128)}, f32[1,2048]{1,0:T(1,128)}) custom-call(bf16[4,256,2048]{2,1,0:T(8,128)(2,1)} %get-tuple-element.62.part_ref, f32[256,2048]{1,0:T(8,128)} %get-tuple-element.60.mid_ref, f32[256,128]{1,0:T(8,128)} %get-tuple-element.63.inv_ref, ...), custom_call_target="tpu_custom_call" | custom-call | bytes 367001600 | tf_op jit(solution)/shard_map/sum_back_gather/pallas_call | solution.py:578
  480.0 4.7 convolution_convert_fusion.3
  484.7 5.0 fusion.13.grad_ref
  489.8 23.4 %attend_back.1 = bf16[640,1024]{1,0:T(8,128)(2,1)} custom-call(bf16[640,1024]{1,0:T(8,128)(2,1)} %get-tuple-element.66.qkv_ref, bf16[1024,128]{1,0:T(8,128)(2,1)} %get-tuple-element.67.kv_ref, bf16[512,1024]{1,0:T(8,128)(2,1)} %get-tuple-element.58.out_ref, f32[8,1024]{1,0:T(8,128)} %get-tuple-element.68.log_ref, bf16[512,1024]{1,0:T(8,128)(2,1)} %fusion.13.grad_ref, ...), custom_call_target="tpu_custom_call" | custom-call | flops 5368709120 | bytes 7864320 | tf_op jit(solution)/shard_map/attend_back/pallas_call | solution.py:797
  513.2 4.6 convolution_convert_fusion.2
  517.8 2.8 pad_maximum_fusion
  521.3 4.1 slice_bitcast_fusion.3
  525.4 4.0 collective-permute-start.5
  531.3 6.9 convolution_convert_fusion
  538.3 124.7 %sum_input_grad.1 = (bf16[256,2048]{1,0:T(8,128)(2,1)}, f32[1,2048]{1,0:T(1,128)}) custom-call(bf16[4,256,2048]{2,1,0:T(8,128)(2,1)} %bitcast.39, bf16[256,2048]{1,0:T(8,128)(2,1)} %x_ref.3, f32[1,2048]{1,0:T(1,128)} %reshape_squeeze.7.gain_ref, f32[256,2048]{1,0:T(8,128)} %get-tuple-element.70.grad_mid_ref), custom_call_target="tpu_custom_call" | custom-call | bytes 262144000 | tf_op jit(solution)/shard_map/sum_input_grad/pallas_call | solution.py:625
  662.9 1.4 reduce.33
  665.0 9.4 %sum_gains.1 = f32[1,128]{1,0:T(1,128)} custom-call(f32[32,1,128]{2,1,0:T(1,128)} %bitcast.43), custom_call_target="tpu_custom_call" | custom-call | tf_op jit(solution)/shard_map/sum_gains/pallas_call | solution.py:651
  674.5 1.3 slice_bitcast_fusion.5
  675.8 3.9 fusion.9
  682.9 1.4 fusion.22
  685.2 8.5 %reduce-scatter.5.cloned.1.call-done = bf16[256,4224]{1,0:T(8,128)(2,1)} async-done(((bf16[2048,4224]{1,0:T(8,128)(2,1)}), bf16[256,4224]{1,0:T(8,128)(2,1)}) %reduce-scatter.5.cloned.1.call-update) | async-done | bytes 2162704 | tf_op jit(solution)/shard_map/reduce_scatter | solution.py:853
  693.7 1.9 convert_element_type.59
  696.8 3.0 copy.25
  699.8 1.8 fusion.21
  (85 shorter events, 17.5 us)
Async XLA Ops:
  7.2 4.7 copy-start.5
  7.2 4.7 copy-start.6
  7.2 102.1 %all-gather.3.cloned.1.call-start = ((), (), s32[]{:S(2)}) async-start(), calls=%async_computation.2 | async-start | bytes 5308416 | tf_op jit(solution)/shard_map/all_gather | solution.py:822
  10.2 4.4 copy-start.17
  10.2 5.7 copy-start.14
  10.3 90.0 %copy-start.4 = (bf16[256,2048]{1,0:T(8,128)(2,1)S(1)}, bf16[256,2048]{1,0:T(8,128)(2,1)}, u32[]{:S(2)}) copy-start(bf16[256,2048]{1,0:T(8,128)(2,1)} %cot_ref.1) | copy-start | bytes 3145732
  10.3 181.0 %all-gather.5.cloned.1.call-start = ((), (), s32[]{:S(2)}) async-start(), calls=%async_computation.3 | async-start | bytes 19464192 | tf_op jit(solution)/shard_map/all_gather | solution.py:826
  13.4 666.3 %reduce-scatter.3.cloned.1.call-start = ((), (), s32[]{:S(2)}) async-start(), calls=%async_computation.4 | async-start | bytes 5308416 | tf_op jit(solution)/shard_map/reduce_scatter | solution.py:868
  18.2 0.5 copy-start.13
  100.2 41.2 %collective-permute-start.2 = (bf16[256,2048]{1,0:T(8,128)(2,1)S(1)}, bf16[256,2048]{1,0:T(8,128)(2,1)S(1)}, u32[]{:S(2)}, u32[]{:S(2)}) collective-permute-start(bf16[256,2048]{1,0:T(8,128)(2,1)S(1)} %copy-done.4), channel_id=1, source_target_pairs={{0,3},{1,0},{2,1},{3,2},{4,7},{5,4},{6,5},{7,6},{8,11},{9,8},{10,9... | collective-permute-start | bytes 3145736 | tf_op jit(solution)/shard_map/ppermute | solution.py:840
  102.1 89.2 %collective-permute-start.1 = (bf16[256,2048]{1,0:T(8,128)(2,1)S(1)}, bf16[256,2048]{1,0:T(8,128)(2,1)}, u32[]{:S(2)}, u32[]{:S(2)}) collective-permute-start(bf16[256,2048]{1,0:T(8,128)(2,1)S(1)} %copy-done.4), channel_id=1, source_target_pairs={{0,2},{1,3},{2,0},{3,1},{4,6},{5,7},{6,4},{7,5},{8,10},{9,11},{10,... | collective-permute-start | bytes 3145736 | tf_op jit(solution)/shard_map/ppermute | solution.py:840
  102.1 89.2 %collective-permute-start = (bf16[256,2048]{1,0:T(8,128)(2,1)S(1)}, bf16[256,2048]{1,0:T(8,128)(2,1)}, u32[]{:S(2)}, u32[]{:S(2)}) collective-permute-start(bf16[256,2048]{1,0:T(8,128)(2,1)S(1)} %copy-done.4), channel_id=1, source_target_pairs={{0,1},{1,2},{2,3},{3,0},{4,5},{5,6},{6,7},{7,4},{8,9},{9,10},{10,1... | collective-permute-start | bytes 3145736 | tf_op jit(solution)/shard_map/ppermute | solution.py:840
  104.9 12.1 %copy-start.8 = (f32[2048]{0:T(1024)}, f32[2048]{0:T(1024)S(1)}, u32[]{:S(2)}) copy-start(f32[2048]{0:T(1024)S(1)} %mul.71) | copy-start | bytes 24580
  108.0 9.0 %copy-start.11 = (f32[1024]{0:T(1024)}, f32[1024]{0:T(1024)S(1)}, u32[]{:S(2)}) copy-start(f32[1024]{0:T(1024)S(1)} %add_rsqrt_fusion) | copy-start | bytes 12292
  141.4 49.8 %copy-start.16 = (bf16[256,2048]{1,0:T(8,128)(2,1)}, bf16[256,2048]{1,0:T(8,128)(2,1)S(1)}, u32[]{:S(2)}) copy-start(bf16[256,2048]{1,0:T(8,128)(2,1)S(1)} %collective-permute-done.2.refs_7_) | copy-start | bytes 3145732
  358.1 121.8 %copy-start.18 = (bf16[512,1024]{1,0:T(8,128)(2,1)S(1)}, bf16[512,1024]{1,0:T(8,128)(2,1)}, u32[]{:S(2)}) copy-start(bf16[512,1024]{1,0:T(8,128)(2,1)} %get-tuple-element.58.out_ref) | copy-start | bytes 3145732
  480.0 4.7 copy-start.15
  489.8 23.4 %copy-start.2 = (bf16[4,256,2048]{2,1,0:T(8,128)(2,1)S(1)}, bf16[4,256,2048]{2,1,0:T(8,128)(2,1)}, u32[]{:S(2)}) copy-start(bf16[4,256,2048]{2,1,0:T(8,128)(2,1)} %get-tuple-element.55) | copy-start | bytes 12582916
  489.8 23.4 %copy-start.9 = (f32[2048]{0:T(1024)S(1)}, f32[2048]{0:T(1024)}, u32[]{:S(2)}) copy-start(f32[2048]{0:T(1024)} %copy-done.8) | copy-start | bytes 24580
  489.8 23.4 %copy-start.12 = (f32[1024]{0:T(1024)S(1)}, f32[1024]{0:T(1024)}, u32[]{:S(2)}) copy-start(f32[1024]{0:T(1024)} %copy-done.11) | copy-start | bytes 12292
  520.7 173.0 %reduce-scatter.5.cloned.1.call-start = ((), (), s32[]{:S(2)}) async-start(), calls=%async_computation.5 | async-start | bytes 19464192 | tf_op jit(solution)/shard_map/reduce_scatter | solution.py:853
  521.2 8.2 %copy-start.7 = (f32[32,1,64]{2,1,0:T(1,128)S(1)}, f32[32,1,64]{2,1,0:T(1,128)}, u32[]{:S(2)}) copy-start(f32[32,1,64]{2,1,0:T(1,128)} %get-tuple-element.95) | copy-start | bytes 24580
  521.3 9.3 %copy-start.10 = (f32[1,2048]{1,0:T(1,128)S(1)}, f32[1,2048]{1,0:T(1,128)}, u32[]{:S(2)}) copy-start(f32[1,2048]{1,0:T(1,128)} %get-tuple-element.73) | copy-start | bytes 24580
  521.3 10.1 %copy-start.19 = (bf16[640,1024]{1,0:T(8,128)(2,1)S(1)}, bf16[640,1024]{1,0:T(8,128)(2,1)}, u32[]{:S(2)}) copy-start(bf16[640,1024]{1,0:T(8,128)(2,1)} %attend_back.1) | copy-start | bytes 3932164
  525.4 150.4 %collective-permute-start.3 = (bf16[256,2048]{1,0:T(8,128)(2,1)}, bf16[256,2048]{1,0:T(8,128)(2,1)S(1)}, u32[]{:S(2)}, u32[]{:S(2)}) collective-permute-start(bf16[256,2048]{1,0:T(8,128)(2,1)} %get-tuple-element.88), channel_id=1, source_target_pairs={{0,1},{1,2},{2,3},{3,0},{4,5},{5,6},{6,7},{7,4},{8,9},{9,10},{10,1... | collective-permute-start | bytes 3145736 | tf_op jit(solution)/shard_map/ppermute | solution.py:840
  525.4 150.4 %collective-permute-start.5 = (bf16[256,2048]{1,0:T(8,128)(2,1)}, bf16[256,2048]{1,0:T(8,128)(2,1)}, u32[]{:S(2)}, u32[]{:S(2)}) collective-permute-start(bf16[256,2048]{1,0:T(8,128)(2,1)} %get-tuple-element.89), channel_id=1, source_target_pairs={{0,3},{1,0},{2,1},{3,2},{4,7},{5,4},{6,5},{7,6},{8,11},{9,8},{10,9... | collective-permute-start | bytes 3145736 | tf_op jit(solution)/shard_map/ppermute | solution.py:840
  529.4 146.4 %collective-permute-start.4 = (bf16[256,2048]{1,0:T(8,128)(2,1)}, bf16[256,2048]{1,0:T(8,128)(2,1)}, u32[]{:S(2)}, u32[]{:S(2)}) collective-permute-start(bf16[256,2048]{1,0:T(8,128)(2,1)} %get-tuple-element.90), channel_id=1, source_target_pairs={{0,2},{1,3},{2,0},{3,1},{4,6},{5,7},{6,4},{7,5},{8,10},{9,11},{10,... | collective-permute-start | bytes 3145736 | tf_op jit(solution)/shard_map/ppermute | solution.py:840
  538.3 137.6 %copy-start.1 = (f32[256,2048]{1,0:T(8,128)S(1)}, f32[256,2048]{1,0:T(8,128)}, u32[]{:S(2)}) copy-start(f32[256,2048]{1,0:T(8,128)} %get-tuple-element.60.mid_ref) | copy-start | bytes 6291460
  695.6 4.2 copy-start
  696.8 4.8 copy-start.3
Sparse Core Ops, SparseCore 0:
  10.5 42.5 all-gather.2
  54.9 91.9 all-gather.4
  520.8 50.2 reduce-scatter.2
  574.6 119.0 reduce-scatter.4

commit v2 on v1

v2 whole, which is shorter than its diff:
```python
import functools
import math

import jax
import jax.numpy as jnp
from jax import lax
from jax.experimental import pallas as pl
from jax.experimental.pallas import tpu as pltpu
from jax.sharding import PartitionSpec as P


HEAD_SIZE = 64
EPS = 1e-05
ROPE_BASE = 10000.0
NEG_LARGE = -1e30
LANES = 128
MESH = pl.DeviceIdType.MESH
F32 = jnp.float32
BF16 = jnp.bfloat16
VMEM_SPEC = pl.BlockSpec(memory_space=pltpu.VMEM)


def tables(sequence_length):
    half = HEAD_SIZE // 2
    frequency = ROPE_BASE ** (-(jnp.arange(half, dtype=F32) * 2.0) / HEAD_SIZE)
    angles = frequency[:, None] * jnp.arange(sequence_length, dtype=F32)[None, :]
    return jnp.cos(angles), jnp.sin(angles)


def dims(contract_left, contract_right):
    return (((contract_left,), (contract_right,)), ((), ()))


def mm(left, right, contract_left=1, contract_right=0):
    return lax.dot_general(
        left, right, dims(contract_left, contract_right), preferred_element_type=F32
    )


def piece_rows(piece, size):
    return pl.ds(pl.multiple_of(piece * size, size), size)


class Line:
    def __init__(self, n):
        self.n = n
        self.me = lax.axis_index("tensor")

    def barrier(self):
        barrier = pltpu.get_barrier_semaphore()
        n, me = self.n, self.me

        @pl.when(me > 0)
        def _():
            pl.semaphore_signal(barrier, inc=1, device_id={"tensor": me - 1}, device_id_type=MESH)

        @pl.when(me < n - 1)
        def _():
            pl.semaphore_signal(barrier, inc=1, device_id={"tensor": me + 1}, device_id_type=MESH)

        inner = (me > 0) & (me < n - 1)

        @pl.when(inner)
        def _():
            pl.semaphore_wait(barrier, 2)

        @pl.when(jnp.logical_not(inner))
        def _():
            pl.semaphore_wait(barrier, 1)

    def copy(self, src, dst, send, recv, step):
        return pltpu.make_async_remote_copy(
            src_ref=src,
            dst_ref=dst,
            send_sem=send,
            recv_sem=recv,
            device_id={"tensor": self.me + step},
            device_id_type=MESH,
        )


class Gather:
    def __init__(self, line, buf, send, recv, pieces):
        self.line, self.buf, self.send, self.recv, self.pieces = line, buf, send, recv, pieces
        self.size = buf.shape[1] // pieces

    def message(self, right, hop, piece, shard):
        d = 0 if right else 1
        part = self.buf.at[shard, piece_rows(piece, self.size)]
        return self.line.copy(
            part, part, self.send.at[d, hop - 1, piece], self.recv.at[d, hop - 1, piece], 1 if right else -1
        )

    def start_own(self, piece):
        line = self.line
        me, n = line.me, line.n

        @pl.when(me < n - 1)
        def _():
            self.message(True, 1, piece, me).start()

        @pl.when(me > 0)
        def _():
            self.message(False, 1, piece, me).start()

    def start_hop(self, hop, piece):
        line = self.line
        me, n = line.me, line.n

        @pl.when((me - (hop - 1) >= 0) & (me < n - 1))
        def _():
            self.message(True, hop, piece, me - (hop - 1)).start()

        @pl.when((me + (hop - 1) <= n - 1) & (me > 0))
        def _():
            self.message(False, hop, piece, me + (hop - 1)).start()

    def receive(self, hop, piece, use=None):
        line = self.line
        me, n = line.me, line.n

        @pl.when(me - hop >= 0)
        def _():
            shard = me - hop
            self.message(True, hop, piece, shard).wait_recv()
            if hop < n - 1:

                @pl.when(me < n - 1)
                def _():
                    self.message(True, hop + 1, piece, shard).start()

            if use is not None:
                use(shard, piece)

        @pl.when(me + hop <= n - 1)
        def _():
            shard = me + hop
            self.message(False, hop, piece, shard).wait_recv()
            if hop < n - 1:

                @pl.when(me > 0)
                def _():
                    self.message(False, hop + 1, piece, shard).start()

            if use is not None:
                use(shard, piece)

    def finish(self, first_hop=1):
        line = self.line
        me, n = line.me, line.n

        @pl.loop(0, self.pieces)
        def _(piece):
            for hop in range(first_hop, n):

                @pl.when((me - (hop - 1) >= 0) & (me < n - 1))
                def _():
                    self.message(True, hop, piece, me - (hop - 1)).wait_send()

                @pl.when((me + (hop - 1) <= n - 1) & (me > 0))
                def _():
                    self.message(False, hop, piece, me + (hop - 1)).wait_send()


class Scatter:
    def __init__(self, line, part, buf, send, recv, pieces):
        self.line, self.part, self.buf, self.pieces = line, part, buf, pieces
        self.send, self.recv = send, recv
        self.size = part.shape[1] // pieces

    def rows(self, piece):
        return piece_rows(piece, self.size)

    def outgoing(self, d, target, piece, from_part=False):
        rows, line = self.rows(piece), self.line
        src = (self.part if from_part else self.buf).at[target, rows]
        slot = target
        if d == 1:
            slot = jnp.where(target == line.me - 1, line.n, target)
        return line.copy(
            src,
            self.buf.at[slot, rows],
            self.send.at[d, target, piece],
            self.recv.at[d, target, piece],
            1 if d == 0 else -1,
        )

    def incoming(self, d, target, slot, piece):
        part = self.buf.at[slot, self.rows(piece)]
        return self.line.copy(
            part, part, self.send.at[d, target, piece], self.recv.at[d, target, piece], 1 if d == 0 else -1
        )

    def start_ends(self, piece):
        line = self.line
        me, n = line.me, line.n

        @pl.when(me == 0)
        def _():
            for target in range(n - 1, 0, -1):
                self.outgoing(0, target, piece, True).start()

        @pl.when(me == n - 1)
        def _():
            for target in range(0, n - 1):
                self.outgoing(1, target, piece, True).start()

    def pass_on(self, d, target, piece):
        buf = self.buf
        self.incoming(d, target, target, piece).wait_recv()
        rows = self.rows(piece)
        total = buf[target, rows].astype(F32) + self.part[target, rows].astype(F32)
        buf[target, rows] = total.astype(BF16)
        self.outgoing(d, target, piece).start()

    def passes(self, piece, right, targets, where):
        line = self.line
        me, n = line.me, line.n
        for target in targets:
            held = (me > 0) & (me < target) if right else (me < n - 1) & (me > target)

            @pl.when(where & held)
            def _():
                self.pass_on(0 if right else 1, target, piece)

    def first(self, piece):
        n, left_half = self.line.n, self.line.me < self.line.n // 2
        self.passes(piece, True, (n - 1,), left_half)
        self.passes(piece, False, (0,), jnp.logical_not(left_half))

    def rest(self, piece):
        n, left_half = self.line.n, self.line.me < self.line.n // 2
        right_half = jnp.logical_not(left_half)
        self.passes(piece, True, range(n - 2, 0, -1), left_half)
        self.passes(piece, False, range(1, n - 1), right_half)
        self.passes(piece, False, range(0, n - 1), left_half)
        self.passes(piece, True, range(n - 1, 0, -1), right_half)

    def middle(self, piece):
        self.first(piece)
        self.rest(piece)

    def result(self, piece, store):
        line = self.line
        me, n = line.me, line.n
        rows = self.rows(piece)

        @pl.when(me > 0)
        def _():
            self.incoming(0, me, me, piece).wait_recv()

        @pl.when(me < n - 1)
        def _():
            self.incoming(1, me, n, piece).wait_recv()

        own = self.part[me, rows].astype(F32)

        @pl.when(me == 0)
        def _():
            store(own + self.buf[n, rows].astype(F32))

        @pl.when(me == n - 1)
        def _():
            store(own + self.buf[me, rows].astype(F32))

        @pl.when((me > 0) & (me < n - 1))
        def _():
            store(own + self.buf[me, rows].astype(F32) + self.buf[n, rows].astype(F32))

    def finish(self):
        line = self.line
        me, n = line.me, line.n

        @pl.loop(0, self.pieces)
        def _(piece):
            for target in range(1, n):

                @pl.when(me < target)
                def _():
                    self.outgoing(0, target, piece).wait_send()

            for target in range(0, n - 1):

                @pl.when(me > target)
                def _():
                    self.outgoing(1, target, piece).wait_send()


def within(piece, pieces):
    return (piece >= 0) & (piece < pieces)


def sems(n, pieces):
    return [pltpu.SemaphoreType.DMA((2, n, pieces)), pltpu.SemaphoreType.DMA((2, n, pieces))]


def comm_params(collective_id):
    return pltpu.CompilerParams(
        collective_id=collective_id, has_side_effects=True, vmem_limit_bytes=56 * 1024 * 1024
    )


def exchange_all(n, dp, send_row, recv_row, send, recv, start_only=False, wait_only=False):
    devices = n * dp
    me = lax.axis_index("dp") * n + lax.axis_index("tensor")

    def message(offset, peer, source):
        return pltpu.make_async_remote_copy(
            src_ref=send_row(peer),
            dst_ref=recv_row(source),
            send_sem=send.at[offset],
            recv_sem=recv.at[offset],
            device_id={"dp": peer // n, "tensor": peer % n},
            device_id_type=MESH,
        )

    if not wait_only:

        @pl.loop(1, devices)
        def _(offset):
            message(offset, lax.rem(me + offset, devices), me).start()

    if not start_only:

        @pl.loop(1, devices)
        def _(offset):
            copy = message(offset, lax.rem(me + offset, devices), me)
            copy.wait_send()
            copy.wait_recv()


def barrier_all(n, dp):
    devices = n * dp
    me = lax.axis_index("dp") * n + lax.axis_index("tensor")
    barrier = pltpu.get_barrier_semaphore()

    @pl.loop(1, devices)
    def _(offset):
        peer = lax.rem(me + offset, devices)
        pl.semaphore_signal(
            barrier, inc=1, device_id={"dp": peer // n, "tensor": peer % n}, device_id_type=MESH
        )

    pl.semaphore_wait(barrier, devices - 1)


def tiles(extent, size):
    return [(start, min(size, extent - start)) for start in range(0, extent, size)]


def mlp_kernel(
    n, pieces, part_ref, x_ref, gain_ref, w_hbm, cot_hbm, near_hbm,
    mid_ref, grad_ref, low_ref, dgain_ref, hid_hbm, wgrad_hbm,
    w, cot, seq, buf, npart, buf_back, hid, dgate, dup, stage, inv_ref,
    ssend, srecv, gsend, grecv, bsend, brecv, csend, crecv, local_sem, stage_sem,
):
    line = Line(n)
    me = line.me
    rows_all, width = part_ref.shape[1:]
    units = hid.shape[2]
    weight_load = pltpu.make_async_copy(w_hbm, w, local_sem.at[0])
    own_load = pltpu.make_async_copy(cot_hbm, cot.at[me], local_sem.at[1])
    inner = (me > 0) & (me < n - 1)

    def near_load(shard):
        return pltpu.make_async_copy(near_hbm.at[shard], cot.at[shard], local_sem.at[5 + shard])

    def each_near(act):
        for shard in range(n):
            here = (me != shard) & (inner | (me - shard == 1) | (shard - me == 1))

            @pl.when(here)
            def _():
                act(near_load(shard))

    each_near(lambda copy: copy.start())
    own_load.start()
    weight_load.start()
    line.barrier()
    scatter = Scatter(line, part_ref, buf, ssend, srecv, pieces)
    gather = Gather(line, seq, gsend, grecv, pieces)
    scatter_back = Scatter(line, npart, buf_back, bsend, brecv, pieces)
    cot_gather = Gather(line, cot, csend, crecv, pieces)
    size = scatter.size
    scatter.start_ends(0)
    dgain_ref[...] = jnp.zeros_like(dgain_ref)

    each_near(lambda copy: copy.wait())

    def each_far(act):
        for hop in range(2, n):

            @pl.when(me == n - 2)
            def _():
                act(True, hop, me - (hop - 1))

            @pl.when(me == 1)
            def _():
                act(False, hop, me + (hop - 1))

    def far_start(piece):
        each_far(lambda right, hop, shard: cot_gather.message(right, hop, piece, shard).start())

    def far_sent(piece):
        each_far(lambda right, hop, shard: cot_gather.message(right, hop, piece, shard).wait_send())

    def far_arrived(piece):
        for hop in range(2, n):

            @pl.when(me == n - 1)
            def _():
                cot_gather.message(True, hop, piece, me - hop).wait_recv()

            @pl.when(me == 0)
            def _():
                cot_gather.message(False, hop, piece, me + hop).wait_recv()

    def norm(piece):
        rows = scatter.rows(piece)

        def store(total):
            mid_ref[rows, :] = x_ref[rows, :].astype(F32) + total

        scatter.result(piece, store)
        mid = mid_ref[rows, :]
        inv = lax.rsqrt(jnp.mean(mid * mid, axis=1, keepdims=True) + EPS)
        inv_ref[rows, :] = jnp.broadcast_to(inv, (size, LANES))
        seq[me, rows, :] = (mid * inv * gain_ref[...]).astype(BF16)

    def back(piece):
        rows = scatter.rows(piece)

        def store(total):
            grad_ref[rows, :] = total

        scatter_back.result(piece, store)
        grad = grad_ref[rows, :]
        mid = mid_ref[rows, :]
        inv = inv_ref[rows, 0:1]
        dgain_ref[...] += jnp.sum(grad * mid * inv, axis=0, keepdims=True)
        scaled = grad * gain_ref[...]
        mean = jnp.mean(scaled * mid, axis=1, keepdims=True)
        out = cot[me, rows, :].astype(F32) + inv * (scaled - mid * (inv * inv * mean))
        grad_ref[rows, :] = out
        low_ref[rows, :] = out.astype(BF16)

    def flat(ref, piece):
        value = ref[:, scatter.rows(piece), :]
        return value.reshape(n * size, value.shape[2])

    def feed(piece):
        rows = scatter.rows(piece)
        for start, count in tiles(units, 512):
            x = flat(seq, piece)
            gate = mm(x, w[:, start : start + count])
            up = mm(x, w[:, units + start : units + start + count])
            dhidden = mm(flat(cot, piece), w[:, 2 * units + start : 2 * units + start + count])
            sigmoid = jax.nn.sigmoid(gate)
            act = gate * sigmoid
            cols = slice(start, start + count)
            shape = (n, size, count)
            hid[:, rows, cols] = (act * up).astype(BF16).reshape(shape)
            dup[:, rows, cols] = (dhidden * act).astype(BF16).reshape(shape)
            dgate[:, rows, cols] = (
                (dhidden * up * sigmoid * (1.0 + gate * (1.0 - sigmoid))).astype(BF16).reshape(shape)
            )
        for start, count in tiles(width, 512):
            cols = slice(start, start + count)
            total = mm(flat(dgate, piece), w[cols, :units], 1, 1)
            total += mm(flat(dup, piece), w[cols, units : 2 * units], 1, 1)
            npart[:, rows, cols] = total.astype(BF16).reshape(n, size, count)

    step_rows = min(LANES, width)
    count = width // step_rows

    def save(index, slot):
        return pltpu.make_async_copy(
            stage.at[slot],
            wgrad_hbm.at[pl.ds(pl.multiple_of(index * step_rows, step_rows), step_rows), :],
            stage_sem.at[slot],
        )

    def weight_grads(events):
        @pl.loop(0, count)
        def _(index):
            for at, event in events:

                @pl.when(index == at)
                def _():
                    event()

            slot = lax.rem(index, 2)
            cols = pl.ds(pl.multiple_of(index * step_rows, step_rows), step_rows)

            @pl.when(index >= 2)
            def _():
                save(index - 2, slot).wait()

            x = seq[:, :, cols].reshape(n * rows_all, step_rows)
            g = cot[:, :, cols].reshape(n * rows_all, step_rows)
            for at, left, right in ((0, x, dgate), (1, x, dup), (2, g, hid)):
                value = right[...].reshape(n * rows_all, units)
                stage[slot, :, at * units : (at + 1) * units] = mm(left, value, 0, 0).astype(BF16)
            save(index, slot).start()

    hid_save = pltpu.make_async_copy(hid, hid_hbm, local_sem.at[2])

    @pl.loop(0, pieces + n - 1)
    def _(step):
        first = step < pieces

        @pl.when(first)
        def _():
            @pl.when(step + 1 < pieces)
            def _():
                scatter.start_ends(step + 1)

            scatter.middle(step)
            far_start(step)

        for hop in range(1, n):
            piece = step - hop

            @pl.when(within(piece, pieces))
            def _():
                gather.receive(hop, piece)

        @pl.when(first)
        def _():
            norm(step)
            gather.start_own(step)

        ready = step - (n - 1)

        @pl.when(ready == 0)
        def _():
            own_load.wait()
            weight_load.wait()

        @pl.when(ready >= 1)
        def _():
            scatter_back.middle(ready - 1)

        @pl.when(ready >= 0)
        def _():
            far_arrived(ready)
            feed(ready)
            scatter_back.start_ends(ready)

        @pl.when(ready >= 1)
        def _():
            back(ready - 1)

    hid_save.start()
    last = pieces - 1
    weight_grads(
        (
            (count * 3 // 8, lambda: scatter_back.first(last)),
            (count * 3 // 4, lambda: scatter_back.rest(last)),
        )
    )
    back(last)
    scatter.finish()
    gather.finish()
    scatter_back.finish()

    @pl.loop(0, pieces)
    def _(piece):
        far_sent(piece)

    hid_save.wait()
    for index in range(max(count - 2, 0), count):
        save(index, index % 2).wait()


def mlp(n, part, x, gain, weights, cotangent, near, pieces=4):
    rows, width = x.shape
    units = weights.shape[1] // 3
    any_spec = pl.BlockSpec(memory_space=pl.ANY)
    return pl.pallas_call(
        functools.partial(mlp_kernel, n, pieces),
        out_shape=(
            jax.ShapeDtypeStruct((rows, width), F32),
            jax.ShapeDtypeStruct((rows, width), F32),
            jax.ShapeDtypeStruct((rows, width), BF16),
            jax.ShapeDtypeStruct((1, width), F32),
            jax.ShapeDtypeStruct((n, rows, units), BF16),
            jax.ShapeDtypeStruct((width, 3 * units), BF16),
        ),
        in_specs=[VMEM_SPEC] * 3 + [any_spec] * 3,
        out_specs=(VMEM_SPEC,) * 4 + (any_spec,) * 2,
        scratch_shapes=[
            pltpu.VMEM((width, 3 * units), BF16),
            pltpu.VMEM((n, rows, width), BF16),
            pltpu.VMEM((n, rows, width), BF16),
            pltpu.VMEM((n + 1, rows, width), BF16),
            pltpu.VMEM((n, rows, width), BF16),
            pltpu.VMEM((n + 1, rows, width), BF16),
            pltpu.VMEM((n, rows, units), BF16),
            pltpu.VMEM((n, rows, units), BF16),
            pltpu.VMEM((n, rows, units), BF16),
            pltpu.VMEM((2, min(LANES, width), 3 * units), BF16),
            pltpu.VMEM((rows, LANES), F32),
        ]
        + sems(n, pieces) * 4
        + [pltpu.SemaphoreType.DMA((5 + n,)), pltpu.SemaphoreType.DMA((2,))],
        compiler_params=pltpu.CompilerParams(
            collective_id=2, has_side_effects=True, vmem_limit_bytes=67043328
        ),
        cost_estimate=pl.CostEstimate(
            flops=18 * n * rows * width * units, bytes_accessed=500 * 1024 * 1024, transcendentals=0
        ),
        name="mlp",
    )(part.reshape(n, rows, width), x, gain, weights, cotangent, near)


def rows_kernel(
    n, pieces, low_ref, mid_ref, hid_hbm, w_hbm, seq_ref, out_ref,
    hid, w, part_ref, buf, ssend, srecv, gsend, grecv, local_sem,
):
    units = hid.shape[2]
    _, width = low_ref.shape
    loads = [
        pltpu.make_async_copy(hid_hbm, hid, local_sem.at[0]),
        pltpu.make_async_copy(w_hbm.at[:, pl.ds(2 * units, units)], w, local_sem.at[1]),
    ]
    for load in loads:
        load.start()
    line = Line(n)
    me = line.me
    line.barrier()
    scatter = Scatter(line, part_ref, buf, ssend, srecv, pieces)
    gather = Gather(line, seq_ref, gsend, grecv, pieces)
    seq_ref[me] = low_ref[...]

    @pl.loop(0, pieces)
    def _(piece):
        gather.start_own(piece)

    def down(piece):
        rows = scatter.rows(piece)
        for start, count in tiles(width, 512):
            cols = slice(start, start + count)
            value = hid[:, rows, :].reshape(n * scatter.size, units)
            value = mm(value, w[cols, :], 1, 1).astype(BF16)
            part_ref[:, rows, cols] = value.reshape(n, scatter.size, count)

    for load in loads:
        load.wait()
    down(0)
    scatter.start_ends(0)

    @pl.loop(0, pieces + n - 2)
    def _(step):
        for hop in range(1, n):
            piece = step + 1 - hop

            @pl.when(within(piece, pieces))
            def _():
                gather.receive(hop, piece)

        @pl.when(step < pieces)
        def _():
            @pl.when(step + 1 < pieces)
            def _():
                down(step + 1)
                scatter.start_ends(step + 1)

            scatter.middle(step)
            rows = scatter.rows(step)

            def store(total):
                out_ref[rows, :] = (mid_ref[rows, :] + total).astype(BF16)

            scatter.result(step, store)

    scatter.finish()
    gather.finish()


def gather_and_sum(n, low, mid, hidden, weights, pieces=4):
    rows, width = low.shape
    units = hidden.shape[2]
    any_spec = pl.BlockSpec(memory_space=pl.ANY)
    return pl.pallas_call(
        functools.partial(rows_kernel, n, pieces),
        out_shape=(
            jax.ShapeDtypeStruct((n, rows, width), BF16),
            jax.ShapeDtypeStruct((rows, width), BF16),
        ),
        in_specs=[VMEM_SPEC] * 2 + [any_spec] * 2,
        out_specs=(VMEM_SPEC,) * 2,
        scratch_shapes=[
            pltpu.VMEM((n, rows, units), BF16),
            pltpu.VMEM((width, units), BF16),
            pltpu.VMEM((n, rows, width), BF16),
            pltpu.VMEM((n + 1, rows, width), BF16),
        ]
        + sems(n, pieces) * 2
        + [pltpu.SemaphoreType.DMA((2,))],
        compiler_params=comm_params(3),
        cost_estimate=pl.CostEstimate(flops=0, bytes_accessed=300 * 1024 * 1024, transcendentals=0),
        name="gather_and_sum",
    )(low, mid, hidden, weights)


def last_kernel(
    n, dp, pieces, part_ref, x_ref, gain_ref, grad_mid_ref, dgain_mlp_ref, out_ref, gains_ref,
    total_ref, dgain_ref, packed, held, buf, ssend, srecv, gsend, grecv,
):
    line = Line(n)
    all_me = lax.axis_index("dp") * n + line.me
    barrier_all(n, dp)
    scatter = Scatter(line, part_ref, buf, ssend, srecv, pieces)
    scatter.start_ends(0)
    dgain_ref[...] = jnp.zeros_like(dgain_ref)
    packed[...] = jnp.zeros_like(packed)

    @pl.loop(0, pieces)
    def _(piece):
        @pl.when(piece + 1 < pieces)
        def _():
            scatter.start_ends(piece + 1)

        scatter.middle(piece)
        rows = scatter.rows(piece)

        def store(total):
            total_ref[...] = total

        scatter.result(piece, store)
        grad = total_ref[...]
        x = x_ref[rows, :].astype(F32)
        inv = lax.rsqrt(jnp.mean(x * x, axis=1, keepdims=True) + EPS)
        dgain_ref[...] += jnp.sum(grad * x * inv, axis=0, keepdims=True)
        scaled = grad * gain_ref[...]
        mean = jnp.mean(scaled * x, axis=1, keepdims=True)
        out = grad_mid_ref[rows, :] + inv * (scaled - x * (inv * inv * mean))
        out_ref[rows, :] = out.astype(BF16)

    per = x_ref.shape[1] // (n * dp)
    for device in range(n * dp):
        cols = slice(device * per, (device + 1) * per)
        packed[device, :, :per] = dgain_ref[:, cols]
        packed[device, :, per : 2 * per] = dgain_mlp_ref[:, cols]
    held[all_me] = packed[all_me]
    exchange_all(n, dp, lambda peer: packed.at[peer], lambda source: held.at[source], gsend, grecv)
    gains_ref[...] = jnp.sum(held[...], axis=0)
    scatter.finish()


def sum_input_grad(n, dp, part, x, gain, grad_mid, dgain_mlp, packed, pieces=4):
    rows, width = x.shape
    return pl.pallas_call(
        functools.partial(last_kernel, n, dp, pieces),
        out_shape=(
            jax.ShapeDtypeStruct((rows, width), BF16),
            jax.ShapeDtypeStruct((1, packed), F32),
        ),
        in_specs=[VMEM_SPEC] * 5,
        out_specs=(VMEM_SPEC,) * 2,
        scratch_shapes=[
            pltpu.VMEM((rows // pieces, width), F32),
            pltpu.VMEM((1, width), F32),
            pltpu.VMEM((n * dp, 1, packed), F32),
            pltpu.VMEM((n * dp, 1, packed), F32),
            pltpu.VMEM((n + 1, rows, width), BF16),
        ]
        + sems(n, pieces)
        + [pltpu.SemaphoreType.DMA((n * dp,)), pltpu.SemaphoreType.DMA((n * dp,))],
        compiler_params=comm_params(4),
        cost_estimate=pl.CostEstimate(flops=0, bytes_accessed=250 * 1024 * 1024, transcendentals=0),
        name="sum_input_grad",
    )(part.reshape(n, rows, width), x, gain, grad_mid, dgain_mlp)


def widen_kernel(mlp_ref, attn_ref, gate_ref, up_ref, down_ref, query_ref, key_ref, value_ref, out_ref):
    units = gate_ref.shape[1]
    gate_ref[...] = mlp_ref[:, :units].astype(F32)
    up_ref[...] = mlp_ref[:, units : 2 * units].astype(F32)
    down_ref[...] = mlp_ref[:, 2 * units :].astype(F32).T
    q_cols, k_cols = query_ref.shape[1], key_ref.shape[1]
    query_ref[...] = attn_ref[:, :q_cols].astype(F32)
    key_ref[...] = attn_ref[:, q_cols : q_cols + k_cols].astype(F32)
    value_ref[...] = attn_ref[:, q_cols + k_cols : q_cols + 2 * k_cols].astype(F32)
    out_ref[...] = attn_ref[:, q_cols + 2 * k_cols :].astype(F32).T


def widen(mlp_grad, attn_grad, q_cols, k_cols):
    rows, units = mlp_grad.shape[0], mlp_grad.shape[1] // 3
    shapes = [(rows, units)] * 2 + [(units, rows), (rows, q_cols)] + [(rows, k_cols)] * 2 + [(q_cols, rows)]
    return pl.pallas_call(
        widen_kernel,
        out_shape=tuple(jax.ShapeDtypeStruct(shape, F32) for shape in shapes),
        in_specs=[VMEM_SPEC] * 2,
        out_specs=(VMEM_SPEC,) * 7,
        compiler_params=pltpu.CompilerParams(vmem_limit_bytes=56 * 1024 * 1024),
        name="widen",
    )(mlp_grad, attn_grad)


def rotate(half_a, half_b, cos, sin):
    return half_a * cos - half_b * sin, half_b * cos + half_a * sin


def unrotate(half_a, half_b, cos, sin):
    return half_a * cos + half_b * sin, half_b * cos - half_a * sin


def mask_block(size, scores):
    key = lax.broadcasted_iota(jnp.int32, (size, size), 0)
    row = lax.broadcasted_iota(jnp.int32, (size, size), 1)
    return jnp.where(key <= row, scores, NEG_LARGE)


def attend_kernel(
    n, dp, heads, block, pieces, x_ref, gain_ref, cos_ref, sin_ref, cot_hbm, wq_hbm, wk_hbm, wv_hbm, wo_hbm,
    norm_ref, attn_gain_ref, mlp_gain_ref, qkv_ref, kv_ref, out_ref, log_ref, part_ref, w_ref, wo_ref, near_hbm,
    seq, act_ref, gains, wq, wk, wv, wo, send, recv, gsend, grecv, wsend, wrecv, own_sem, csend, crecv,
):
    half = HEAD_SIZE // 2
    rows_all, width = x_ref.shape
    length = n * rows_all
    line = Line(n)
    me = line.me
    mine = lax.axis_index("dp")
    barrier_all(n, dp)
    seq[me] = x_ref[...]
    gains[mine * n + me] = gain_ref[...]
    gather = Gather(line, seq, send, recv, pieces)

    @pl.loop(0, pieces)
    def _(piece):
        gather.start_own(piece)

    def gain_rows(**kind):
        exchange_all(
            n, dp, lambda peer: gain_ref, lambda source: gains.at[source], gsend, grecv, **kind
        )

    gain_rows(start_only=True)

    shards = ((wq_hbm, wq), (wk_hbm, wk), (wv_hbm, wv), (wo_hbm, wo))
    own = [pltpu.make_async_copy(src, dst.at[mine], own_sem.at[i]) for i, (src, dst) in enumerate(shards)]
    pair = mine + 1 - 2 * lax.rem(mine, 2)

    def even_copy(i, offset):
        src, dst = shards[i]
        return pltpu.make_async_remote_copy(
            src_ref=src,
            dst_ref=dst.at[mine],
            send_sem=wsend.at[0, i, offset],
            recv_sem=wrecv.at[0, i, offset],
            device_id={"dp": lax.rem(mine + 2 * offset, dp)},
            device_id_type=MESH,
        )

    def pair_copy(i, offset):
        dst = shards[i][1].at[lax.rem(mine + 2 * offset, dp)]
        return pltpu.make_async_remote_copy(
            src_ref=dst,
            dst_ref=dst,
            send_sem=wsend.at[1, i, offset],
            recv_sem=wrecv.at[1, i, offset],
            device_id={"dp": pair},
            device_id_type=MESH,
        )

    for i in range(4):
        own[i].start()

    @pl.loop(1, dp // 2)
    def _(offset):
        for i in range(4):
            even_copy(i, offset).start()

    def cot_copy(right, hop):
        d = 0 if right else 1
        shard = me - (hop - 1) if right else me + (hop - 1)
        src = cot_hbm if hop == 1 else near_hbm.at[shard]
        return line.copy(src, near_hbm.at[shard], csend.at[d, hop - 1], crecv.at[d, hop - 1], 1 if right else -1)

    inner = (me > 0) & (me < n - 1)

    @pl.when(me == 0)
    def _():
        cot_copy(True, 1).start()

    @pl.when(me == n - 1)
    def _():
        cot_copy(False, 1).start()

    q_cols, k_cols = wq.shape[2], wk.shape[2]
    w_rows, w_cols = wq.shape[1], wo.shape[2]

    def project(shard):
        x = seq[shard].astype(F32)
        inv = lax.rsqrt(jnp.mean(x * x, axis=1, keepdims=True) + EPS)
        norm = (x * inv * attn_gain_ref[...]).astype(BF16)
        rows = piece_rows(shard, rows_all)
        norm_ref[rows, :] = norm
        act_ref[:, rows] = mm(w_ref[...], norm, 0, 1)

    def project_at(hop):
        @pl.when(me - hop >= 0)
        def _():
            project(me - hop)

        @pl.when(me + hop <= n - 1)
        def _():
            project(me + hop)

    def prepare():
        gain_rows(wait_only=True)
        per = width // (n * dp)
        for device in range(n * dp):
            attn_gain_ref[:, device * per : (device + 1) * per] = gains[device, :, :per]
            mlp_gain_ref[:, device * per : (device + 1) * per] = gains[device, :, per : 2 * per]

        @pl.loop(0, dp // 2)
        def _(offset):
            for i in range(4):
                pair_copy(i, offset).wait_recv()

        for d in range(dp):
            rows = slice(d * w_rows, (d + 1) * w_rows)
            w_ref[rows, :q_cols] = wq[d]
            w_ref[rows, q_cols : q_cols + k_cols] = wk[d]
            w_ref[rows, q_cols + k_cols :] = wv[d]
            wo_ref[:, d * w_cols : (d + 1) * w_cols] = wo[d]
        project(me)

    def start_pair():
        for i in range(4):
            own[i].wait()

        @pl.loop(1, dp // 2)
        def _(offset):
            for i in range(4):
                even_copy(i, offset).wait_recv()

        @pl.loop(0, dp // 2)
        def _(offset):
            for i in range(4):
                pair_copy(i, offset).start()

    ready = min(2, n - 1)
    for hop in range(1, n):

        @pl.loop(0, pieces)
        def _(piece):
            gather.receive(hop, piece)
            if hop == ready:

                @pl.when(piece == pieces // 2)
                def _():
                    start_pair()

        @pl.when((me == hop) & (me < n - 1))
        def _():
            cot_copy(True, 1).start()

        @pl.when((n - 1 - me == hop) & (me > 0))
        def _():
            cot_copy(False, 1).start()

        if hop == ready:
            if n == 4:

                @pl.when(me == 1)
                def _():
                    cot_copy_in(line, near_hbm, me - 1, crecv.at[0, 0], csend.at[0, 0], -1).wait_recv()
                    cot_copy(True, 2).start()

                @pl.when(me == 2)
                def _():
                    cot_copy_in(line, near_hbm, me + 1, crecv.at[1, 0], csend.at[1, 0], 1).wait_recv()
                    cot_copy(False, 2).start()

            prepare()
            for earlier in range(1, hop + 1):
                project_at(earlier)
        elif hop > ready:
            project_at(hop)

    cos, sin = cos_ref[...], sin_ref[...]

    @pl.loop(0, heads + 1)
    def _(h):
        base = pl.multiple_of(h * HEAD_SIZE, HEAD_SIZE)
        a, b = rotate(act_ref[pl.ds(base, half), :], act_ref[pl.ds(base + half, half), :], cos, sin)
        qkv_ref[pl.ds(base, half), :] = a.astype(BF16)
        qkv_ref[pl.ds(base + half, half), :] = b.astype(BF16)

    values = pl.ds((heads + 1) * HEAD_SIZE, HEAD_SIZE)
    qkv_ref[values, :] = act_ref[values, :].astype(BF16)
    scale = 1.0 / math.sqrt(HEAD_SIZE)
    kv_ref[...] = qkv_ref[pl.ds(heads * HEAD_SIZE, 2 * HEAD_SIZE), :].T

    @pl.loop(0, heads)
    def _(h):
        base = pl.multiple_of(h * HEAD_SIZE, HEAD_SIZE)
        for i in range(length // block):
            cols = pl.ds(i * block, block)
            query = qkv_ref[pl.ds(base, HEAD_SIZE), cols]
            scores = []
            peak = None
            for j in range(i + 1):
                s = mm(kv_ref[pl.ds(j * block, block), :HEAD_SIZE], query) * scale
                if i == j:
                    s = mask_block(block, s)
                top = jnp.max(s, axis=0, keepdims=True)
                peak = top if peak is None else jnp.maximum(peak, top)
                scores.append(s)
            weights = [jnp.exp(s - peak) for s in scores]
            total = sum(jnp.sum(w, axis=0, keepdims=True) for w in weights)
            log_ref[pl.ds(h, 1), cols] = peak + jnp.log(total)
            inverse = 1.0 / total
            mixed = None
            for j in range(i + 1):
                w = (weights[j] * inverse).astype(BF16)
                v = qkv_ref[values, pl.ds(j * block, block)]
                term = mm(v, w)
                mixed = term if mixed is None else mixed + term
            out_ref[pl.ds(base, HEAD_SIZE), cols] = mixed.astype(BF16)

    for start, count in tiles(width, 512):
        cols = slice(start, start + count)
        part_ref[:, cols] = mm(out_ref[...], wo_ref[:, cols], 0, 0).astype(BF16)

    gather.finish()

    @pl.loop(1, dp // 2)
    def _(offset):
        for i in range(4):
            even_copy(i, offset).wait_send()

    @pl.loop(0, dp // 2)
    def _(offset):
        for i in range(4):
            pair_copy(i, offset).wait_send()

    def arrived(d, hop, shard):
        cot_copy_in(
            line, near_hbm, shard, crecv.at[d, hop - 1], csend.at[d, hop - 1], 1 if d == 1 else -1
        ).wait_recv()

    if n == 4:

        @pl.when(me == 1)
        def _():
            arrived(1, 1, me + 1)
            arrived(1, 2, me + 2)
            cot_copy(True, 2).wait_send()

        @pl.when(me == 2)
        def _():
            arrived(0, 1, me - 1)
            arrived(0, 2, me - 2)
            cot_copy(False, 2).wait_send()

    else:

        @pl.when(inner)
        def _():
            arrived(0, 1, me - 1)
            arrived(1, 1, me + 1)

    @pl.when(me == 0)
    def _():
        arrived(1, 1, me + 1)

    @pl.when(me == n - 1)
    def _():
        arrived(0, 1, me - 1)

    @pl.when(me < n - 1)
    def _():
        cot_copy(True, 1).wait_send()

    @pl.when(me > 0)
    def _():
        cot_copy(False, 1).wait_send()


def cot_copy_in(line, near_hbm, shard, recv, send, step):
    part = near_hbm.at[shard]
    return line.copy(part, part, send, recv, step)


def attend(n, dp, x, gains, weights, cos, sin, cotangent, block=256, pieces=4):
    assert n <= 4 and dp % 2 == 0
    rows, width = x.shape
    length = n * rows
    q_cols, k_cols = weights[0].shape[1], weights[1].shape[1]
    cols_in = q_cols + 2 * k_cols
    heads = cols_in // HEAD_SIZE - 2
    any_spec = pl.BlockSpec(memory_space=pl.ANY)
    dma = pltpu.SemaphoreType.DMA
    return pl.pallas_call(
        functools.partial(attend_kernel, n, dp, heads, block, pieces),
        out_shape=(
            jax.ShapeDtypeStruct((length, width), BF16),
            jax.ShapeDtypeStruct((1, width), F32),
            jax.ShapeDtypeStruct((1, width), F32),
            jax.ShapeDtypeStruct((cols_in, length), BF16),
            jax.ShapeDtypeStruct((length, 2 * HEAD_SIZE), BF16),
            jax.ShapeDtypeStruct((heads * HEAD_SIZE, length), BF16),
            jax.ShapeDtypeStruct((heads, length), F32),
            jax.ShapeDtypeStruct((length, width), BF16),
            jax.ShapeDtypeStruct((width, cols_in), BF16),
            jax.ShapeDtypeStruct((q_cols, width), BF16),
            jax.ShapeDtypeStruct((n,) + cotangent.shape, BF16),
        ),
        in_specs=[VMEM_SPEC] * 4 + [any_spec] * 5,
        out_specs=(VMEM_SPEC,) * 10 + (any_spec,),
        scratch_shapes=[
            pltpu.VMEM((n, rows, width), BF16),
            pltpu.VMEM((cols_in, length), F32),
            pltpu.VMEM((n * dp, 1, gains.shape[1]), F32),
        ]
        + [pltpu.VMEM((dp,) + w.shape, BF16) for w in weights]
        + sems(n, pieces)
        + [dma((n * dp,)), dma((n * dp,)), dma((2, 4, dp // 2)), dma((2, 4, dp // 2)), dma((4,))]
        + [dma((2, 2)), dma((2, 2))],
        compiler_params=comm_params(1),
        cost_estimate=pl.CostEstimate(
            flops=2 * length * width * (cols_in + q_cols),
            bytes_accessed=350 * 1024 * 1024,
            transcendentals=heads * length * length,
        ),
        name="attend",
    )(x, gains, cos, sin, cotangent, *weights)


def attend_back_kernel(
    heads, block, seq_ref, w_ref, wo_ref, qkv_ref, kv_ref, out_ref, log_ref, norm_ref, cos_ref, sin_ref,
    part_ref, wgrad_ref, dkv, grad_ref, dqkv_ref,
):
    half = HEAD_SIZE // 2
    length, width = seq_ref.shape
    cols_in = qkv_ref.shape[0]
    scale = 1.0 / math.sqrt(HEAD_SIZE)
    dkv[...] = jnp.zeros_like(dkv)
    keys = pl.ds(heads * HEAD_SIZE, HEAD_SIZE)
    for first in range(0, length, block):
        rows = pl.ds(first, block)
        grad_ref[:, rows] = mm(wo_ref[...], seq_ref[rows, :], 1, 1).astype(BF16)

    @pl.loop(0, heads)
    def _(h):
        base = pl.multiple_of(h * HEAD_SIZE, HEAD_SIZE)
        mine = pl.ds(base, HEAD_SIZE)
        for i in range(length // block):
            cols = pl.ds(i * block, block)
            query = qkv_ref[mine, cols]
            grad = grad_ref[mine, cols]
            delta = jnp.sum(
                grad.astype(F32) * out_ref[mine, cols].astype(F32), axis=0, keepdims=True
            )
            log_total = log_ref[pl.ds(h, 1), cols]
            dquery = None
            for j in range(i + 1):
                rows = pl.ds(j * block, block)
                s = mm(kv_ref[rows, :HEAD_SIZE], query) * scale
                if i == j:
                    s = mask_block(block, s)
                probs = jnp.exp(s - log_total)
                dprobs = mm(kv_ref[rows, HEAD_SIZE:], grad)
                dscores = (probs * (dprobs - delta) * scale).astype(BF16)
                dkv[0, rows, :] += mm(dscores, query, 1, 1)
                dkv[1, rows, :] += mm(probs.astype(BF16), grad, 1, 1)
                term = mm(qkv_ref[keys, rows], dscores)
                dquery = term if dquery is None else dquery + term
            cos, sin = cos_ref[:, cols], sin_ref[:, cols]
            a, b = unrotate(dquery[:half], dquery[half:], cos, sin)
            dqkv_ref[pl.ds(base, half), cols] = a.astype(BF16)
            dqkv_ref[pl.ds(base + half, half), cols] = b.astype(BF16)

    dkeys = dkv[0].T
    a, b = unrotate(dkeys[:half], dkeys[half:], cos_ref[...], sin_ref[...])
    dqkv_ref[pl.ds(heads * HEAD_SIZE, half), :] = a.astype(BF16)
    dqkv_ref[pl.ds(heads * HEAD_SIZE + half, half), :] = b.astype(BF16)
    dqkv_ref[pl.ds((heads + 1) * HEAD_SIZE, HEAD_SIZE), :] = dkv[1].T.astype(BF16)
    for start, count in tiles(width, 512):
        cols = slice(start, start + count)
        part_ref[:, cols] = mm(dqkv_ref[...], w_ref[cols, :], 0, 1).astype(BF16)
        wgrad_ref[cols, :cols_in] = mm(norm_ref[:, cols], dqkv_ref[...], 0, 1).astype(BF16)
        wgrad_ref[cols, cols_in:] = mm(seq_ref[:, cols], out_ref[...], 0, 1).astype(BF16)


def attend_back(seq, weights, w_out, qkv, kv, out, log_total, norm, cos, sin, block=256):
    length, width = seq.shape
    cols_in = qkv.shape[0]
    heads = cols_in // HEAD_SIZE - 2
    return pl.pallas_call(
        functools.partial(attend_back_kernel, heads, block),
        out_shape=(
            jax.ShapeDtypeStruct((length, width), BF16),
            jax.ShapeDtypeStruct((width, cols_in + w_out.shape[0]), BF16),
        ),
        in_specs=[VMEM_SPEC] * 10,
        out_specs=(VMEM_SPEC,) * 2,
        scratch_shapes=[
            pltpu.VMEM((2, length, HEAD_SIZE), F32),
            pltpu.VMEM((heads * HEAD_SIZE, length), BF16),
            pltpu.VMEM((cols_in, length), BF16),
        ],
        compiler_params=pltpu.CompilerParams(vmem_limit_bytes=56 * 1024 * 1024),
        cost_estimate=pl.CostEstimate(
            flops=6 * length * width * (cols_in + w_out.shape[0]),
            bytes_accessed=120 * 1024 * 1024,
            transcendentals=heads * length * length,
        ),
        name="attend_back",
    )(seq, weights, w_out, qkv, kv, out, log_total, norm, cos, sin)


def local(
    n, dp, x, gain_attn, gain_mlp, w_query, w_key, w_value, w_out, w_gate, w_up, w_down, cotangent
):
    rows, width = x.shape
    length = n * rows
    per = gain_attn.shape[0]
    packed = 2 * per + (-2 * per) % LANES

    mlp_all = lax.all_gather(
        jnp.concatenate([w_gate, w_up, w_down.T], axis=1), "dp", axis=0, tiled=True
    )
    gains = [gain_attn, gain_mlp]
    if packed > 2 * per:
        gains.append(jnp.zeros((packed - 2 * per,), F32))
    cos, sin = tables(length)
    norm_attn, full_attn, full_mlp, qkv, kv, attended, log_total, out_part, w_qkv, w_out_all, near = attend(
        n,
        dp,
        x,
        jnp.concatenate(gains).reshape(1, packed),
        (w_query, w_key, w_value, w_out),
        cos,
        sin,
        cotangent,
    )
    mid, grad_mid, grad_low, dgain_mlp, hidden, mlp_grad = mlp(
        n, out_part, x, full_mlp, mlp_all, cotangent, near
    )
    mlp_grad = lax.psum_scatter(mlp_grad, "dp", scatter_dimension=0, tiled=True)
    grad_mid_seq, block_output = gather_and_sum(n, grad_low, mid, hidden, mlp_all)
    attn_part, attn_grad = attend_back(
        grad_mid_seq.reshape(length, width),
        w_qkv,
        w_out_all,
        qkv,
        kv,
        attended,
        log_total,
        norm_attn,
        cos,
        sin,
    )
    attn_grad = lax.psum_scatter(attn_grad, "dp", scatter_dimension=0, tiled=True)
    input_grad, dgains = sum_input_grad(n, dp, attn_part, x, full_attn, grad_mid, dgain_mlp, packed)
    gate, up, down, query, key, value, out = widen(
        mlp_grad, attn_grad, w_query.shape[1], w_key.shape[1]
    )
    return (
        block_output,
        input_grad,
        dgains[0, :per],
        dgains[0, per : 2 * per],
        query,
        key,
        value,
        out,
        gate,
        up,
        down,
    )


def solution(mesh):
    rows = P(("dp", "tensor"), None)
    gain = P(("dp", "tensor"))
    into = P("dp", "tensor")
    back = P("tensor", "dp")
    in_specs = (rows, gain, gain, into, into, into, back, into, into, back, rows)
    out_specs = (rows, rows, gain, gain, into, into, into, back, into, into, back)

    def body(*args):
        return local(mesh.shape["tensor"], mesh.shape["dp"], *args)

    return jax.shard_map(body, mesh=mesh, in_specs=in_specs, out_specs=out_specs, check_vma=False)
```

time: 720 us -> 688 us (0.956)
  matrix products: 35.3 us -> 0 us
  waiting for transfers between devices: 58.9 us -> 88.9 us
  other arithmetic: 23.5 us -> 4.67 us
  Pallas kernels: 546 us -> 563 us
  local copies, waits for them, and re-layouts: 24.9 us -> 9.47 us
    reduce_scatter x1, waiting for transfers between devices: 8.47 us -> 88 us  [local(): mlp_grad = lax.psum_scatter(mlp_grad, 'dp', scatter_dimension=0, tiled=True)]
    pallas_call x1, Pallas kernels: 167 us -> 217 us  [mlp(): pl.pallas_call(functools.partial(mlp_kernel, n, pieces), out_shape=(jax.S...]
    ppermute x6 -> x0, waiting for transfers between devices: 49.8 us -> none  [shift(): return lax.ppermute(value, 'tensor', pairs)]
    pallas_call x5 -> x4, Pallas kernels: 356 us -> 306 us  [the longest x1 116 us: attend(): pl.pallas_call(functools.partial(attend_kernel, n, dp, heads, block, piec...]
    dot_general x6 -> x0, matrix products: 35.3 us -> none  [mm(): lax.dot_general(left, right, dims(contract_left, contract_right), preferr...]
    pallas_call x1, Pallas kernels: 23.4 us -> 39.4 us  [attend_back(): pl.pallas_call(functools.partial(attend_back_kernel, heads, block), out_s...]
  transfers between devices with their start and end apart: 10 -> 3, of which waited for: 2 -> 2; matrix products, arithmetic and copies ran while one was open for 8% -> 1% of each run, Pallas kernels for 33% -> 29%
where the time goes in v2:
time: 688 us; the launch traced here: 680 us
  Pallas kernels  563 us (82%)
  waiting for transfers between devices  88.9 us (13%)
  between operations  14.3 us (2%)
  local copies, waits for them, and re-layouts  9.47 us (1%)
    pallas_call x1, Pallas kernels, mlp(): pl.pallas_call(functools.partial(mlp_kernel, n, pieces), out_shape=(jax.S...  217 us
    pallas_call x1, Pallas kernels, attend(): pl.pallas_call(functools.partial(attend_kernel, n, dp, heads, block, piec...  116 us
    pallas_call x1, Pallas kernels, gather_and_sum(): pl.pallas_call(functools.partial(rows_kernel, n, pieces), out_shape=(jax....  101 us
    reduce_scatter x1, waiting for transfers between devices, local(): mlp_grad = lax.psum_scatter(mlp_grad, 'dp', scatter_dimension=0, tiled=True)  88 us
    pallas_call x1, Pallas kernels, sum_input_grad(): pl.pallas_call(functools.partial(last_kernel, n, dp, pieces), out_shape=(...  84.8 us
    pallas_call x1, Pallas kernels, attend_back(): pl.pallas_call(functools.partial(attend_back_kernel, heads, block), out_s...  39.4 us
  transfers between devices with their start and end apart: 3, of which 2 were waited for; matrix products, arithmetic and copies ran while one was open for 1% of the time, Pallas kernels for 29%

profile of v2, /device:TPU:0, one launch (start us, length us, event | category | flops | bytes accessed | tf_op | source)
XLA Modules:
  0.0 680.3 jit_solution(12449620594787407013)
XLA Ops:
  7.2 0.0 all-gather.2.cloned.1.call-start
  7.2 1.4 copy.24
  8.7 0.0 copy-start.2
  8.7 0.0 copy-start.3
  8.7 0.0 copy-start.4
  8.7 0.0 copy-start.5
  8.7 2.8 pad_maximum_fusion
  11.6 0.0 all-gather.2.cloned.1.call-update
  11.6 0.0 reduce-scatter.5.cloned.1.call-start
  11.6 0.0 copy-done.2
  11.6 0.7 copy.22.wk_hbm
  12.4 0.0 copy-done.3
  12.4 0.7 copy.23.wv_hbm
  13.1 0.0 copy-done.4
  13.1 0.6 maximum_bitcast_fusion.gain_ref
  13.7 1.2 fusion
  15.0 115.8 %attend.1 = (bf16[1024,2048]{1,0:T(8,128)(2,1)}, f32[1,2048]{1,0:T(1,128)}, f32[1,2048]{1,0:T(1,128)}, bf16[640,1024]{1,0:T(8,128)(2,1)}, bf16[1024,128]{1,0:T(8...) custom-call(bf16[256,2048]{1,0:T(8,128)(2,1)} %x_ref.5, ...), custom_call_target="tpu_custom_call" | custom-call | flops 4831838208 | bytes 367001600 | tf_op jit(solution)/shard_map/attend/pallas_call | solution.py:1100
  130.8 0.2 all-gather.2.cloned.1.call-done.w_hbm
  130.9 217.3 %mlp.1 = (f32[256,2048]{1,0:T(8,128)}, f32[256,2048]{1,0:T(8,128)}, bf16[256,2048]{1,0:T(8,128)(2,1)}, f32[1,2048]{1,0:T(1,128)}, bf16[4,256,1408]{2,1,0:T(8,128)(2,1)}, /*index=5*/bf16[2048,4224]{1,0:T(8,128)(2,1)}) custom-call(bf16[4,256,2048]{2,1,0:T(8,128)(2,1)} %bitcast.13, bf16[256,2048]{1,0:T(8,128)(2,1)} %x_ref.5, ...), custom_call_target="tpu_custom_call" | custom-call | flops 53150220288 | bytes 524288000 | tf_op jit(solution)/shard_map/mlp/pallas_call | solution.py:580
  348.3 101.0 %gather_and_sum.1 = (bf16[4,256,2048]{2,1,0:T(8,128)(2,1)}, bf16[256,2048]{1,0:T(8,128)(2,1)}) custom-call(bf16[256,2048]{1,0:T(8,128)(2,1)} %get-tuple-element.44.low_ref, f32[256,2048]{1,0:T(8,128)} %get-tuple-element.45.mid_ref, bf16[4,256,1408]{2,1,0:T(8,128)(2,1)} %get-tuple-element.46.hid_hbm, bf16[2048,4224]{1,0:T(8,128)(2,1)} %all-gather.2.cloned.1.call-done.w_hbm), custom_call_target="tpu_custom_call" | custom-call | bytes 314572800 | tf_op jit(solution)/shard_map/gather_and_sum/pallas_call | solution.py:685
  449.3 39.4 %attend_back.1 = (bf16[1024,2048]{1,0:T(8,128)(2,1)}, bf16[2048,1152]{1,0:T(8,128)(2,1)}) custom-call(bf16[1024,2048]{1,0:T(8,128)(2,1)} %bitcast.12, bf16[2048,640]{1,0:T(8,128)(2,1)} %get-tuple-element.49.w_ref, bf16[512,2048]{1,0:T(8,128)(2,1)} %get-tuple-element.50.wo_ref, bf16[640,1024]{1,0:T(8,128)(2,1)} %get-tuple-element.51.qkv_ref, ...), custom_call_target="tpu_custom_call" | custom-call | flops 14495514624 | bytes 125829120 | tf_op jit(solution)/shard_map/attend_back/pallas_call | solution.py:1196
  488.7 0.0 reduce-scatter.5.cloned.1.call-update
  488.7 0.0 reduce-scatter.3.cloned.1.call-start
  488.7 0.7 reduce-scatter.3.cloned.1.call-update
  489.4 84.8 %sum_input_grad.1 = (bf16[256,2048]{1,0:T(8,128)(2,1)}, f32[1,128]{1,0:T(1,128)}) custom-call(bf16[4,256,2048]{2,1,0:T(8,128)(2,1)} %bitcast.10, bf16[256,2048]{1,0:T(8,128)(2,1)} %x_ref.5, f32[1,2048]{1,0:T(1,128)} %get-tuple-element.57.gain_ref, f32[256,2048]{1,0:T(8,128)} %get-tuple-element.58.grad_mid_ref, f32[1,2048]{1,0:T(1,128)} %get-tuple-element.59.dgain_mlp_ref), custom_call_target="tpu_custom_call" | custom-call | bytes 262144000 | tf_op jit(solution)/shard_map/sum_input_grad/pallas_call | solution.py:754
  574.2 1.3 slice_bitcast_fusion
  575.6 88.0 %reduce-scatter.3.cloned.1.call-done.mlp_ref = bf16[256,4224]{1,0:T(8,128)(2,1)} async-done(((bf16[2048,4224]{1,0:T(8,128)(2,1)}), bf16[256,4224]{1,0:T(8,128)(2,1)}) %reduce-scatter.3.cloned.1.call-update) | async-done | bytes 2162704 | tf_op jit(solution)/shard_map/reduce_scatter | solution.py:1247
  663.6 4.5 widen.1
  668.1 1.6 copy.25
  669.8 1.6 copy.26
  671.4 1.0 copy.29
  672.3 1.0 copy.30
  (7 shorter events, 0.0 us)
Async XLA Ops:
  7.2 123.8 %all-gather.2.cloned.1.call-start = ((), (), s32[]{:S(2)}) async-start(), calls=%async_computation.2 | async-start | bytes 19464192 | tf_op jit(solution)/shard_map/all_gather | solution.py:1227
  8.7 3.0 copy-start.2
  8.7 3.7 copy-start.3
  8.7 4.4 copy-start.4
  8.7 4.4 copy-start.5
  11.6 564.0 %reduce-scatter.5.cloned.1.call-start = ((), (), s32[]{:S(2)}) async-start(), calls=%async_computation.4 | async-start | bytes 5308416 | tf_op jit(solution)/shard_map/reduce_scatter | solution.py:1261
  488.7 174.9 %reduce-scatter.3.cloned.1.call-start = ((), (), s32[]{:S(2)}) async-start(), calls=%async_computation.3 | async-start | bytes 19464192 | tf_op jit(solution)/shard_map/reduce_scatter | solution.py:1247
  574.2 97.2 %copy-start = (bf16[256,2048]{1,0:T(8,128)(2,1)S(1)}, bf16[256,2048]{1,0:T(8,128)(2,1)}, u32[]{:S(2)}) copy-start(bf16[256,2048]{1,0:T(8,128)(2,1)} %get-tuple-element.97) | copy-start | bytes 3145732
  574.2 98.1 %copy-start.1 = (bf16[256,2048]{1,0:T(8,128)(2,1)S(1)}, bf16[256,2048]{1,0:T(8,128)(2,1)}, u32[]{:S(2)}) copy-start(bf16[256,2048]{1,0:T(8,128)(2,1)} %get-tuple-element.98) | copy-start | bytes 3145732
Sparse Core Ops, SparseCore 0:
  11.7 119.2 all-gather.1
  488.8 52.1 reduce-scatter.4
  544.7 118.8 reduce-scatter.2

commit v3 on v2

--- a/solution.py
+++ b/solution.py
@@ -18,6 +18,7 @@
 F32 = jnp.float32
 BF16 = jnp.bfloat16
 VMEM_SPEC = pl.BlockSpec(memory_space=pltpu.VMEM)
+EARLY = 0
 
 
 def tables(sequence_length):
@@ -123,9 +124,9 @@
         def _():
             shard = me - hop
             self.message(True, hop, piece, shard).wait_recv()
-            if hop < n - 1:
-
-                @pl.when(me < n - 1)
+            if not isinstance(hop, int) or hop < n - 1:
+
+                @pl.when((me < n - 1) & (hop < n - 1))
                 def _():
                     self.message(True, hop + 1, piece, shard).start()
 
@@ -136,22 +137,22 @@
         def _():
             shard = me + hop
             self.message(False, hop, piece, shard).wait_recv()
-            if hop < n - 1:
-
-                @pl.when(me > 0)
+            if not isinstance(hop, int) or hop < n - 1:
+
+                @pl.when((me > 0) & (hop < n - 1))
                 def _():
                     self.message(False, hop + 1, piece, shard).start()
 
             if use is not None:
                 use(shard, piece)
 
-    def finish(self, first_hop=1):
+    def finish(self, first_piece=0, end_piece=None):
         line = self.line
         me, n = line.me, line.n
 
-        @pl.loop(0, self.pieces)
+        @pl.loop(first_piece, self.pieces if end_piece is None else end_piece)
         def _(piece):
-            for hop in range(first_hop, n):
+            for hop in range(1, n):
 
                 @pl.when((me - (hop - 1) >= 0) & (me < n - 1))
                 def _():
@@ -267,23 +268,26 @@
         def _():
             store(own + self.buf[me, rows].astype(F32) + self.buf[n, rows].astype(F32))
 
-    def finish(self):
+    def finish(self, ends=True, middles=True):
         line = self.line
         me, n = line.me, line.n
-
-        @pl.loop(0, self.pieces)
-        def _(piece):
-            for target in range(1, n):
-
-                @pl.when(me < target)
-                def _():
-                    self.outgoing(0, target, piece).wait_send()
-
-            for target in range(0, n - 1):
-
-                @pl.when(me > target)
-                def _():
-                    self.outgoing(1, target, piece).wait_send()
+        inner = (me > 0) & (me < n - 1)
+
+        @pl.when((inner & middles) | (jnp.logical_not(inner) & ends))
+        def _():
+            @pl.loop(0, self.pieces)
+            def _(piece):
+                for target in range(1, n):
+
+                    @pl.when(me < target)
+                    def _():
+                        self.outgoing(0, target, piece).wait_send()
+
+                for target in range(0, n - 1):
+
+                    @pl.when(me > target)
+                    def _():
+                        self.outgoing(1, target, piece).wait_send()
 
 
 def within(piece, pieces):
@@ -296,7 +300,7 @@
 
 def comm_params(collective_id):
     return pltpu.CompilerParams(
-        collective_id=collective_id, has_side_effects=True, vmem_limit_bytes=56 * 1024 * 1024
+        collective_id=collective_id, has_side_effects=True, vmem_limit_bytes=60 * 1024 * 1024
     )
 
 
@@ -350,9 +354,9 @@
 
 def mlp_kernel(
     n, pieces, part_ref, x_ref, gain_ref, w_hbm, cot_hbm, near_hbm,
-    mid_ref, grad_ref, low_ref, dgain_ref, hid_hbm, wgrad_hbm,
+    mid_ref, grad_ref, dgain_ref, hid_hbm, wgrad_hbm, low_hbm,
     w, cot, seq, buf, npart, buf_back, hid, dgate, dup, stage, inv_ref,
-    ssend, srecv, gsend, grecv, bsend, brecv, csend, crecv, local_sem, stage_sem,
+    ssend, srecv, gsend, grecv, bsend, brecv, csend, crecv, lsend, lrecv, local_sem, stage_sem,
 ):
     line = Line(n)
     me = line.me
@@ -381,6 +385,7 @@
     gather = Gather(line, seq, gsend, grecv, pieces)
     scatter_back = Scatter(line, npart, buf_back, bsend, brecv, pieces)
     cot_gather = Gather(line, cot, csend, crecv, pieces)
+    low_gather = Gather(line, buf, lsend, lrecv, pieces)
     size = scatter.size
     scatter.start_ends(0)
     dgain_ref[...] = jnp.zeros_like(dgain_ref)
@@ -414,6 +419,9 @@
             @pl.when(me == 0)
             def _():
                 cot_gather.message(False, hop, piece, me + hop).wait_recv()
+
+    for piece in range(min(2, pieces)):
+        far_start(piece)
 
     def norm(piece):
         rows = scatter.rows(piece)
@@ -442,7 +450,7 @@
         mean = jnp.mean(scaled * mid, axis=1, keepdims=True)
         out = cot[me, rows, :].astype(F32) + inv * (scaled - mid * (inv * inv * mean))
         grad_ref[rows, :] = out
-        low_ref[rows, :] = out.astype(BF16)
+        buf[me, rows, :] = out.astype(BF16)
 
     def flat(ref, piece):
         value = ref[:, scatter.rows(piece), :]
@@ -516,7 +524,10 @@
                 scatter.start_ends(step + 1)
 
             scatter.middle(step)
-            far_start(step)
+
+            @pl.when(step + 2 < pieces)
+            def _():
+                far_start(step + 2)
 
         for hop in range(1, n):
             piece = step - hop
@@ -537,6 +548,17 @@
             own_load.wait()
             weight_load.wait()
 
+        @pl.when(ready == 1)
+        def _():
+            scatter.finish(ends=False)
+
+        for hop in range(1, n):
+            piece = ready - 1 - hop
+
+            @pl.when(within(piece, EARLY))
+            def _():
+                low_gather.receive(hop, piece)
+
         @pl.when(ready >= 1)
         def _():
             scatter_back.middle(ready - 1)
@@ -551,23 +573,53 @@
         def _():
             back(ready - 1)
 
+            @pl.when(ready - 1 < EARLY)
+            def _():
+                low_gather.start_own(ready - 1)
+
     hid_save.start()
     last = pieces - 1
-    weight_grads(
-        (
-            (count * 3 // 8, lambda: scatter_back.first(last)),
-            (count * 3 // 4, lambda: scatter_back.rest(last)),
+
+    def low_arrivals(step):
+        for hop in range(1, n):
+            piece = step - hop
+            if 0 <= piece < EARLY:
+                low_gather.receive(hop, piece)
+
+    late = [
+        (lambda step: lambda: low_arrivals(step))(step) for step in range(pieces - 1, pieces + n - 2)
+    ]
+    events = [
+        (count * 3 // 8, lambda: scatter_back.first(last)),
+        (count * 3 // 4, lambda: scatter_back.rest(last)),
+    ]
+    if EARLY:
+        events += [(count * (2 * i + 1) // (2 * len(late)), event) for i, event in enumerate(late)]
+    weight_grads(events)
+    back(last)
+    own_rows, early_rows = pl.ds(EARLY * size, rows_all - EARLY * size), pl.ds(0, EARLY * size)
+    low_saves = [
+        pltpu.make_async_copy(buf.at[me, own_rows], low_hbm.at[me, own_rows], local_sem.at[4])
+    ]
+    if EARLY:
+        low_saves.append(
+            pltpu.make_async_copy(
+                buf.at[pl.ds(0, n), early_rows], low_hbm.at[:, early_rows], local_sem.at[3]
+            )
         )
-    )
-    back(last)
-    scatter.finish()
+    for save_low in low_saves:
+        save_low.start()
+    scatter.finish(middles=False)
     gather.finish()
     scatter_back.finish()
+    low_gather.finish(0, EARLY)
 
     @pl.loop(0, pieces)
     def _(piece):
         far_sent(piece)
 
+    for save_low in low_saves:
+        save_low.wait()
     hid_save.wait()
     for index in range(max(count - 2, 0), count):
         save(index, index % 2).wait()
@@ -582,13 +634,13 @@
         out_shape=(
             jax.ShapeDtypeStruct((rows, width), F32),
             jax.ShapeDtypeStruct((rows, width), F32),
-            jax.ShapeDtypeStruct((rows, width), BF16),
             jax.ShapeDtypeStruct((1, width), F32),
             jax.ShapeDtypeStruct((n, rows, units), BF16),
             jax.ShapeDtypeStruct((width, 3 * units), BF16),
+            jax.ShapeDtypeStruct((n, rows, width), BF16),
         ),
         in_specs=[VMEM_SPEC] * 3 + [any_spec] * 3,
-        out_specs=(VMEM_SPEC,) * 4 + (any_spec,) * 2,
+        out_specs=(VMEM_SPEC,) * 3 + (any_spec,) * 3,
         scratch_shapes=[
             pltpu.VMEM((width, 3 * units), BF16),
             pltpu.VMEM((n, rows, width), BF16),
@@ -602,7 +654,7 @@
             pltpu.VMEM((2, min(LANES, width), 3 * units), BF16),
             pltpu.VMEM((rows, LANES), F32),
         ]
-        + sems(n, pieces) * 4
+        + sems(n, pieces) * 5
         + [pltpu.SemaphoreType.DMA((5 + n,)), pltpu.SemaphoreType.DMA((2,))],
         compiler_params=pltpu.CompilerParams(
             collective_id=2, has_side_effects=True, vmem_limit_bytes=67043328
@@ -612,96 +664,6 @@
         ),
         name="mlp",
     )(part.reshape(n, rows, width), x, gain, weights, cotangent, near)
-
-
-def rows_kernel(
-    n, pieces, low_ref, mid_ref, hid_hbm, w_hbm, seq_ref, out_ref,
-    hid, w, part_ref, buf, ssend, srecv, gsend, grecv, local_sem,
-):
-    units = hid.shape[2]
-    _, width = low_ref.shape
-    loads = [
-        pltpu.make_async_copy(hid_hbm, hid, local_sem.at[0]),
-        pltpu.make_async_copy(w_hbm.at[:, pl.ds(2 * units, units)], w, local_sem.at[1]),
-    ]
-    for load in loads:
-        load.start()
-    line = Line(n)
-    me = line.me
-    line.barrier()
-    scatter = Scatter(line, part_ref, buf, ssend, srecv, pieces)
-    gather = Gather(line, seq_ref, gsend, grecv, pieces)
-    seq_ref[me] = low_ref[...]
-
-    @pl.loop(0, pieces)
-    def _(piece):
-        gather.start_own(piece)
-
-    def down(piece):
-        rows = scatter.rows(piece)
-        for start, count in tiles(width, 512):
-            cols = slice(start, start + count)
-            value = hid[:, rows, :].reshape(n * scatter.size, units)
-            value = mm(value, w[cols, :], 1, 1).astype(BF16)
-            part_ref[:, rows, cols] = value.reshape(n, scatter.size, count)
-
-    for load in loads:
-        load.wait()
-    down(0)
-    scatter.start_ends(0)
-
-    @pl.loop(0, pieces + n - 2)
-    def _(step):
-        for hop in range(1, n):
-            piece = step + 1 - hop
-
-            @pl.when(within(piece, pieces))
-            def _():
-                gather.receive(hop, piece)
-
-        @pl.when(step < pieces)
-        def _():
-            @pl.when(step + 1 < pieces)
-            def _():
-                down(step + 1)
-                scatter.start_ends(step + 1)
-
-            scatter.middle(step)
-            rows = scatter.rows(step)
-
-            def store(total):
-                out_ref[rows, :] = (mid_ref[rows, :] + total).astype(BF16)
-
-            scatter.result(step, store)
-
-    scatter.finish()
-    gather.finish()
-
-
-def gather_and_sum(n, low, mid, hidden, weights, pieces=4):
-    rows, width = low.shape
-    units = hidden.shape[2]
-    any_spec = pl.BlockSpec(memory_space=pl.ANY)
-    return pl.pallas_call(
-        functools.partial(rows_kernel, n, pieces),
-        out_shape=(
-            jax.ShapeDtypeStruct((n, rows, width), BF16),
-            jax.ShapeDtypeStruct((rows, width), BF16),
-        ),
-        in_specs=[VMEM_SPEC] * 2 + [any_spec] * 2,
-        out_specs=(VMEM_SPEC,) * 2,
-        scratch_shapes=[
-            pltpu.VMEM((n, rows, units), BF16),
-            pltpu.VMEM((width, units), BF16),
-            pltpu.VMEM((n, rows, width), BF16),
-            pltpu.VMEM((n + 1, rows, width), BF16),
-        ]
-        + sems(n, pieces) * 2
-        + [pltpu.SemaphoreType.DMA((2,))],
-        compiler_params=comm_params(3),
-        cost_estimate=pl.CostEstimate(flops=0, bytes_accessed=300 * 1024 * 1024, transcendentals=0),
-        name="gather_and_sum",
-    )(low, mid, hidden, weights)
 
 
 def last_kernel(
@@ -779,16 +741,16 @@
     gate_ref[...] = mlp_ref[:, :units].astype(F32)
     up_ref[...] = mlp_ref[:, units : 2 * units].astype(F32)
     down_ref[...] = mlp_ref[:, 2 * units :].astype(F32).T
-    q_cols, k_cols = query_ref.shape[1], key_ref.shape[1]
+    q_cols, k_cols = query_ref.shape[1], key_ref.shape[0]
     query_ref[...] = attn_ref[:, :q_cols].astype(F32)
-    key_ref[...] = attn_ref[:, q_cols : q_cols + k_cols].astype(F32)
-    value_ref[...] = attn_ref[:, q_cols + k_cols : q_cols + 2 * k_cols].astype(F32)
+    key_ref[...] = attn_ref[:, q_cols : q_cols + k_cols].astype(F32).T
+    value_ref[...] = attn_ref[:, q_cols + k_cols : q_cols + 2 * k_cols].astype(F32).T
     out_ref[...] = attn_ref[:, q_cols + 2 * k_cols :].astype(F32).T
 
 
 def widen(mlp_grad, attn_grad, q_cols, k_cols):
     rows, units = mlp_grad.shape[0], mlp_grad.shape[1] // 3
-    shapes = [(rows, units)] * 2 + [(units, rows), (rows, q_cols)] + [(rows, k_cols)] * 2 + [(q_cols, rows)]
+    shapes = [(rows, units)] * 2 + [(units, rows), (rows, q_cols)] + [(k_cols, rows)] * 2 + [(q_cols, rows)]
     return pl.pallas_call(
         widen_kernel,
         out_shape=tuple(jax.ShapeDtypeStruct(shape, F32) for shape in shapes),
@@ -807,16 +769,16 @@
     return half_a * cos + half_b * sin, half_b * cos - half_a * sin
 
 
-def mask_block(size, scores):
+def mask_block(size):
     key = lax.broadcasted_iota(jnp.int32, (size, size), 0)
     row = lax.broadcasted_iota(jnp.int32, (size, size), 1)
-    return jnp.where(key <= row, scores, NEG_LARGE)
+    return jnp.where(key <= row, 0.0, NEG_LARGE)
 
 
 def attend_kernel(
     n, dp, heads, block, pieces, x_ref, gain_ref, cos_ref, sin_ref, cot_hbm, wq_hbm, wk_hbm, wv_hbm, wo_hbm,
     norm_ref, attn_gain_ref, mlp_gain_ref, qkv_ref, kv_ref, out_ref, log_ref, part_ref, w_ref, wo_ref, near_hbm,
-    seq, act_ref, gains, wq, wk, wv, wo, send, recv, gsend, grecv, wsend, wrecv, own_sem, csend, crecv,
+    seq, act_ref, mask_ref, gains, wq, wk, wv, wo, send, recv, gsend, grecv, wsend, wrecv, own_sem, csend, crecv,
 ):
     half = HEAD_SIZE // 2
     rows_all, width = x_ref.shape
@@ -890,7 +852,7 @@
     def _():
         cot_copy(False, 1).start()
 
-    q_cols, k_cols = wq.shape[2], wk.shape[2]
+    q_cols, k_cols = wq.shape[2], wk.shape[1]
     w_rows, w_cols = wq.shape[1], wo.shape[2]
 
     def project(shard):
@@ -925,8 +887,8 @@
         for d in range(dp):
             rows = slice(d * w_rows, (d + 1) * w_rows)
             w_ref[rows, :q_cols] = wq[d]
-            w_ref[rows, q_cols : q_cols + k_cols] = wk[d]
-            w_ref[rows, q_cols + k_cols :] = wv[d]
+            w_ref[rows, q_cols : q_cols + k_cols] = wk[d].T
+            w_ref[rows, q_cols + k_cols :] = wv[d].T
             wo_ref[:, d * w_cols : (d + 1) * w_cols] = wo[d]
         project(me)
 
@@ -985,16 +947,20 @@
 
     cos, sin = cos_ref[...], sin_ref[...]
 
+    scale = 1.0 / math.sqrt(HEAD_SIZE)
+
     @pl.loop(0, heads + 1)
     def _(h):
         base = pl.multiple_of(h * HEAD_SIZE, HEAD_SIZE)
         a, b = rotate(act_ref[pl.ds(base, half), :], act_ref[pl.ds(base + half, half), :], cos, sin)
+        factor = jnp.where(h < heads, scale, 1.0)
+        a, b = a * factor, b * factor
         qkv_ref[pl.ds(base, half), :] = a.astype(BF16)
         qkv_ref[pl.ds(base + half, half), :] = b.astype(BF16)
 
     values = pl.ds((heads + 1) * HEAD_SIZE, HEAD_SIZE)
     qkv_ref[values, :] = act_ref[values, :].astype(BF16)
-    scale = 1.0 / math.sqrt(HEAD_SIZE)
+    mask_ref[...] = mask_block(block)
     kv_ref[...] = qkv_ref[pl.ds(heads * HEAD_SIZE, 2 * HEAD_SIZE), :].T
 
     @pl.loop(0, heads)
@@ -1006,9 +972,9 @@
             scores = []
             peak = None
             for j in range(i + 1):
-                s = mm(kv_ref[pl.ds(j * block, block), :HEAD_SIZE], query) * scale
+                s = mm(kv_ref[pl.ds(j * block, block), :HEAD_SIZE], query)
                 if i == j:
-                    s = mask_block(block, s)
+                    s = s + mask_ref[...]
                 top = jnp.max(s, axis=0, keepdims=True)
                 peak = top if peak is None else jnp.maximum(peak, top)
                 scores.append(s)
@@ -1092,7 +1058,7 @@
     assert n <= 4 and dp % 2 == 0
     rows, width = x.shape
     length = n * rows
-    q_cols, k_cols = weights[0].shape[1], weights[1].shape[1]
+    q_cols, k_cols = weights[0].shape[1], weights[1].shape[0]
     cols_in = q_cols + 2 * k_cols
     heads = cols_in // HEAD_SIZE - 2
     any_spec = pl.BlockSpec(memory_space=pl.ANY)
@@ -1117,6 +1083,7 @@
         scratch_shapes=[
             pltpu.VMEM((n, rows, width), BF16),
             pltpu.VMEM((cols_in, length), F32),
+            pltpu.VMEM((block, block), F32),
             pltpu.VMEM((n * dp, 1, gains.shape[1]), F32),
         ]
         + [pltpu.VMEM((dp,) + w.shape, BF16) for w in weights]
@@ -1134,25 +1101,87 @@
 
 
 def attend_back_kernel(
-    heads, block, seq_ref, w_ref, wo_ref, qkv_ref, kv_ref, out_ref, log_ref, norm_ref, cos_ref, sin_ref,
-    part_ref, wgrad_ref, dkv, grad_ref, dqkv_ref,
+    n, heads, block, pieces, mid_ref, kv_ref, log_ref, cos_ref, sin_ref,
+    low_hbm, hid_hbm, w_mlp_hbm, wo_hbm, w_hbm, qkv_hbm, out_hbm, norm_hbm,
+    rows_ref, part_ref, wgrad_hbm,
+    seq, hid, w_down, down_ref, buf, wo_ref, w_ref, qkv_ref, out_ref, norm_ref,
+    dkv, mask_ref, grad_ref, dqkv_ref, wgrad, ssend, srecv, gsend, grecv, load_sem, save_sem,
 ):
     half = HEAD_SIZE // 2
-    length, width = seq_ref.shape
+    rows_all, width = mid_ref.shape
+    units = hid.shape[2]
     cols_in = qkv_ref.shape[0]
     scale = 1.0 / math.sqrt(HEAD_SIZE)
+    me = lax.axis_index("tensor")
+    size = rows_all // pieces
+    own_rows, early_rows = pl.ds(EARLY * size, rows_all - EARLY * size), pl.ds(0, EARLY * size)
+    pairs = (
+        (low_hbm.at[me, own_rows], seq.at[me, own_rows]),
+        (hid_hbm, hid),
+        (w_mlp_hbm.at[:, pl.ds(2 * units, units)], w_down),
+        (wo_hbm, wo_ref),
+        (qkv_hbm, qkv_ref),
+        (out_hbm, out_ref),
+        (w_hbm, w_ref),
+        (norm_hbm, norm_ref),
+    )
+    if EARLY:
+        pairs += ((low_hbm.at[:, early_rows], seq.at[:, early_rows]),)
+    loads = [pltpu.make_async_copy(src, dst, load_sem.at[i]) for i, (src, dst) in enumerate(pairs)]
+    for load in loads:
+        load.start()
+    line = Line(n)
+    line.barrier()
+    scatter = Scatter(line, down_ref, buf, ssend, srecv, pieces)
+    gather = Gather(line, seq, gsend, grecv, pieces)
+    loads[0].wait()
+
+    @pl.loop(EARLY, pieces)
+    def _(piece):
+        gather.start_own(piece)
+
     dkv[...] = jnp.zeros_like(dkv)
+    mask_ref[...] = mask_block(block)
     keys = pl.ds(heads * HEAD_SIZE, HEAD_SIZE)
-    for first in range(0, length, block):
-        rows = pl.ds(first, block)
-        grad_ref[:, rows] = mm(wo_ref[...], seq_ref[rows, :], 1, 1).astype(BF16)
-
-    @pl.loop(0, heads)
-    def _(h):
-        base = pl.multiple_of(h * HEAD_SIZE, HEAD_SIZE)
-        mine = pl.ds(base, HEAD_SIZE)
-        for i in range(length // block):
-            cols = pl.ds(i * block, block)
+
+    def project(shard):
+        grad_ref[:, piece_rows(shard, rows_all)] = mm(wo_ref[...], seq[shard], 1, 1).astype(BF16)
+
+    def start_sums():
+        loads[1].wait()
+        loads[2].wait()
+
+        @pl.loop(0, pieces)
+        def _(piece):
+            rows = scatter.rows(piece)
+            for start, count in tiles(width, 512):
+                cols = slice(start, start + count)
+                value = hid[:, rows, :].reshape(n * scatter.size, units)
+                value = mm(value, w_down[cols, :], 1, 1).astype(BF16)
+                down_ref[:, rows, cols] = value.reshape(n, scatter.size, count)
+            scatter.start_ends(piece)
+
+    def sum_piece(piece):
+        scatter.middle(piece)
+        rows = scatter.rows(piece)
+
+        def store(total):
+            rows_ref[rows, :] = (mid_ref[rows, :] + total).astype(BF16)
+
+        scatter.result(piece, store)
+
+    start_sums()
+    for load in loads[3:]:
+        load.wait()
+
+    def attention_rows(i):
+        cols = pl.ds(i * block, block)
+        cos, sin = cos_ref[:, cols], sin_ref[:, cols]
+
+        @pl.loop(0, heads)
+        def _(h):
+            base = pl.multiple_of(h * HEAD_SIZE, HEAD_SIZE)
+            mine = pl.ds(base, HEAD_SIZE)
             query = qkv_ref[mine, cols]
             grad = grad_ref[mine, cols]
             delta = jnp.sum(
@@ -1162,64 +1191,128 @@
             dquery = None
             for j in range(i + 1):
                 rows = pl.ds(j * block, block)
-                s = mm(kv_ref[rows, :HEAD_SIZE], query) * scale
+                s = mm(kv_ref[rows, :HEAD_SIZE], query)
                 if i == j:
-                    s = mask_block(block, s)
+                    s = s + mask_ref[...]
                 probs = jnp.exp(s - log_total)
                 dprobs = mm(kv_ref[rows, HEAD_SIZE:], grad)
-                dscores = (probs * (dprobs - delta) * scale).astype(BF16)
+                dscores = (probs * (dprobs - delta)).astype(BF16)
                 dkv[0, rows, :] += mm(dscores, query, 1, 1)
                 dkv[1, rows, :] += mm(probs.astype(BF16), grad, 1, 1)
                 term = mm(qkv_ref[keys, rows], dscores)
                 dquery = term if dquery is None else dquery + term
-            cos, sin = cos_ref[:, cols], sin_ref[:, cols]
+            dquery = dquery * scale
             a, b = unrotate(dquery[:half], dquery[half:], cos, sin)
             dqkv_ref[pl.ds(base, half), cols] = a.astype(BF16)
             dqkv_ref[pl.ds(base + half, half), cols] = b.astype(BF16)
+
+    @pl.loop(0, 2 * n - 1)
+    def _(turn):
+        hop = (turn + 1) // 2
+        leftward = lax.rem(turn, 2) == 1
+        shard = jnp.where(leftward, me - hop, me + hop)
+
+        @pl.when(leftward)
+        def _():
+            @pl.loop(EARLY, pieces)
+            def _(piece):
+                gather.receive(hop, piece)
+
+        @pl.when(within(shard, n))
+        def _():
+            project(shard)
+            for i in range(n):
+
+                @pl.when(shard == i)
+                def _():
+                    attention_rows(i)
+
+        @pl.when(jnp.logical_not(leftward) & within(hop - 1, min(n, pieces) - 1))
+        def _():
+            sum_piece(hop - 1)
 
     dkeys = dkv[0].T
     a, b = unrotate(dkeys[:half], dkeys[half:], cos_ref[...], sin_ref[...])
     dqkv_ref[pl.ds(heads * HEAD_SIZE, half), :] = a.astype(BF16)
     dqkv_ref[pl.ds(heads * HEAD_SIZE + half, half), :] = b.astype(BF16)
     dqkv_ref[pl.ds((heads + 1) * HEAD_SIZE, HEAD_SIZE), :] = dkv[1].T.astype(BF16)
+    saves = []
+    for index, (start, count) in enumerate(tiles(width, 512)):
+        cols = slice(start, start + count)
+        wgrad[cols, :cols_in] = mm(norm_ref[:, cols], dqkv_ref[...], 0, 1).astype(BF16)
+        for shard in range(n):
+            term = mm(seq[shard, :, cols], out_ref[:, shard * rows_all : (shard + 1) * rows_all], 0, 1)
+            total = term if shard == 0 else total + term
+        wgrad[cols, cols_in:] = total.astype(BF16)
+        save = pltpu.make_async_copy(
+            wgrad.at[pl.ds(start, count), :], wgrad_hbm.at[pl.ds(start, count), :], save_sem.at[index]
+        )
+        save.start()
+        saves.append(save)
     for start, count in tiles(width, 512):
         cols = slice(start, start + count)
         part_ref[:, cols] = mm(dqkv_ref[...], w_ref[cols, :], 0, 1).astype(BF16)
-        wgrad_ref[cols, :cols_in] = mm(norm_ref[:, cols], dqkv_ref[...], 0, 1).astype(BF16)
-        wgrad_ref[cols, cols_in:] = mm(seq_ref[:, cols], out_ref[...], 0, 1).astype(BF16)
-
-
-def attend_back(seq, weights, w_out, qkv, kv, out, log_total, norm, cos, sin, block=256):
-    length, width = seq.shape
+    for piece in range(min(n, pieces) - 1, pieces):
+        sum_piece(piece)
+    scatter.finish()
+    gather.finish(EARLY, pieces)
+    for save in saves:
+        save.wait()
+
+
+def attend_back(
+    n, mid, kv, log_total, cos, sin, low, hidden, w_mlp, w_out, w_qkv, qkv, out, norm, pieces=4
+):
+    rows, width = mid.shape
+    block = rows
+    length = n * rows
     cols_in = qkv.shape[0]
     heads = cols_in // HEAD_SIZE - 2
+    units = hidden.shape[2]
+    any_spec = pl.BlockSpec(memory_space=pl.ANY)
+    wgrad_shape = (width, cols_in + w_out.shape[0])
     return pl.pallas_call(
-        functools.partial(attend_back_kernel, heads, block),
+        functools.partial(attend_back_kernel, n, heads, block, pieces),
         out_shape=(
+            jax.ShapeDtypeStruct((rows, width), BF16),
             jax.ShapeDtypeStruct((length, width), BF16),
-            jax.ShapeDtypeStruct((width, cols_in + w_out.shape[0]), BF16),
+            jax.ShapeDtypeStruct(wgrad_shape, BF16),
         ),
-        in_specs=[VMEM_SPEC] * 10,
-        out_specs=(VMEM_SPEC,) * 2,
+        in_specs=[VMEM_SPEC] * 5 + [any_spec] * 8,
+        out_specs=(VMEM_SPEC,) * 2 + (any_spec,),
         scratch_shapes=[
+            pltpu.VMEM((n, rows, width), BF16),
+            pltpu.VMEM((n, rows, units), BF16),
+            pltpu.VMEM((width, units), BF16),
+            pltpu.VMEM((n, rows, width), BF16),
+            pltpu.VMEM((n + 1, rows, width), BF16),
+            pltpu.VMEM(w_out.shape, BF16),
+            pltpu.VMEM(w_qkv.shape, BF16),
+            pltpu.VMEM(qkv.shape, BF16),
+            pltpu.VMEM(out.shape, BF16),
+            pltpu.VMEM(norm.shape, BF16),
             pltpu.VMEM((2, length, HEAD_SIZE), F32),
+            pltpu.VMEM((block, block), F32),
             pltpu.VMEM((heads * HEAD_SIZE, length), BF16),
             pltpu.VMEM((cols_in, length), BF16),
-        ],
-        compiler_params=pltpu.CompilerParams(vmem_limit_bytes=56 * 1024 * 1024),
+            pltpu.VMEM(wgrad_shape, BF16),
+        ]
+        + sems(n, pieces) * 2
+        + [pltpu.SemaphoreType.DMA((9,)), pltpu.SemaphoreType.DMA((len(tiles(width, 512)),))],
+        compiler_params=comm_params(3),
         cost_estimate=pl.CostEstimate(
-            flops=6 * length * width * (cols_in + w_out.shape[0]),
-            bytes_accessed=120 * 1024 * 1024,
+            flops=6 * length * width * wgrad_shape[1],
+            bytes_accessed=350 * 1024 * 1024,
             transcendentals=heads * length * length,
         ),
         name="attend_back",
-    )(seq, weights, w_out, qkv, kv, out, log_total, norm, cos, sin)
+    )(mid, kv, log_total, cos, sin, low, hidden, w_mlp, w_out, w_qkv, qkv, out, norm)
 
 
 def local(
     n, dp, x, gain_attn, gain_mlp, w_query, w_key, w_value, w_out, w_gate, w_up, w_down, cotangent
 ):
-    rows, width = x.shape
+    rows, _ = x.shape
     length = n * rows
     per = gain_attn.shape[0]
     packed = 2 * per + (-2 * per) % LANES
@@ -1236,27 +1329,17 @@
         dp,
         x,
         jnp.concatenate(gains).reshape(1, packed),
-        (w_query, w_key, w_value, w_out),
+        (w_query, w_key.T, w_value.T, w_out),
         cos,
         sin,
         cotangent,
     )
-    mid, grad_mid, grad_low, dgain_mlp, hidden, mlp_grad = mlp(
+    mid, grad_mid, dgain_mlp, hidden, mlp_grad, grad_low = mlp(
         n, out_part, x, full_mlp, mlp_all, cotangent, near
     )
     mlp_grad = lax.psum_scatter(mlp_grad, "dp", scatter_dimension=0, tiled=True)
-    grad_mid_seq, block_output = gather_and_sum(n, grad_low, mid, hidden, mlp_all)
-    attn_part, attn_grad = attend_back(
-        grad_mid_seq.reshape(length, width),
-        w_qkv,
-        w_out_all,
-        qkv,
-        kv,
-        attended,
-        log_total,
-        norm_attn,
-        cos,
-        sin,
+    block_output, attn_part, attn_grad = attend_back(
+        n, mid, kv, log_total, cos, sin, grad_low, hidden, mlp_all, w_out_all, w_qkv, qkv, attended, norm_attn
     )
     attn_grad = lax.psum_scatter(attn_grad, "dp", scatter_dimension=0, tiled=True)
     input_grad, dgains = sum_input_grad(n, dp, attn_part, x, full_attn, grad_mid, dgain_mlp, packed)
@@ -1269,8 +1352,8 @@
         dgains[0, :per],
         dgains[0, per : 2 * per],
         query,
-        key,
-        value,
+        key.T,
+        value.T,
         out,
         gate,
         up,

time: 688 us -> 643 us (0.935)
  Pallas kernels: 563 us -> 517 us
    pallas_call x2 -> x1, Pallas kernels: 140 us -> 114 us  [attend_back(): pl.pallas_call(functools.partial(attend_back_kernel, n, heads, block, pie...]
    pallas_call x1, Pallas kernels: 217 us -> 205 us  [mlp(): pl.pallas_call(functools.partial(mlp_kernel, n, pieces), out_shape=(jax.S...]
    pallas_call x1, Pallas kernels: 116 us -> 108 us  [attend(): pl.pallas_call(functools.partial(attend_kernel, n, dp, heads, block, piec...]
  transfers between devices with their start and end apart: 3 -> 3, of which waited for: 2 -> 2; matrix products, arithmetic and copies ran while one was open for 1% -> 1% of each run, Pallas kernels for 29% -> 30%
where the time goes in v3:
time: 643 us; the launch traced here: 635 us
  Pallas kernels  517 us (80%)
  waiting for transfers between devices  94.4 us (15%)
  between operations  14.2 us (2%)
    pallas_call x1, Pallas kernels, mlp(): pl.pallas_call(functools.partial(mlp_kernel, n, pieces), out_shape=(jax.S...  205 us
    pallas_call x1, Pallas kernels, attend_back(): pl.pallas_call(functools.partial(attend_back_kernel, n, heads, block, pie...  114 us
    pallas_call x1, Pallas kernels, attend(): pl.pallas_call(functools.partial(attend_kernel, n, dp, heads, block, piec...  108 us
    reduce_scatter x1, waiting for transfers between devices, local(): mlp_grad = lax.psum_scatter(mlp_grad, 'dp', scatter_dimension=0, tiled=True)  87.8 us
    pallas_call x1, Pallas kernels, sum_input_grad(): pl.pallas_call(functools.partial(last_kernel, n, dp, pieces), out_shape=(...  85.9 us
  transfers between devices with their start and end apart: 3, of which 2 were waited for; matrix products, arithmetic and copies ran while one was open for 1% of the time, Pallas kernels for 30%

profile of v3, /device:TPU:0, one launch (start us, length us, event | category | flops | bytes accessed | tf_op | source)
XLA Modules:
  0.0 635.1 jit_solution(6149213761794907759)
XLA Ops:
  7.2 0.0 all-gather.2.cloned.1.call-start
  7.2 1.4 copy.22
  8.7 0.0 copy-start.2
  8.7 0.0 copy-start.3
  8.7 2.8 pad_maximum_fusion
  11.5 0.0 all-gather.2.cloned.1.call-update
  11.6 0.0 reduce-scatter.5.cloned.1.call-start
  11.6 0.0 copy-done.2
  11.6 0.0 copy-done.3
  11.7 0.6 maximum_bitcast_fusion.gain_ref
  12.2 1.2 fusion
  13.5 107.6 %attend.1 = (bf16[1024,2048]{1,0:T(8,128)(2,1)}, f32[1,2048]{1,0:T(1,128)}, f32[1,2048]{1,0:T(1,128)}, bf16[640,1024]{1,0:T(8,128)(2,1)}, bf16[1024,128]{1,0:T(8...) custom-call(bf16[256,2048]{1,0:T(8,128)(2,1)} %x_ref.5, ...), custom_call_target="tpu_custom_call" | custom-call | flops 4831838208 | bytes 367001600 | tf_op jit(solution)/shard_map/attend/pallas_call | solution.py:1066
  121.1 5.9 all-gather.2.cloned.1.call-done.w_hbm.w_mlp_hbm
  126.9 205.2 %mlp.1 = (f32[256,2048]{1,0:T(8,128)}, f32[256,2048]{1,0:T(8,128)}, f32[1,2048]{1,0:T(1,128)}, bf16[4,256,1408]{2,1,0:T(8,128)(2,1)}, bf16[2048,4224]{1,0:T(8,128)(2,1)}, /*index=5*/bf16[4,256,2048]{2,1,0:T(8,128)(2,1)}) custom-call(bf16[4,256,2048]{2,1,0:T(8,128)(2,1)} %bitcast.19, bf16[256,2048]{1,0:T(8,128)(2,1)} %x_ref.5, ...), custom_call_target="tpu_custom_call" | custom-call | flops 53150220288 | bytes 524288000 | tf_op jit(solution)/shard_map/mlp/pallas_call | solution.py:632
  332.1 113.7 %attend_back.1 = (bf16[256,2048]{1,0:T(8,128)(2,1)}, bf16[1024,2048]{1,0:T(8,128)(2,1)}, bf16[2048,1152]{1,0:T(8,128)(2,1)}) custom-call(f32[256,2048]{1,0:T(8,128)} %get-tuple-element.43.mid_ref, bf16[1024,128]{1,0:T(8,128)(2,1)} %get-tuple-element.44.kv_ref, f32[8,1024]{1,0:T(8,128)} %get-tuple-element.45.log_ref, f32[32,1024]{1,0:T(8,128)} %get-tuple-element.72.cos_ref, ...), custom_call_target="tpu_custom_call" | custom-call | flops 14495514624 | bytes 367001600 | tf_op jit(solution)/shard_map/attend_back/pallas_call | solution.py:1274
  445.8 0.0 reduce-scatter.5.cloned.1.call-update
  445.8 0.0 reduce-scatter.3.cloned.1.call-start
  445.9 0.7 reduce-scatter.3.cloned.1.call-update
  446.6 85.9 %sum_input_grad.1 = (bf16[256,2048]{1,0:T(8,128)(2,1)}, f32[1,128]{1,0:T(1,128)}) custom-call(bf16[4,256,2048]{2,1,0:T(8,128)(2,1)} %bitcast.13, bf16[256,2048]{1,0:T(8,128)(2,1)} %x_ref.5, f32[1,2048]{1,0:T(1,128)} %get-tuple-element.55.gain_ref, f32[256,2048]{1,0:T(8,128)} %get-tuple-element.56.grad_mid_ref, f32[1,2048]{1,0:T(1,128)} %get-tuple-element.57.dgain_mlp_ref), custom_call_target="tpu_custom_call" | custom-call | bytes 262144000 | tf_op jit(solution)/shard_map/sum_input_grad/pallas_call | solution.py:716
  532.5 0.0 copy-start
  532.5 0.0 copy-start.1
  532.5 1.4 slice_bitcast_fusion
  533.9 0.0 reduce-scatter.5.cloned.1.call-done.attn_ref
  533.9 87.8 %reduce-scatter.3.cloned.1.call-done.mlp_ref = bf16[256,4224]{1,0:T(8,128)(2,1)} async-done(((bf16[2048,4224]{1,0:T(8,128)(2,1)}), bf16[256,4224]{1,0:T(8,128)(2,1)}) %reduce-scatter.3.cloned.1.call-update) | async-done | bytes 2162704 | tf_op jit(solution)/shard_map/reduce_scatter | solution.py:1340
  621.7 4.6 widen.1
  626.3 0.0 copy-done
  626.3 1.0 copy.25
  627.3 0.0 copy-done.1
  627.3 1.0 copy.26
  (1 shorter events, 0.0 us)
Async XLA Ops:
  7.2 119.8 %all-gather.2.cloned.1.call-start = ((), (), s32[]{:S(2)}) async-start(), calls=%async_computation.2 | async-start | bytes 19464192 | tf_op jit(solution)/shard_map/all_gather | solution.py:1320
  8.7 3.0 copy-start.2
  8.7 3.0 copy-start.3
  11.6 522.3 %reduce-scatter.5.cloned.1.call-start = ((), (), s32[]{:S(2)}) async-start(), calls=%async_computation.4 | async-start | bytes 5308416 | tf_op jit(solution)/shard_map/reduce_scatter | solution.py:1344
  445.8 175.9 %reduce-scatter.3.cloned.1.call-start = ((), (), s32[]{:S(2)}) async-start(), calls=%async_computation.3 | async-start | bytes 19464192 | tf_op jit(solution)/shard_map/reduce_scatter | solution.py:1340
  532.5 93.8 %copy-start = (bf16[256,2048]{1,0:T(8,128)(2,1)S(1)}, bf16[256,2048]{1,0:T(8,128)(2,1)}, u32[]{:S(2)}) copy-start(bf16[256,2048]{1,0:T(8,128)(2,1)} %get-tuple-element.84) | copy-start | bytes 3145732
  532.5 94.8 %copy-start.1 = (bf16[256,2048]{1,0:T(8,128)(2,1)S(1)}, bf16[256,2048]{1,0:T(8,128)(2,1)}, u32[]{:S(2)}) copy-start(bf16[256,2048]{1,0:T(8,128)(2,1)} %get-tuple-element.85) | copy-start | bytes 3145732
Sparse Core Ops, SparseCore 0:
  11.7 115.2 all-gather.1
  446.0 53.1 reduce-scatter.4
  502.8 118.8 reduce-scatter.2

commit v4 on v3

--- a/solution.py
+++ b/solution.py
@@ -19,6 +19,7 @@
 BF16 = jnp.bfloat16
 VMEM_SPEC = pl.BlockSpec(memory_space=pltpu.VMEM)
 EARLY = 0
+FAR_DONE = 3
 
 
 def tables(sequence_length):
@@ -353,21 +354,36 @@
 
 
 def mlp_kernel(
-    n, pieces, part_ref, x_ref, gain_ref, w_hbm, cot_hbm, near_hbm,
-    mid_ref, grad_ref, dgain_ref, hid_hbm, wgrad_hbm, low_hbm,
-    w, cot, seq, buf, npart, buf_back, hid, dgate, dup, stage, inv_ref,
-    ssend, srecv, gsend, grecv, bsend, brecv, csend, crecv, lsend, lrecv, local_sem, stage_sem,
+    n, pieces, gain_ref, part_hbm, x_hbm, w_hbm, cot_hbm, near_hbm,
+    dgain_ref, mid_hbm, grad_hbm, hid_hbm, wgrad_hbm, low_hbm,
+    part_ref, x_ref, mid_ref, grad_ref, w, cot, seq, buf, npart, buf_back, hid, dgate, dup, stage, inv_ref,
+    ssend, srecv, gsend, grecv, bsend, brecv, csend, crecv, lsend, lrecv, local_sem, stage_sem, part_sem,
 ):
     line = Line(n)
     me = line.me
     rows_all, width = part_ref.shape[1:]
+
+    def part_load(piece):
+        rows = piece_rows(piece, rows_all // pieces)
+        return pltpu.make_async_copy(part_hbm.at[:, rows], part_ref.at[:, rows], part_sem.at[0, piece])
+
+    def piece_save(which, ref, hbm, piece):
+        rows = piece_rows(piece, rows_all // pieces)
+        return pltpu.make_async_copy(ref.at[rows], hbm.at[rows], part_sem.at[which, piece])
+
+    x_load = pltpu.make_async_copy(x_hbm, x_ref, local_sem.at[3])
+    for piece in range(pieces):
+        part_load(piece).start()
+    x_load.start()
+
     units = hid.shape[2]
     weight_load = pltpu.make_async_copy(w_hbm, w, local_sem.at[0])
     own_load = pltpu.make_async_copy(cot_hbm, cot.at[me], local_sem.at[1])
     inner = (me > 0) & (me < n - 1)
 
-    def near_load(shard):
-        return pltpu.make_async_copy(near_hbm.at[shard], cot.at[shard], local_sem.at[5 + shard])
+    def near_load(shard, count):
+        rows = pl.ds(0, count)
+        return pltpu.make_async_copy(near_hbm.at[shard, rows], cot.at[shard, rows], local_sem.at[5 + shard])
 
     def each_near(act):
         for shard in range(n):
@@ -375,7 +391,13 @@
 
             @pl.when(here)
             def _():
-                act(near_load(shard))
+                act(near_load(shard, rows_all))
+
+            if n == 4:
+
+                @pl.when(jnp.logical_not(inner) & ((me - shard == 2) | (shard - me == 2)))
+                def _():
+                    act(near_load(shard, rows_all // pieces * FAR_DONE))
 
     each_near(lambda copy: copy.start())
     own_load.start()
@@ -387,41 +409,48 @@
     cot_gather = Gather(line, cot, csend, crecv, pieces)
     low_gather = Gather(line, buf, lsend, lrecv, pieces)
     size = scatter.size
+    part_load(0).wait()
     scatter.start_ends(0)
+    for piece in range(1, pieces):
+        part_load(piece).wait()
+    x_load.wait()
     dgain_ref[...] = jnp.zeros_like(dgain_ref)
 
     each_near(lambda copy: copy.wait())
 
-    def each_far(act):
+    def still_far(hop, piece):
+        return (piece >= FAR_DONE) if hop == 2 and n == 4 else (piece >= 0)
+
+    def each_far(piece, act):
         for hop in range(2, n):
 
-            @pl.when(me == n - 2)
+            @pl.when((me == n - 2) & still_far(hop, piece))
             def _():
                 act(True, hop, me - (hop - 1))
 
-            @pl.when(me == 1)
+            @pl.when((me == 1) & still_far(hop, piece))
             def _():
                 act(False, hop, me + (hop - 1))
 
     def far_start(piece):
-        each_far(lambda right, hop, shard: cot_gather.message(right, hop, piece, shard).start())
+        each_far(piece, lambda right, hop, shard: cot_gather.message(right, hop, piece, shard).start())
 
     def far_sent(piece):
-        each_far(lambda right, hop, shard: cot_gather.message(right, hop, piece, shard).wait_send())
+        each_far(piece, lambda right, hop, shard: cot_gather.message(right, hop, piece, shard).wait_send())
 
     def far_arrived(piece):
         for hop in range(2, n):
 
-            @pl.when(me == n - 1)
+            @pl.when((me == n - 1) & still_far(hop, piece))
             def _():
                 cot_gather.message(True, hop, piece, me - hop).wait_recv()
 
-            @pl.when(me == 0)
+            @pl.when((me == 0) & still_far(hop, piece))
             def _():
                 cot_gather.message(False, hop, piece, me + hop).wait_recv()
 
-    for piece in range(min(2, pieces)):
-        far_start(piece)
+    for piece in range(min(3, pieces)):
+        far_start(jnp.int32(piece))
 
     def norm(piece):
         rows = scatter.rows(piece)
@@ -434,6 +463,7 @@
         inv = lax.rsqrt(jnp.mean(mid * mid, axis=1, keepdims=True) + EPS)
         inv_ref[rows, :] = jnp.broadcast_to(inv, (size, LANES))
         seq[me, rows, :] = (mid * inv * gain_ref[...]).astype(BF16)
+        piece_save(1, mid_ref, mid_hbm, piece).start()
 
     def back(piece):
         rows = scatter.rows(piece)
@@ -451,6 +481,7 @@
         out = cot[me, rows, :].astype(F32) + inv * (scaled - mid * (inv * inv * mean))
         grad_ref[rows, :] = out
         buf[me, rows, :] = out.astype(BF16)
+        piece_save(2, grad_ref, grad_hbm, piece).start()
 
     def flat(ref, piece):
         value = ref[:, scatter.rows(piece), :]
@@ -525,9 +556,9 @@
 
             scatter.middle(step)
 
-            @pl.when(step + 2 < pieces)
+            @pl.when(step + 3 < pieces)
             def _():
-                far_start(step + 2)
+                far_start(step + 3)
 
         for hop in range(1, n):
             piece = step - hop
@@ -590,8 +621,8 @@
         (lambda step: lambda: low_arrivals(step))(step) for step in range(pieces - 1, pieces + n - 2)
     ]
     events = [
-        (count * 3 // 8, lambda: scatter_back.first(last)),
-        (count * 3 // 4, lambda: scatter_back.rest(last)),
+        (count // 4, lambda: scatter_back.first(last)),
+        (count * 5 // 8, lambda: scatter_back.rest(last)),
     ]
     if EARLY:
         events += [(count * (2 * i + 1) // (2 * len(late)), event) for i, event in enumerate(late)]
@@ -604,7 +635,7 @@
     if EARLY:
         low_saves.append(
             pltpu.make_async_copy(
-                buf.at[pl.ds(0, n), early_rows], low_hbm.at[:, early_rows], local_sem.at[3]
+                buf.at[pl.ds(0, n), early_rows], low_hbm.at[:, early_rows], local_sem.at[0]
             )
         )
     for save_low in low_saves:
@@ -617,6 +648,8 @@
     @pl.loop(0, pieces)
     def _(piece):
         far_sent(piece)
+        piece_save(1, mid_ref, mid_hbm, piece).wait()
+        piece_save(2, grad_ref, grad_hbm, piece).wait()
 
     for save_low in low_saves:
         save_low.wait()
@@ -632,16 +665,20 @@
     return pl.pallas_call(
         functools.partial(mlp_kernel, n, pieces),
         out_shape=(
+            jax.ShapeDtypeStruct((1, width), F32),
             jax.ShapeDtypeStruct((rows, width), F32),
             jax.ShapeDtypeStruct((rows, width), F32),
-            jax.ShapeDtypeStruct((1, width), F32),
             jax.ShapeDtypeStruct((n, rows, units), BF16),
             jax.ShapeDtypeStruct((width, 3 * units), BF16),
             jax.ShapeDtypeStruct((n, rows, width), BF16),
         ),
-        in_specs=[VMEM_SPEC] * 3 + [any_spec] * 3,
-        out_specs=(VMEM_SPEC,) * 3 + (any_spec,) * 3,
+        in_specs=[VMEM_SPEC] + [any_spec] * 5,
+        out_specs=(VMEM_SPEC,) + (any_spec,) * 5,
         scratch_shapes=[
+            pltpu.VMEM((n, rows, width), BF16),
+            pltpu.VMEM((rows, width), BF16),
+            pltpu.VMEM((rows, width), F32),
+            pltpu.VMEM((rows, width), F32),
             pltpu.VMEM((width, 3 * units), BF16),
             pltpu.VMEM((n, rows, width), BF16),
             pltpu.VMEM((n, rows, width), BF16),
@@ -655,7 +692,7 @@
             pltpu.VMEM((rows, LANES), F32),
         ]
         + sems(n, pieces) * 5
-        + [pltpu.SemaphoreType.DMA((5 + n,)), pltpu.SemaphoreType.DMA((2,))],
+        + [pltpu.SemaphoreType.DMA((5 + n,)), pltpu.SemaphoreType.DMA((2,)), pltpu.SemaphoreType.DMA((3, pieces))],
         compiler_params=pltpu.CompilerParams(
             collective_id=2, has_side_effects=True, vmem_limit_bytes=67043328
         ),
@@ -663,18 +700,35 @@
             flops=18 * n * rows * width * units, bytes_accessed=500 * 1024 * 1024, transcendentals=0
         ),
         name="mlp",
-    )(part.reshape(n, rows, width), x, gain, weights, cotangent, near)
+    )(gain, part.reshape(n, rows, width), x, weights, cotangent, near)
 
 
 def last_kernel(
-    n, dp, pieces, part_ref, x_ref, gain_ref, grad_mid_ref, dgain_mlp_ref, out_ref, gains_ref,
-    total_ref, dgain_ref, packed, held, buf, ssend, srecv, gsend, grecv,
+    n, dp, pieces, gain_ref, dgain_mlp_ref, part_hbm, x_hbm, grad_mid_hbm, out_ref, gains_ref,
+    part_ref, x_ref, grad_mid_ref, total_ref, dgain_ref, packed, held, buf, ssend, srecv, gsend, grecv, load_sem,
 ):
+    def part_load(piece):
+        rows = piece_rows(piece, part_ref.shape[1] // pieces)
+        return pltpu.make_async_copy(part_hbm.at[:, rows], part_ref.at[:, rows], load_sem.at[2 + piece])
+
+    others = [
+        pltpu.make_async_copy(x_hbm, x_ref, load_sem.at[0]),
+        pltpu.make_async_copy(grad_mid_hbm, grad_mid_ref, load_sem.at[1]),
+    ]
+    for piece in range(pieces):
+        part_load(piece).start()
+    for load in others:
+        load.start()
     line = Line(n)
     all_me = lax.axis_index("dp") * n + line.me
     barrier_all(n, dp)
     scatter = Scatter(line, part_ref, buf, ssend, srecv, pieces)
+    part_load(0).wait()
     scatter.start_ends(0)
+    for piece in range(1, pieces):
+        part_load(piece).wait()
+    for load in others:
+        load.wait()
     dgain_ref[...] = jnp.zeros_like(dgain_ref)
     packed[...] = jnp.zeros_like(packed)
 
@@ -711,17 +765,21 @@
     scatter.finish()
 
 
-def sum_input_grad(n, dp, part, x, gain, grad_mid, dgain_mlp, packed, pieces=4):
+def sum_input_grad(n, dp, part, x, gain, grad_mid, dgain_mlp, packed, pieces=8):
     rows, width = x.shape
+    any_spec = pl.BlockSpec(memory_space=pl.ANY)
     return pl.pallas_call(
         functools.partial(last_kernel, n, dp, pieces),
         out_shape=(
             jax.ShapeDtypeStruct((rows, width), BF16),
             jax.ShapeDtypeStruct((1, packed), F32),
         ),
-        in_specs=[VMEM_SPEC] * 5,
+        in_specs=[VMEM_SPEC] * 2 + [any_spec] * 3,
         out_specs=(VMEM_SPEC,) * 2,
         scratch_shapes=[
+            pltpu.VMEM((n, rows, width), BF16),
+            pltpu.VMEM((rows, width), BF16),
+            pltpu.VMEM((rows, width), F32),
             pltpu.VMEM((rows // pieces, width), F32),
             pltpu.VMEM((1, width), F32),
             pltpu.VMEM((n * dp, 1, packed), F32),
@@ -729,15 +787,25 @@
             pltpu.VMEM((n + 1, rows, width), BF16),
         ]
         + sems(n, pieces)
-        + [pltpu.SemaphoreType.DMA((n * dp,)), pltpu.SemaphoreType.DMA((n * dp,))],
+        + [pltpu.SemaphoreType.DMA((n * dp,)), pltpu.SemaphoreType.DMA((n * dp,))]
+        + [pltpu.SemaphoreType.DMA((2 + pieces,))],
         compiler_params=comm_params(4),
         cost_estimate=pl.CostEstimate(flops=0, bytes_accessed=250 * 1024 * 1024, transcendentals=0),
         name="sum_input_grad",
-    )(part.reshape(n, rows, width), x, gain, grad_mid, dgain_mlp)
-
-
-def widen_kernel(mlp_ref, attn_ref, gate_ref, up_ref, down_ref, query_ref, key_ref, value_ref, out_ref):
+    )(gain, dgain_mlp, part.reshape(n, rows, width), x, grad_mid)
+
+
+def widen_kernel(
+    mlp_ref, attn_ref, gains_ref, rows_ref, input_ref,
+    gate_ref, up_ref, down_ref, query_ref, key_ref, value_ref, out_ref,
+    attn_gain_ref, mlp_gain_ref, rows_out_ref, input_out_ref,
+):
     units = gate_ref.shape[1]
+    per = attn_gain_ref.shape[1]
+    attn_gain_ref[...] = gains_ref[:, :per]
+    mlp_gain_ref[...] = gains_ref[:, per : 2 * per]
+    rows_out_ref[...] = rows_ref[...]
+    input_out_ref[...] = input_ref[...]
     gate_ref[...] = mlp_ref[:, :units].astype(F32)
     up_ref[...] = mlp_ref[:, units : 2 * units].astype(F32)
     down_ref[...] = mlp_ref[:, 2 * units :].astype(F32).T
@@ -748,17 +816,18 @@
     out_ref[...] = attn_ref[:, q_cols + 2 * k_cols :].astype(F32).T
 
 
-def widen(mlp_grad, attn_grad, q_cols, k_cols):
+def widen(mlp_grad, attn_grad, gains, rows_out, input_out, per, q_cols, k_cols):
     rows, units = mlp_grad.shape[0], mlp_grad.shape[1] // 3
     shapes = [(rows, units)] * 2 + [(units, rows), (rows, q_cols)] + [(k_cols, rows)] * 2 + [(q_cols, rows)]
     return pl.pallas_call(
         widen_kernel,
-        out_shape=tuple(jax.ShapeDtypeStruct(shape, F32) for shape in shapes),
-        in_specs=[VMEM_SPEC] * 2,
-        out_specs=(VMEM_SPEC,) * 7,
+        out_shape=tuple(jax.ShapeDtypeStruct(shape, F32) for shape in shapes + [(1, per)] * 2)
+        + (jax.ShapeDtypeStruct(rows_out.shape, BF16),) * 2,
+        in_specs=[VMEM_SPEC] * 5,
+        out_specs=(VMEM_SPEC,) * 11,
         compiler_params=pltpu.CompilerParams(vmem_limit_bytes=56 * 1024 * 1024),
         name="widen",
-    )(mlp_grad, attn_grad)
+    )(mlp_grad, attn_grad, gains, rows_out, input_out)
 
 
 def rotate(half_a, half_b, cos, sin):
@@ -777,8 +846,8 @@
 
 def attend_kernel(
     n, dp, heads, block, pieces, x_ref, gain_ref, cos_ref, sin_ref, cot_hbm, wq_hbm, wk_hbm, wv_hbm, wo_hbm,
-    norm_ref, attn_gain_ref, mlp_gain_ref, qkv_ref, kv_ref, out_ref, log_ref, part_ref, w_ref, wo_ref, near_hbm,
-    seq, act_ref, mask_ref, gains, wq, wk, wv, wo, send, recv, gsend, grecv, wsend, wrecv, own_sem, csend, crecv,
+    attn_gain_ref, mlp_gain_ref, kv_ref, out_ref, log_ref, norm_hbm, qkv_hbm, part_hbm, w_out_hbm, wo_out_hbm, near_hbm,
+    norm_ref, qkv_ref, part_ref, w_ref, wo_ref, seq, act_ref, mask_ref, gains, wq, wk, wv, wo, send, recv, gsend, grecv, wsend, wrecv, own_sem, csend, crecv, fsend, frecv, save_sem,
 ):
     half = HEAD_SIZE // 2
     rows_all, width = x_ref.shape
@@ -855,6 +924,13 @@
     q_cols, k_cols = wq.shape[2], wk.shape[1]
     w_rows, w_cols = wq.shape[1], wo.shape[2]
 
+    saves = [
+        pltpu.make_async_copy(src, dst, save_sem.at[i])
+        for i, (src, dst) in enumerate(
+            ((w_ref, w_out_hbm), (wo_ref, wo_out_hbm), (norm_ref, norm_hbm), (qkv_ref, qkv_hbm))
+        )
+    ]
+
     def project(shard):
         x = seq[shard].astype(F32)
         inv = lax.rsqrt(jnp.mean(x * x, axis=1, keepdims=True) + EPS)
@@ -890,6 +966,8 @@
             w_ref[rows, q_cols : q_cols + k_cols] = wk[d].T
             w_ref[rows, q_cols + k_cols :] = wv[d].T
             wo_ref[:, d * w_cols : (d + 1) * w_cols] = wo[d]
+        saves[0].start()
+        saves[1].start()
         project(me)
 
     def start_pair():
@@ -905,6 +983,11 @@
         def _(offset):
             for i in range(4):
                 pair_copy(i, offset).start()
+
+    def arrived(d, hop, shard):
+        cot_copy_in(
+            line, near_hbm, shard, crecv.at[d, hop - 1], csend.at[d, hop - 1], 1 if d == 1 else -1
+        ).wait_recv()
 
     ready = min(2, n - 1)
     for hop in range(1, n):
@@ -944,6 +1027,23 @@
                 project_at(earlier)
         elif hop > ready:
             project_at(hop)
+
+    def far_copy(right, shard):
+        part = near_hbm.at[shard, pl.ds(0, rows_all // pieces * FAR_DONE)]
+        d = 0 if right else 1
+        return line.copy(part, part, fsend.at[d], frecv.at[d], jnp.where(inner, 1 if right else -1, jnp.where(me == 0, 1, -1)))
+
+    if n == 4:
+
+        @pl.when(me == 1)
+        def _():
+            arrived(1, 1, me + 1)
+            far_copy(False, me + 1).start()
+
+        @pl.when(me == 2)
+        def _():
+            arrived(0, 1, me - 1)
+            far_copy(True, me - 1).start()
 
     cos, sin = cos_ref[...], sin_ref[...]
 
@@ -960,6 +1060,8 @@
 
     values = pl.ds((heads + 1) * HEAD_SIZE, HEAD_SIZE)
     qkv_ref[values, :] = act_ref[values, :].astype(BF16)
+    saves[2].start()
+    saves[3].start()
     mask_ref[...] = mask_block(block)
     kv_ref[...] = qkv_ref[pl.ds(heads * HEAD_SIZE, 2 * HEAD_SIZE), :].T
 
@@ -993,8 +1095,15 @@
     for start, count in tiles(width, 512):
         cols = slice(start, start + count)
         part_ref[:, cols] = mm(out_ref[...], wo_ref[:, cols], 0, 0).astype(BF16)
+        save = pltpu.make_async_copy(
+            part_ref.at[:, pl.ds(start, count)], part_hbm.at[:, pl.ds(start, count)], save_sem.at[len(saves)]
+        )
+        save.start()
+        saves.append(save)
 
     gather.finish()
+    for save in saves:
+        save.wait()
 
     @pl.loop(1, dp // 2)
     def _(offset):
@@ -1006,24 +1115,27 @@
         for i in range(4):
             pair_copy(i, offset).wait_send()
 
-    def arrived(d, hop, shard):
-        cot_copy_in(
-            line, near_hbm, shard, crecv.at[d, hop - 1], csend.at[d, hop - 1], 1 if d == 1 else -1
-        ).wait_recv()
-
     if n == 4:
 
         @pl.when(me == 1)
         def _():
-            arrived(1, 1, me + 1)
             arrived(1, 2, me + 2)
             cot_copy(True, 2).wait_send()
+            far_copy(False, me + 1).wait_send()
 
         @pl.when(me == 2)
         def _():
-            arrived(0, 1, me - 1)
             arrived(0, 2, me - 2)
             cot_copy(False, 2).wait_send()
+            far_copy(True, me - 1).wait_send()
+
+        @pl.when(me == 0)
+        def _():
+            far_copy(False, me + 2).wait_recv()
+
+        @pl.when(me == n - 1)
+        def _():
+            far_copy(True, me - 2).wait_recv()
 
     else:
 
@@ -1066,21 +1178,26 @@
     return pl.pallas_call(
         functools.partial(attend_kernel, n, dp, heads, block, pieces),
         out_shape=(
-            jax.ShapeDtypeStruct((length, width), BF16),
             jax.ShapeDtypeStruct((1, width), F32),
             jax.ShapeDtypeStruct((1, width), F32),
-            jax.ShapeDtypeStruct((cols_in, length), BF16),
             jax.ShapeDtypeStruct((length, 2 * HEAD_SIZE), BF16),
             jax.ShapeDtypeStruct((heads * HEAD_SIZE, length), BF16),
             jax.ShapeDtypeStruct((heads, length), F32),
+            jax.ShapeDtypeStruct((length, width), BF16),
+            jax.ShapeDtypeStruct((cols_in, length), BF16),
             jax.ShapeDtypeStruct((length, width), BF16),
             jax.ShapeDtypeStruct((width, cols_in), BF16),
             jax.ShapeDtypeStruct((q_cols, width), BF16),
             jax.ShapeDtypeStruct((n,) + cotangent.shape, BF16),
         ),
         in_specs=[VMEM_SPEC] * 4 + [any_spec] * 5,
-        out_specs=(VMEM_SPEC,) * 10 + (any_spec,),
+        out_specs=(VMEM_SPEC,) * 5 + (any_spec,) * 6,
         scratch_shapes=[
+            pltpu.VMEM((length, width), BF16),
+            pltpu.VMEM((cols_in, length), BF16),
+            pltpu.VMEM((length, width), BF16),
+            pltpu.VMEM((width, cols_in), BF16),
+            pltpu.VMEM((q_cols, width), BF16),
             pltpu.VMEM((n, rows, width), BF16),
             pltpu.VMEM((cols_in, length), F32),
             pltpu.VMEM((block, block), F32),
@@ -1089,7 +1206,7 @@
         + [pltpu.VMEM((dp,) + w.shape, BF16) for w in weights]
         + sems(n, pieces)
         + [dma((n * dp,)), dma((n * dp,)), dma((2, 4, dp // 2)), dma((2, 4, dp // 2)), dma((4,))]
-        + [dma((2, 2)), dma((2, 2))],
+        + [dma((2, 2)), dma((2, 2)), dma((2,)), dma((2,)), dma((4 + len(tiles(width, 512)),))],
         compiler_params=comm_params(1),
         cost_estimate=pl.CostEstimate(
             flops=2 * length * width * (cols_in + q_cols),
@@ -1101,10 +1218,10 @@
 
 
 def attend_back_kernel(
-    n, heads, block, pieces, mid_ref, kv_ref, log_ref, cos_ref, sin_ref,
-    low_hbm, hid_hbm, w_mlp_hbm, wo_hbm, w_hbm, qkv_hbm, out_hbm, norm_hbm,
-    rows_ref, part_ref, wgrad_hbm,
-    seq, hid, w_down, down_ref, buf, wo_ref, w_ref, qkv_ref, out_ref, norm_ref,
+    n, heads, block, pieces, kv_ref, log_ref, cos_ref, sin_ref,
+    mid_hbm, low_hbm, hid_hbm, w_mlp_hbm, wo_hbm, w_hbm, qkv_hbm, out_hbm, norm_hbm,
+    rows_ref, part_hbm, wgrad_hbm,
+    mid_ref, part_ref, seq, hid, w_down, down_ref, buf, wo_ref, w_ref, qkv_ref, out_ref, norm_ref,
     dkv, mask_ref, grad_ref, dqkv_ref, wgrad, ssend, srecv, gsend, grecv, load_sem, save_sem,
 ):
     half = HEAD_SIZE // 2
@@ -1124,6 +1241,7 @@
         (out_hbm, out_ref),
         (w_hbm, w_ref),
         (norm_hbm, norm_ref),
+        (mid_hbm, mid_ref),
     )
     if EARLY:
         pairs += ((low_hbm.at[:, early_rows], seq.at[:, early_rows]),)
@@ -1237,6 +1355,17 @@
     dqkv_ref[pl.ds(heads * HEAD_SIZE + half, half), :] = b.astype(BF16)
     dqkv_ref[pl.ds((heads + 1) * HEAD_SIZE, HEAD_SIZE), :] = dkv[1].T.astype(BF16)
     saves = []
+    count_tiles = len(tiles(width, 512))
+    for index, (start, count) in enumerate(tiles(width, 512)):
+        cols = slice(start, start + count)
+        part_ref[:, cols] = mm(dqkv_ref[...], w_ref[cols, :], 0, 1).astype(BF16)
+        save = pltpu.make_async_copy(
+            part_ref.at[:, pl.ds(start, count)],
+            part_hbm.at[:, pl.ds(start, count)],
+            save_sem.at[count_tiles + index],
+        )
+        save.start()
+        saves.append(save)
     for index, (start, count) in enumerate(tiles(width, 512)):
         cols = slice(start, start + count)
         wgrad[cols, :cols_in] = mm(norm_ref[:, cols], dqkv_ref[...], 0, 1).astype(BF16)
@@ -1249,9 +1378,6 @@
         )
         save.start()
         saves.append(save)
-    for start, count in tiles(width, 512):
-        cols = slice(start, start + count)
-        part_ref[:, cols] = mm(dqkv_ref[...], w_ref[cols, :], 0, 1).astype(BF16)
     for piece in range(min(n, pieces) - 1, pieces):
         sum_piece(piece)
     scatter.finish()
@@ -1278,9 +1404,11 @@
             jax.ShapeDtypeStruct((length, width), BF16),
             jax.ShapeDtypeStruct(wgrad_shape, BF16),
         ),
-        in_specs=[VMEM_SPEC] * 5 + [any_spec] * 8,
-        out_specs=(VMEM_SPEC,) * 2 + (any_spec,),
+        in_specs=[VMEM_SPEC] * 4 + [any_spec] * 9,
+        out_specs=(VMEM_SPEC,) + (any_spec,) * 2,
         scratch_shapes=[
+            pltpu.VMEM(mid.shape, F32),
+            pltpu.VMEM((length, width), BF16),
             pltpu.VMEM((n, rows, width), BF16),
             pltpu.VMEM((n, rows, units), BF16),
             pltpu.VMEM((width, units), BF16),
@@ -1298,7 +1426,7 @@
             pltpu.VMEM(wgrad_shape, BF16),
         ]
         + sems(n, pieces) * 2
-        + [pltpu.SemaphoreType.DMA((9,)), pltpu.SemaphoreType.DMA((len(tiles(width, 512)),))],
+        + [pltpu.SemaphoreType.DMA((9,)), pltpu.SemaphoreType.DMA((2 * len(tiles(width, 512)),))],
         compiler_params=comm_params(3),
         cost_estimate=pl.CostEstimate(
             flops=6 * length * width * wgrad_shape[1],
@@ -1306,7 +1434,7 @@
             transcendentals=heads * length * length,
         ),
         name="attend_back",
-    )(mid, kv, log_total, cos, sin, low, hidden, w_mlp, w_out, w_qkv, qkv, out, norm)
+    )(kv, log_total, cos, sin, mid, low, hidden, w_mlp, w_out, w_qkv, qkv, out, norm)
 
 
 def local(
@@ -1324,7 +1452,7 @@
     if packed > 2 * per:
         gains.append(jnp.zeros((packed - 2 * per,), F32))
     cos, sin = tables(length)
-    norm_attn, full_attn, full_mlp, qkv, kv, attended, log_total, out_part, w_qkv, w_out_all, near = attend(
+    full_attn, full_mlp, kv, attended, log_total, norm_attn, qkv, out_part, w_qkv, w_out_all, near = attend(
         n,
         dp,
         x,
@@ -1334,7 +1462,7 @@
         sin,
         cotangent,
     )
-    mid, grad_mid, dgain_mlp, hidden, mlp_grad, grad_low = mlp(
+    dgain_mlp, mid, grad_mid, hidden, mlp_grad, grad_low = mlp(
         n, out_part, x, full_mlp, mlp_all, cotangent, near
     )
     mlp_grad = lax.psum_scatter(mlp_grad, "dp", scatter_dimension=0, tiled=True)
@@ -1342,15 +1470,17 @@
         n, mid, kv, log_total, cos, sin, grad_low, hidden, mlp_all, w_out_all, w_qkv, qkv, attended, norm_attn
     )
     attn_grad = lax.psum_scatter(attn_grad, "dp", scatter_dimension=0, tiled=True)
-    input_grad, dgains = sum_input_grad(n, dp, attn_part, x, full_attn, grad_mid, dgain_mlp, packed)
-    gate, up, down, query, key, value, out = widen(
-        mlp_grad, attn_grad, w_query.shape[1], w_key.shape[1]
+    input_grad, dgains = sum_input_grad(
+        n, dp, attn_part, x, full_attn, grad_mid, dgain_mlp, packed
+    )
+    gate, up, down, query, key, value, out, dgain_attn, dgain_mlp, block_output, input_grad = widen(
+        mlp_grad, attn_grad, dgains, block_output, input_grad, per, w_query.shape[1], w_key.shape[1]
     )
     return (
         block_output,
         input_grad,
-        dgains[0, :per],
-        dgains[0, per : 2 * per],
+        dgain_attn.reshape(per),
+        dgain_mlp.reshape(per),
         query,
         key.T,
         value.T,

time: 643 us -> 624 us (0.970)
  Pallas kernels: 517 us -> 506 us
    pallas_call x1, Pallas kernels: 205 us -> 185 us  [mlp(): pl.pallas_call(functools.partial(mlp_kernel, n, pieces), out_shape=(jax.S...]
    pallas_call x1, Pallas kernels: 108 us -> 120 us  [attend(): pl.pallas_call(functools.partial(attend_kernel, n, dp, heads, block, piec...]
  transfers between devices with their start and end apart: 3 -> 3, of which waited for: 2 -> 1; matrix products, arithmetic and copies ran while one was open for 1% -> 0% of each run, Pallas kernels for 30% -> 33%
where the time goes in v4:
time: 624 us; the launch traced here: 616 us
  Pallas kernels  506 us (81%)
  waiting for transfers between devices  90.2 us (14%)
  between operations  14.2 us (2%)
    pallas_call x1, Pallas kernels, mlp(): pl.pallas_call(functools.partial(mlp_kernel, n, pieces), out_shape=(jax.S...  185 us
    pallas_call x1, Pallas kernels, attend(): pl.pallas_call(functools.partial(attend_kernel, n, dp, heads, block, piec...  120 us
    pallas_call x1, Pallas kernels, attend_back(): pl.pallas_call(functools.partial(attend_back_kernel, n, heads, block, pie...  109 us
    reduce_scatter x1, waiting for transfers between devices, local(): mlp_grad = lax.psum_scatter(mlp_grad, 'dp', scatter_dimension=0, tiled=True)  89.4 us
    pallas_call x1, Pallas kernels, sum_input_grad(): pl.pallas_call(functools.partial(last_kernel, n, dp, pieces), out_shape=(...  86 us
  transfers between devices with their start and end apart: 3, of which 1 were waited for; matrix products, arithmetic and copies ran while one was open for 0% of the time, Pallas kernels for 33%

profile of v4, /device:TPU:0, one launch (start us, length us, event | category | flops | bytes accessed | tf_op | source)
XLA Modules:
  0.0 616.4 jit_solution(13452526518733939256)
XLA Ops:
  7.2 0.0 all-gather.2.cloned.1.call-start
  7.2 1.4 copy.22
  8.7 0.0 copy-start
  8.7 0.0 copy-start.1
  8.7 2.8 pad_maximum_fusion
  11.5 0.0 all-gather.2.cloned.1.call-update
  11.5 0.0 reduce-scatter.5.cloned.1.call-start
  11.6 0.0 copy-done
  11.6 0.0 copy-done.1
  11.6 0.6 maximum_bitcast_fusion.gain_ref
  12.2 1.2 fusion
  13.5 120.0 %attend.1 = (f32[1,2048]{1,0:T(1,128)}, f32[1,2048]{1,0:T(1,128)}, bf16[1024,128]{1,0:T(8,128)(2,1)}, bf16[512,1024]{1,0:T(8,128)(2,1)}, f32[8,1024]{1,0:T(8,128...) custom-call(bf16[256,2048]{1,0:T(8,128)(2,1)} %x_hbm.3, ...), custom_call_target="tpu_custom_call" | custom-call | flops 4831838208 | bytes 367001600 | tf_op jit(solution)/shard_map/attend/pallas_call | solution.py:1178
  133.4 0.0 all-gather.2.cloned.1.call-done.w_hbm.w_mlp_hbm
  133.5 185.0 %mlp.1 = (f32[1,2048]{1,0:T(1,128)}, f32[256,2048]{1,0:T(8,128)}, f32[256,2048]{1,0:T(8,128)}, bf16[4,256,1408]{2,1,0:T(8,128)(2,1)}, bf16[2048,4224]{1,0:T(8,128)(2,1)}, /*index=5*/bf16[4,256,2048]{2,1,0:T(8,128)(2,1)}) custom-call(f32[1,2048]{1,0:T(1,128)} %get-tuple-element.44.gain_ref, bf16[4,256,2048]{2,1,0:T(8,128)(2,1)} %bitcast.19, ...), custom_call_target="tpu_custom_call" | custom-call | flops 53150220288 | bytes 524288000 | tf_op jit(solution)/shard_map/mlp/pallas_call | solution.py:665
  318.4 108.9 %attend_back.1 = (bf16[256,2048]{1,0:T(8,128)(2,1)}, bf16[1024,2048]{1,0:T(8,128)(2,1)}, bf16[2048,1152]{1,0:T(8,128)(2,1)}) custom-call(bf16[1024,128]{1,0:T(8,128)(2,1)} %get-tuple-element.48.kv_ref, f32[8,1024]{1,0:T(8,128)} %get-tuple-element.49.log_ref, f32[32,1024]{1,0:T(8,128)} %get-tuple-element.78.cos_ref, f32[32,1024]{1,0:T(8,128)} %get-tuple-element.77.sin_ref, ...), custom_call_target="tpu_custom_call" | custom-call | flops 14495514624 | bytes 367001600 | tf_op jit(solution)/shard_map/attend_back/pallas_call | solution.py:1400
  427.4 0.0 reduce-scatter.5.cloned.1.call-update
  427.4 0.0 reduce-scatter.3.cloned.1.call-start
  427.5 0.7 reduce-scatter.3.cloned.1.call-update
  428.1 86.0 %sum_input_grad.1 = (bf16[256,2048]{1,0:T(8,128)(2,1)}, f32[1,128]{1,0:T(1,128)}) custom-call(f32[1,2048]{1,0:T(1,128)} %get-tuple-element.59.gain_ref, f32[1,2048]{1,0:T(1,128)} %get-tuple-element.60.dgain_mlp_ref, bf16[4,256,2048]{2,1,0:T(8,128)(2,1)} %bitcast.11, bf16[256,2048]{1,0:T(8,128)(2,1)} %x_hbm.3, f32[256,2048]{1,0:T(8,128)} %get-tuple-element.62.grad_mid_hbm), custom_call_target="tpu_custom_call" | custom-call | bytes 262144000 | tf_op jit(solution)/shard_map/sum_input_grad/pallas_call | solution.py:771
  514.1 0.0 reduce-scatter.5.cloned.1.call-done.attn_ref
  514.2 89.4 %reduce-scatter.3.cloned.1.call-done.mlp_ref = bf16[256,4224]{1,0:T(8,128)(2,1)} async-done(((bf16[2048,4224]{1,0:T(8,128)(2,1)}), bf16[256,4224]{1,0:T(8,128)(2,1)}) %reduce-scatter.3.cloned.1.call-update) | async-done | bytes 2162704 | tf_op jit(solution)/shard_map/reduce_scatter | solution.py:1468
  603.6 5.9 widen.1
  (1 shorter events, 0.0 us)
Async XLA Ops:
  7.2 126.3 %all-gather.2.cloned.1.call-start = ((), (), s32[]{:S(2)}) async-start(), calls=%async_computation.2 | async-start | bytes 19464192 | tf_op jit(solution)/shard_map/all_gather | solution.py:1448
  8.7 2.9 copy-start
  8.7 2.9 copy-start.1
  11.5 502.6 %reduce-scatter.5.cloned.1.call-start = ((), (), s32[]{:S(2)}) async-start(), calls=%async_computation.4 | async-start | bytes 5308416 | tf_op jit(solution)/shard_map/reduce_scatter | solution.py:1472
  427.4 176.2 %reduce-scatter.3.cloned.1.call-start = ((), (), s32[]{:S(2)}) async-start(), calls=%async_computation.3 | async-start | bytes 19464192 | tf_op jit(solution)/shard_map/reduce_scatter | solution.py:1468
Sparse Core Ops, SparseCore 0:
  11.7 115.2 all-gather.1
  427.5 53.4 reduce-scatter.4
  484.7 118.8 reduce-scatter.2

commit v5 on v4

--- a/solution.py
+++ b/solution.py
@@ -347,6 +347,10 @@
         )
 
     pl.semaphore_wait(barrier, devices - 1)
+
+
+def even_tile(extent):
+    return 512 if extent % 512 == 0 else extent
 
 
 def tiles(extent, size):
@@ -503,11 +507,14 @@
             dgate[:, rows, cols] = (
                 (dhidden * up * sigmoid * (1.0 + gate * (1.0 - sigmoid))).astype(BF16).reshape(shape)
             )
-        for start, count in tiles(width, 512):
-            cols = slice(start, start + count)
+        tile = even_tile(width)
+
+        @pl.loop(0, width // tile)
+        def _(index):
+            cols = piece_rows(index, tile)
             total = mm(flat(dgate, piece), w[cols, :units], 1, 1)
             total += mm(flat(dup, piece), w[cols, units : 2 * units], 1, 1)
-            npart[:, rows, cols] = total.astype(BF16).reshape(n, size, count)
+            npart[:, rows, cols] = total.astype(BF16).reshape(n, size, tile)
 
     step_rows = min(LANES, width)
     count = width // step_rows
@@ -704,8 +711,8 @@
 
 
 def last_kernel(
-    n, dp, pieces, gain_ref, dgain_mlp_ref, part_hbm, x_hbm, grad_mid_hbm, out_ref, gains_ref,
-    part_ref, x_ref, grad_mid_ref, total_ref, dgain_ref, packed, held, buf, ssend, srecv, gsend, grecv, load_sem,
+    n, dp, pieces, gain_ref, dgain_mlp_ref, part_hbm, x_hbm, grad_mid_hbm, seq_hbm, out_ref, gains_ref,
+    part_ref, x_ref, grad_mid_ref, seq_ref, total_ref, dgain_ref, packed, held, buf, ssend, srecv, gsend, grecv, load_sem,
 ):
     def part_load(piece):
         rows = piece_rows(piece, part_ref.shape[1] // pieces)
@@ -714,6 +721,7 @@
     others = [
         pltpu.make_async_copy(x_hbm, x_ref, load_sem.at[0]),
         pltpu.make_async_copy(grad_mid_hbm, grad_mid_ref, load_sem.at[1]),
+        pltpu.make_async_copy(seq_hbm, seq_ref, load_sem.at[2 + pieces]),
     ]
     for piece in range(pieces):
         part_load(piece).start()
@@ -732,11 +740,44 @@
     dgain_ref[...] = jnp.zeros_like(dgain_ref)
     packed[...] = jnp.zeros_like(packed)
 
+    width = x_ref.shape[1]
+    per = width // (n * dp)
+    half = pieces // 2
+    share = x_ref.shape[0] // half
+
+    def exchange(**kind):
+        exchange_all(
+            n, dp, lambda peer: packed.at[peer], lambda source: held.at[source], gsend, grecv, **kind
+        )
+
+    def gain_share(index):
+        rows = piece_rows(index, share)
+        x = seq_ref[:, rows, :].reshape(n * share, width).astype(F32)
+        term = part_ref[:, rows, :].reshape(n * share, width).astype(F32)
+        inv = lax.rsqrt(jnp.mean(x * x, axis=1, keepdims=True) + EPS)
+        dgain_ref[...] += jnp.sum(term * x * inv, axis=0, keepdims=True)
+
+    def send_gains():
+        for device in range(n * dp):
+            cols = slice(device * per, (device + 1) * per)
+            packed[device, :, :per] = dgain_ref[:, cols]
+            packed[device, :, per : 2 * per] = dgain_mlp_ref[:, cols]
+        held[all_me] = packed[all_me]
+        exchange(start_only=True)
+
     @pl.loop(0, pieces)
     def _(piece):
         @pl.when(piece + 1 < pieces)
         def _():
             scatter.start_ends(piece + 1)
+
+        @pl.when(piece < half)
+        def _():
+            gain_share(piece)
+
+        @pl.when(piece == half)
+        def _():
+            send_gains()
 
         scatter.middle(piece)
         rows = scatter.rows(piece)
@@ -748,24 +789,17 @@
         grad = total_ref[...]
         x = x_ref[rows, :].astype(F32)
         inv = lax.rsqrt(jnp.mean(x * x, axis=1, keepdims=True) + EPS)
-        dgain_ref[...] += jnp.sum(grad * x * inv, axis=0, keepdims=True)
         scaled = grad * gain_ref[...]
         mean = jnp.mean(scaled * x, axis=1, keepdims=True)
         out = grad_mid_ref[rows, :] + inv * (scaled - x * (inv * inv * mean))
         out_ref[rows, :] = out.astype(BF16)
 
-    per = x_ref.shape[1] // (n * dp)
-    for device in range(n * dp):
-        cols = slice(device * per, (device + 1) * per)
-        packed[device, :, :per] = dgain_ref[:, cols]
-        packed[device, :, per : 2 * per] = dgain_mlp_ref[:, cols]
-    held[all_me] = packed[all_me]
-    exchange_all(n, dp, lambda peer: packed.at[peer], lambda source: held.at[source], gsend, grecv)
+    exchange(wait_only=True)
     gains_ref[...] = jnp.sum(held[...], axis=0)
     scatter.finish()
 
 
-def sum_input_grad(n, dp, part, x, gain, grad_mid, dgain_mlp, packed, pieces=8):
+def sum_input_grad(n, dp, part, x, gain, grad_mid, dgain_mlp, seq, packed, pieces=8):
     rows, width = x.shape
     any_spec = pl.BlockSpec(memory_space=pl.ANY)
     return pl.pallas_call(
@@ -774,12 +808,13 @@
             jax.ShapeDtypeStruct((rows, width), BF16),
             jax.ShapeDtypeStruct((1, packed), F32),
         ),
-        in_specs=[VMEM_SPEC] * 2 + [any_spec] * 3,
+        in_specs=[VMEM_SPEC] * 2 + [any_spec] * 4,
         out_specs=(VMEM_SPEC,) * 2,
         scratch_shapes=[
             pltpu.VMEM((n, rows, width), BF16),
             pltpu.VMEM((rows, width), BF16),
             pltpu.VMEM((rows, width), F32),
+            pltpu.VMEM((n, rows, width), BF16),
             pltpu.VMEM((rows // pieces, width), F32),
             pltpu.VMEM((1, width), F32),
             pltpu.VMEM((n * dp, 1, packed), F32),
@@ -788,11 +823,11 @@
         ]
         + sems(n, pieces)
         + [pltpu.SemaphoreType.DMA((n * dp,)), pltpu.SemaphoreType.DMA((n * dp,))]
-        + [pltpu.SemaphoreType.DMA((2 + pieces,))],
+        + [pltpu.SemaphoreType.DMA((3 + pieces,))],
         compiler_params=comm_params(4),
         cost_estimate=pl.CostEstimate(flops=0, bytes_accessed=250 * 1024 * 1024, transcendentals=0),
         name="sum_input_grad",
-    )(gain, dgain_mlp, part.reshape(n, rows, width), x, grad_mid)
+    )(gain, dgain_mlp, part.reshape(n, rows, width), x, grad_mid, seq)
 
 
 def widen_kernel(
@@ -846,7 +881,7 @@
 
 def attend_kernel(
     n, dp, heads, block, pieces, x_ref, gain_ref, cos_ref, sin_ref, cot_hbm, wq_hbm, wk_hbm, wv_hbm, wo_hbm,
-    attn_gain_ref, mlp_gain_ref, kv_ref, out_ref, log_ref, norm_hbm, qkv_hbm, part_hbm, w_out_hbm, wo_out_hbm, near_hbm,
+    attn_gain_ref, mlp_gain_ref, kv_ref, out_ref, log_ref, norm_hbm, qkv_hbm, part_hbm, w_out_hbm, wo_out_hbm, near_hbm, seq_hbm,
     norm_ref, qkv_ref, part_ref, w_ref, wo_ref, seq, act_ref, mask_ref, gains, wq, wk, wv, wo, send, recv, gsend, grecv, wsend, wrecv, own_sem, csend, crecv, fsend, frecv, save_sem,
 ):
     half = HEAD_SIZE // 2
@@ -927,7 +962,13 @@
     saves = [
         pltpu.make_async_copy(src, dst, save_sem.at[i])
         for i, (src, dst) in enumerate(
-            ((w_ref, w_out_hbm), (wo_ref, wo_out_hbm), (norm_ref, norm_hbm), (qkv_ref, qkv_hbm))
+            (
+                (w_ref, w_out_hbm),
+                (wo_ref, wo_out_hbm),
+                (norm_ref, norm_hbm),
+                (qkv_ref, qkv_hbm),
+                (seq, seq_hbm),
+            )
         )
     ]
 
@@ -938,15 +979,6 @@
         rows = piece_rows(shard, rows_all)
         norm_ref[rows, :] = norm
         act_ref[:, rows] = mm(w_ref[...], norm, 0, 1)
-
-    def project_at(hop):
-        @pl.when(me - hop >= 0)
-        def _():
-            project(me - hop)
-
-        @pl.when(me + hop <= n - 1)
-        def _():
-            project(me + hop)
 
     def prepare():
         gain_rows(wait_only=True)
@@ -968,7 +1000,6 @@
             wo_ref[:, d * w_cols : (d + 1) * w_cols] = wo[d]
         saves[0].start()
         saves[1].start()
-        project(me)
 
     def start_pair():
         for i in range(4):
@@ -990,7 +1021,7 @@
         ).wait_recv()
 
     ready = min(2, n - 1)
-    for hop in range(1, n):
+    for hop in range(1, ready + 1):
 
         @pl.loop(0, pieces)
         def _(piece):
@@ -1009,24 +1040,37 @@
         def _():
             cot_copy(False, 1).start()
 
-        if hop == ready:
-            if n == 4:
-
-                @pl.when(me == 1)
-                def _():
-                    cot_copy_in(line, near_hbm, me - 1, crecv.at[0, 0], csend.at[0, 0], -1).wait_recv()
-                    cot_copy(True, 2).start()
-
-                @pl.when(me == 2)
-                def _():
-                    cot_copy_in(line, near_hbm, me + 1, crecv.at[1, 0], csend.at[1, 0], 1).wait_recv()
-                    cot_copy(False, 2).start()
-
-            prepare()
-            for earlier in range(1, hop + 1):
-                project_at(earlier)
-        elif hop > ready:
-            project_at(hop)
+    if n == 4:
+
+        @pl.when(me == 1)
+        def _():
+            arrived(0, 1, me - 1)
+            cot_copy(True, 2).start()
+
+        @pl.when(me == 2)
+        def _():
+            arrived(1, 1, me + 1)
+            cot_copy(False, 2).start()
+
+    prepare()
+
+    @pl.loop(0, 2 * n - 1)
+    def _(turn):
+        hop = (turn + 1) // 2
+        leftward = lax.rem(turn, 2) == 1
+        shard = jnp.where(leftward, me - hop, me + hop)
+
+        @pl.when(leftward & (hop > ready))
+        def _():
+            @pl.loop(0, pieces)
+            def _(piece):
+                gather.receive(hop, piece)
+
+        @pl.when(within(shard, n))
+        def _():
+            project(shard)
+
+    saves[4].start()
 
     def far_copy(right, shard):
         part = near_hbm.at[shard, pl.ds(0, rows_all // pieces * FAR_DONE)]
@@ -1092,18 +1136,25 @@
                 mixed = term if mixed is None else mixed + term
             out_ref[pl.ds(base, HEAD_SIZE), cols] = mixed.astype(BF16)
 
-    for start, count in tiles(width, 512):
-        cols = slice(start, start + count)
+    def part_save(index):
+        cols = piece_rows(index, tile)
+        return pltpu.make_async_copy(part_ref.at[:, cols], part_hbm.at[:, cols], save_sem.at[len(saves) + index])
+
+    tile = even_tile(width)
+
+    @pl.loop(0, width // tile)
+    def _(index):
+        cols = piece_rows(index, tile)
         part_ref[:, cols] = mm(out_ref[...], wo_ref[:, cols], 0, 0).astype(BF16)
-        save = pltpu.make_async_copy(
-            part_ref.at[:, pl.ds(start, count)], part_hbm.at[:, pl.ds(start, count)], save_sem.at[len(saves)]
-        )
-        save.start()
-        saves.append(save)
+        part_save(index).start()
 
     gather.finish()
     for save in saves:
         save.wait()
+
+    @pl.loop(0, width // tile)
+    def _(index):
+        part_save(index).wait()
 
     @pl.loop(1, dp // 2)
     def _(offset):
@@ -1189,9 +1240,10 @@
             jax.ShapeDtypeStruct((width, cols_in), BF16),
             jax.ShapeDtypeStruct((q_cols, width), BF16),
             jax.ShapeDtypeStruct((n,) + cotangent.shape, BF16),
+            jax.ShapeDtypeStruct((n, rows, width), BF16),
         ),
         in_specs=[VMEM_SPEC] * 4 + [any_spec] * 5,
-        out_specs=(VMEM_SPEC,) * 5 + (any_spec,) * 6,
+        out_specs=(VMEM_SPEC,) * 5 + (any_spec,) * 7,
         scratch_shapes=[
             pltpu.VMEM((length, width), BF16),
             pltpu.VMEM((cols_in, length), BF16),
@@ -1206,7 +1258,7 @@
         + [pltpu.VMEM((dp,) + w.shape, BF16) for w in weights]
         + sems(n, pieces)
         + [dma((n * dp,)), dma((n * dp,)), dma((2, 4, dp // 2)), dma((2, 4, dp // 2)), dma((4,))]
-        + [dma((2, 2)), dma((2, 2)), dma((2,)), dma((2,)), dma((4 + len(tiles(width, 512)),))],
+        + [dma((2, 2)), dma((2, 2)), dma((2,)), dma((2,)), dma((5 + width // even_tile(width),))],
         compiler_params=comm_params(1),
         cost_estimate=pl.CostEstimate(
             flops=2 * length * width * (cols_in + q_cols),
@@ -1265,6 +1317,8 @@
     def project(shard):
         grad_ref[:, piece_rows(shard, rows_all)] = mm(wo_ref[...], seq[shard], 1, 1).astype(BF16)
 
+    tile = even_tile(width)
+
     def start_sums():
         loads[1].wait()
         loads[2].wait()
@@ -1272,11 +1326,14 @@
         @pl.loop(0, pieces)
         def _(piece):
             rows = scatter.rows(piece)
-            for start, count in tiles(width, 512):
-                cols = slice(start, start + count)
+
+            @pl.loop(0, width // tile)
+            def _(index):
+                cols = piece_rows(index, tile)
                 value = hid[:, rows, :].reshape(n * scatter.size, units)
                 value = mm(value, w_down[cols, :], 1, 1).astype(BF16)
-                down_ref[:, rows, cols] = value.reshape(n, scatter.size, count)
+                down_ref[:, rows, cols] = value.reshape(n, scatter.size, tile)
+
             scatter.start_ends(piece)
 
     def sum_piece(piece):
@@ -1354,36 +1411,40 @@
     dqkv_ref[pl.ds(heads * HEAD_SIZE, half), :] = a.astype(BF16)
     dqkv_ref[pl.ds(heads * HEAD_SIZE + half, half), :] = b.astype(BF16)
     dqkv_ref[pl.ds((heads + 1) * HEAD_SIZE, HEAD_SIZE), :] = dkv[1].T.astype(BF16)
-    saves = []
-    count_tiles = len(tiles(width, 512))
-    for index, (start, count) in enumerate(tiles(width, 512)):
-        cols = slice(start, start + count)
+
+    def part_save(index):
+        cols = piece_rows(index, tile)
+        return pltpu.make_async_copy(part_ref.at[:, cols], part_hbm.at[:, cols], save_sem.at[0, index])
+
+    def wgrad_save(index):
+        rows = piece_rows(index, tile)
+        return pltpu.make_async_copy(wgrad.at[rows, :], wgrad_hbm.at[rows, :], save_sem.at[1, index])
+
+    @pl.loop(0, width // tile)
+    def _(index):
+        cols = piece_rows(index, tile)
         part_ref[:, cols] = mm(dqkv_ref[...], w_ref[cols, :], 0, 1).astype(BF16)
-        save = pltpu.make_async_copy(
-            part_ref.at[:, pl.ds(start, count)],
-            part_hbm.at[:, pl.ds(start, count)],
-            save_sem.at[count_tiles + index],
-        )
-        save.start()
-        saves.append(save)
-    for index, (start, count) in enumerate(tiles(width, 512)):
-        cols = slice(start, start + count)
+        part_save(index).start()
+
+    @pl.loop(0, width // tile)
+    def _(index):
+        cols = piece_rows(index, tile)
         wgrad[cols, :cols_in] = mm(norm_ref[:, cols], dqkv_ref[...], 0, 1).astype(BF16)
         for shard in range(n):
             term = mm(seq[shard, :, cols], out_ref[:, shard * rows_all : (shard + 1) * rows_all], 0, 1)
             total = term if shard == 0 else total + term
         wgrad[cols, cols_in:] = total.astype(BF16)
-        save = pltpu.make_async_copy(
-            wgrad.at[pl.ds(start, count), :], wgrad_hbm.at[pl.ds(start, count), :], save_sem.at[index]
-        )
-        save.start()
-        saves.append(save)
+        wgrad_save(index).start()
+
     for piece in range(min(n, pieces) - 1, pieces):
         sum_piece(piece)
     scatter.finish()
     gather.finish(EARLY, pieces)
-    for save in saves:
-        save.wait()
+
+    @pl.loop(0, width // tile)
+    def _(index):
+        part_save(index).wait()
+        wgrad_save(index).wait()
 
 
 def attend_back(
@@ -1426,7 +1487,7 @@
             pltpu.VMEM(wgrad_shape, BF16),
         ]
         + sems(n, pieces) * 2
-        + [pltpu.SemaphoreType.DMA((9,)), pltpu.SemaphoreType.DMA((2 * len(tiles(width, 512)),))],
+        + [pltpu.SemaphoreType.DMA((9,)), pltpu.SemaphoreType.DMA((2, width // even_tile(width)))],
         compiler_params=comm_params(3),
         cost_estimate=pl.CostEstimate(
             flops=6 * length * width * wgrad_shape[1],
@@ -1452,7 +1513,7 @@
     if packed > 2 * per:
         gains.append(jnp.zeros((packed - 2 * per,), F32))
     cos, sin = tables(length)
-    full_attn, full_mlp, kv, attended, log_total, norm_attn, qkv, out_part, w_qkv, w_out_all, near = attend(
+    full_attn, full_mlp, kv, attended, log_total, norm_attn, qkv, out_part, w_qkv, w_out_all, near, x_seq = attend(
         n,
         dp,
         x,
@@ -1471,7 +1532,7 @@
     )
     attn_grad = lax.psum_scatter(attn_grad, "dp", scatter_dimension=0, tiled=True)
     input_grad, dgains = sum_input_grad(
-        n, dp, attn_part, x, full_attn, grad_mid, dgain_mlp, packed
+        n, dp, attn_part, x, full_attn, grad_mid, dgain_mlp, x_seq, packed
     )
     gate, up, down, query, key, value, out, dgain_attn, dgain_mlp, block_output, input_grad = widen(
         mlp_grad, attn_grad, dgains, block_output, input_grad, per, w_query.shape[1], w_key.shape[1]

time: 624 us -> 618 us (level); the launches traced: 616 us -> 618 us
  transfers between devices with their start and end apart: 3 -> 3, of which waited for: 1 -> 1; matrix products, arithmetic and copies ran while one was open for 0% -> 0% of each run, Pallas kernels for 33% -> 32%
where the time goes in v5:
time: 618 us
  Pallas kernels  502 us (81%)
  waiting for transfers between devices  96.3 us (16%)
  between operations  13.8 us (2%)
    pallas_call x1, Pallas kernels, mlp(): pl.pallas_call(functools.partial(mlp_kernel, n, pieces), out_shape=(jax.S...  186 us
    pallas_call x1, Pallas kernels, attend(): pl.pallas_call(functools.partial(attend_kernel, n, dp, heads, block, piec...  120 us
    pallas_call x1, Pallas kernels, attend_back(): pl.pallas_call(functools.partial(attend_back_kernel, n, heads, block, pie...  109 us
    reduce_scatter x1, waiting for transfers between devices, local(): mlp_grad = lax.psum_scatter(mlp_grad, 'dp', scatter_dimension=0, tiled=True)  95.6 us
    pallas_call x1, Pallas kernels, sum_input_grad(): pl.pallas_call(functools.partial(last_kernel, n, dp, pieces), out_shape=(...  80.1 us
  transfers between devices with their start and end apart: 3, of which 1 were waited for; matrix products, arithmetic and copies ran while one was open for 0% of the time, Pallas kernels for 32%

profile of v5, /device:TPU:0, one launch (start us, length us, event | category | flops | bytes accessed | tf_op | source)
XLA Modules:
  0.0 617.9 jit_solution(15798907125418249155)
XLA Ops:
  7.2 0.0 all-gather.2.cloned.1.call-start
  7.2 1.4 copy.22
  8.7 0.0 copy-start
  8.7 0.0 copy-start.1
  8.7 2.8 pad_maximum_fusion
  11.5 0.0 all-gather.2.cloned.1.call-update
  11.6 0.0 reduce-scatter.5.cloned.1.call-start
  11.6 0.0 copy-done
  11.6 0.0 copy-done.1
  11.7 0.6 maximum_bitcast_fusion.gain_ref
  12.2 1.2 fusion
  13.5 120.0 %attend.1 = (f32[1,2048]{1,0:T(1,128)}, f32[1,2048]{1,0:T(1,128)}, bf16[1024,128]{1,0:T(8,128)(2,1)}, bf16[512,1024]{1,0:T(8,128)(2,1)}, f32[8,1024]{1,0:T(8,128...) custom-call(bf16[256,2048]{1,0:T(8,128)(2,1)} %x_hbm.3, ...), custom_call_target="tpu_custom_call" | custom-call | flops 4831838208 | bytes 367001600 | tf_op jit(solution)/shard_map/attend/pallas_call | solution.py:1229
  133.5 0.0 all-gather.2.cloned.1.call-done.w_hbm.w_mlp_hbm
  133.5 186.3 %mlp.1 = (f32[1,2048]{1,0:T(1,128)}, f32[256,2048]{1,0:T(8,128)}, f32[256,2048]{1,0:T(8,128)}, bf16[4,256,1408]{2,1,0:T(8,128)(2,1)}, bf16[2048,4224]{1,0:T(8,128)(2,1)}, /*index=5*/bf16[4,256,2048]{2,1,0:T(8,128)(2,1)}) custom-call(f32[1,2048]{1,0:T(1,128)} %get-tuple-element.45.gain_ref, bf16[4,256,2048]{2,1,0:T(8,128)(2,1)} %bitcast.19, ...), custom_call_target="tpu_custom_call" | custom-call | flops 53150220288 | bytes 524288000 | tf_op jit(solution)/shard_map/mlp/pallas_call | solution.py:672
  319.8 109.2 %attend_back.1 = (bf16[256,2048]{1,0:T(8,128)(2,1)}, bf16[1024,2048]{1,0:T(8,128)(2,1)}, bf16[2048,1152]{1,0:T(8,128)(2,1)}) custom-call(bf16[1024,128]{1,0:T(8,128)(2,1)} %get-tuple-element.49.kv_ref, f32[8,1024]{1,0:T(8,128)} %get-tuple-element.50.log_ref, f32[32,1024]{1,0:T(8,128)} %get-tuple-element.80.cos_ref, f32[32,1024]{1,0:T(8,128)} %get-tuple-element.79.sin_ref, ...), custom_call_target="tpu_custom_call" | custom-call | flops 14495514624 | bytes 367001600 | tf_op jit(solution)/shard_map/attend_back/pallas_call | solution.py:1461
  429.0 0.0 reduce-scatter.5.cloned.1.call-update
  429.1 0.0 reduce-scatter.3.cloned.1.call-start
  429.1 0.7 reduce-scatter.3.cloned.1.call-update
  429.8 80.1 %sum_input_grad.1 = (bf16[256,2048]{1,0:T(8,128)(2,1)}, f32[1,128]{1,0:T(1,128)}) custom-call(f32[1,2048]{1,0:T(1,128)} %get-tuple-element.60.gain_ref, f32[1,2048]{1,0:T(1,128)} %get-tuple-element.61.dgain_mlp_ref, bf16[4,256,2048]{2,1,0:T(8,128)(2,1)} %bitcast.11, bf16[256,2048]{1,0:T(8,128)(2,1)} %x_hbm.3, f32[256,2048]{1,0:T(8,128)} %get-tuple-element.63.grad_mid_hbm, ...), custom_call_target="tpu_custom_call" | custom-call | bytes 262144000 | tf_op jit(solution)/shard_map/sum_input_grad/pallas_call | solution.py:805
  509.9 0.0 reduce-scatter.5.cloned.1.call-done.attn_ref
  509.9 95.6 %reduce-scatter.3.cloned.1.call-done.mlp_ref = bf16[256,4224]{1,0:T(8,128)(2,1)} async-done(((bf16[2048,4224]{1,0:T(8,128)(2,1)}), bf16[256,4224]{1,0:T(8,128)(2,1)}) %reduce-scatter.3.cloned.1.call-update) | async-done | bytes 2162704 | tf_op jit(solution)/shard_map/reduce_scatter | solution.py:1529
  605.5 5.9 widen.1
  (1 shorter events, 0.0 us)
Async XLA Ops:
  7.2 126.3 %all-gather.2.cloned.1.call-start = ((), (), s32[]{:S(2)}) async-start(), calls=%async_computation.2 | async-start | bytes 19464192 | tf_op jit(solution)/shard_map/all_gather | solution.py:1509
  8.7 3.0 copy-start
  8.7 3.0 copy-start.1
  11.6 498.4 %reduce-scatter.5.cloned.1.call-start = ((), (), s32[]{:S(2)}) async-start(), calls=%async_computation.4 | async-start | bytes 5308416 | tf_op jit(solution)/shard_map/reduce_scatter | solution.py:1533
  429.1 176.4 %reduce-scatter.3.cloned.1.call-start = ((), (), s32[]{:S(2)}) async-start(), calls=%async_computation.3 | async-start | bytes 19464192 | tf_op jit(solution)/shard_map/reduce_scatter | solution.py:1529
Sparse Core Ops, SparseCore 0:
  11.7 115.2 all-gather.1
  429.2 53.7 reduce-scatter.4
  486.6 118.8 reduce-scatter.2

commit v6 on v5

--- a/solution.py
+++ b/solution.py
@@ -18,7 +18,6 @@
 F32 = jnp.float32
 BF16 = jnp.bfloat16
 VMEM_SPEC = pl.BlockSpec(memory_space=pltpu.VMEM)
-EARLY = 0
 FAR_DONE = 3
 
 
@@ -361,7 +360,7 @@
     n, pieces, gain_ref, part_hbm, x_hbm, w_hbm, cot_hbm, near_hbm,
     dgain_ref, mid_hbm, grad_hbm, hid_hbm, wgrad_hbm, low_hbm,
     part_ref, x_ref, mid_ref, grad_ref, w, cot, seq, buf, npart, buf_back, hid, dgate, dup, stage, inv_ref,
-    ssend, srecv, gsend, grecv, bsend, brecv, csend, crecv, lsend, lrecv, local_sem, stage_sem, part_sem,
+    ssend, srecv, gsend, grecv, bsend, brecv, csend, crecv, local_sem, stage_sem, part_sem,
 ):
     line = Line(n)
     me = line.me
@@ -411,7 +410,6 @@
     gather = Gather(line, seq, gsend, grecv, pieces)
     scatter_back = Scatter(line, npart, buf_back, bsend, brecv, pieces)
     cot_gather = Gather(line, cot, csend, crecv, pieces)
-    low_gather = Gather(line, buf, lsend, lrecv, pieces)
     size = scatter.size
     part_load(0).wait()
     scatter.start_ends(0)
@@ -551,106 +549,81 @@
 
     hid_save = pltpu.make_async_copy(hid, hid_hbm, local_sem.at[2])
 
+    def receive_rows(hop, piece):
+        @pl.when(within(piece, pieces))
+        def _():
+            gather.receive(hop, piece)
+
     @pl.loop(0, pieces + n - 1)
     def _(step):
         first = step < pieces
+        ready = step - (n - 1)
+        receive_rows(n - 1, ready)
+
+        @pl.when(step + 1 < pieces)
+        def _():
+            scatter.start_ends(step + 1)
+
+        @pl.when(ready == 0)
+        def _():
+            own_load.wait()
+            weight_load.wait()
+
+        @pl.when(ready >= 0)
+        def _():
+            far_arrived(ready)
+            feed(ready)
+            scatter_back.start_ends(ready)
 
         @pl.when(first)
         def _():
-            @pl.when(step + 1 < pieces)
-            def _():
-                scatter.start_ends(step + 1)
-
             scatter.middle(step)
 
             @pl.when(step + 3 < pieces)
             def _():
                 far_start(step + 3)
 
-        for hop in range(1, n):
-            piece = step - hop
-
-            @pl.when(within(piece, pieces))
-            def _():
-                gather.receive(hop, piece)
+        for hop in range(n - 2, 1, -1):
+            receive_rows(hop, step - hop)
+
+        @pl.when(ready >= 1)
+        def _():
+            scatter_back.middle(ready - 1)
+
+        if n > 2:
+            receive_rows(1, step - 1)
 
         @pl.when(first)
         def _():
             norm(step)
             gather.start_own(step)
 
-        ready = step - (n - 1)
-
-        @pl.when(ready == 0)
-        def _():
-            own_load.wait()
-            weight_load.wait()
-
-        @pl.when(ready == 1)
+        @pl.when(ready == 2)
         def _():
             scatter.finish(ends=False)
 
-        for hop in range(1, n):
-            piece = ready - 1 - hop
-
-            @pl.when(within(piece, EARLY))
-            def _():
-                low_gather.receive(hop, piece)
-
-        @pl.when(ready >= 1)
-        def _():
-            scatter_back.middle(ready - 1)
-
-        @pl.when(ready >= 0)
-        def _():
-            far_arrived(ready)
-            feed(ready)
-            scatter_back.start_ends(ready)
-
-        @pl.when(ready >= 1)
-        def _():
-            back(ready - 1)
-
-            @pl.when(ready - 1 < EARLY)
-            def _():
-                low_gather.start_own(ready - 1)
+        @pl.when(ready >= 2)
+        def _():
+            back(ready - 2)
 
     hid_save.start()
     last = pieces - 1
 
-    def low_arrivals(step):
-        for hop in range(1, n):
-            piece = step - hop
-            if 0 <= piece < EARLY:
-                low_gather.receive(hop, piece)
-
-    late = [
-        (lambda step: lambda: low_arrivals(step))(step) for step in range(pieces - 1, pieces + n - 2)
-    ]
     events = [
         (count // 4, lambda: scatter_back.first(last)),
         (count * 5 // 8, lambda: scatter_back.rest(last)),
     ]
-    if EARLY:
-        events += [(count * (2 * i + 1) // (2 * len(late)), event) for i, event in enumerate(late)]
     weight_grads(events)
-    back(last)
-    own_rows, early_rows = pl.ds(EARLY * size, rows_all - EARLY * size), pl.ds(0, EARLY * size)
-    low_saves = [
-        pltpu.make_async_copy(buf.at[me, own_rows], low_hbm.at[me, own_rows], local_sem.at[4])
-    ]
-    if EARLY:
-        low_saves.append(
-            pltpu.make_async_copy(
-                buf.at[pl.ds(0, n), early_rows], low_hbm.at[:, early_rows], local_sem.at[0]
-            )
-        )
-    for save_low in low_saves:
-        save_low.start()
+
+    @pl.loop(max(last - 1, 0), pieces)
+    def _(piece):
+        back(piece)
+
+    low_save = pltpu.make_async_copy(buf.at[me], low_hbm, local_sem.at[4])
+    low_save.start()
     scatter.finish(middles=False)
     gather.finish()
     scatter_back.finish()
-    low_gather.finish(0, EARLY)
 
     @pl.loop(0, pieces)
     def _(piece):
@@ -658,8 +631,7 @@
         piece_save(1, mid_ref, mid_hbm, piece).wait()
         piece_save(2, grad_ref, grad_hbm, piece).wait()
 
-    for save_low in low_saves:
-        save_low.wait()
+    low_save.wait()
     hid_save.wait()
     for index in range(max(count - 2, 0), count):
         save(index, index % 2).wait()
@@ -677,7 +649,7 @@
             jax.ShapeDtypeStruct((rows, width), F32),
             jax.ShapeDtypeStruct((n, rows, units), BF16),
             jax.ShapeDtypeStruct((width, 3 * units), BF16),
-            jax.ShapeDtypeStruct((n, rows, width), BF16),
+            jax.ShapeDtypeStruct((rows, width), BF16),
         ),
         in_specs=[VMEM_SPEC] + [any_spec] * 5,
         out_specs=(VMEM_SPEC,) + (any_spec,) * 5,
@@ -698,7 +670,7 @@
             pltpu.VMEM((2, min(LANES, width), 3 * units), BF16),
             pltpu.VMEM((rows, LANES), F32),
         ]
-        + sems(n, pieces) * 5
+        + sems(n, pieces) * 4
         + [pltpu.SemaphoreType.DMA((5 + n,)), pltpu.SemaphoreType.DMA((2,)), pltpu.SemaphoreType.DMA((3, pieces))],
         compiler_params=pltpu.CompilerParams(
             collective_id=2, has_side_effects=True, vmem_limit_bytes=67043328
@@ -1282,10 +1254,8 @@
     cols_in = qkv_ref.shape[0]
     scale = 1.0 / math.sqrt(HEAD_SIZE)
     me = lax.axis_index("tensor")
-    size = rows_all // pieces
-    own_rows, early_rows = pl.ds(EARLY * size, rows_all - EARLY * size), pl.ds(0, EARLY * size)
     pairs = (
-        (low_hbm.at[me, own_rows], seq.at[me, own_rows]),
+        (low_hbm, seq.at[me]),
         (hid_hbm, hid),
         (w_mlp_hbm.at[:, pl.ds(2 * units, units)], w_down),
         (wo_hbm, wo_ref),
@@ -1295,8 +1265,6 @@
         (norm_hbm, norm_ref),
         (mid_hbm, mid_ref),
     )
-    if EARLY:
-        pairs += ((low_hbm.at[:, early_rows], seq.at[:, early_rows]),)
     loads = [pltpu.make_async_copy(src, dst, load_sem.at[i]) for i, (src, dst) in enumerate(pairs)]
     for load in loads:
         load.start()
@@ -1306,7 +1274,7 @@
     gather = Gather(line, seq, gsend, grecv, pieces)
     loads[0].wait()
 
-    @pl.loop(EARLY, pieces)
+    @pl.loop(0, pieces)
     def _(piece):
         gather.start_own(piece)
 
@@ -1389,7 +1357,7 @@
 
         @pl.when(leftward)
         def _():
-            @pl.loop(EARLY, pieces)
+            @pl.loop(0, pieces)
             def _(piece):
                 gather.receive(hop, piece)
 
@@ -1439,7 +1407,7 @@
     for piece in range(min(n, pieces) - 1, pieces):
         sum_piece(piece)
     scatter.finish()
-    gather.finish(EARLY, pieces)
+    gather.finish()
 
     @pl.loop(0, width // tile)
     def _(index):

time: 618 us -> 609 us (0.985)
  Pallas kernels: 502 us -> 495 us
    pallas_call x1, Pallas kernels: 186 us -> 171 us  [mlp(): pl.pallas_call(functools.partial(mlp_kernel, n, pieces), out_shape=(jax.S...]
    pallas_call x1, Pallas kernels: 109 us -> 119 us  [attend_back(): pl.pallas_call(functools.partial(attend_back_kernel, n, heads, block, pie...]
  transfers between devices with their start and end apart: 3 -> 3, of which waited for: 1 -> 1; matrix products, arithmetic and copies ran while one was open for 0% -> 0% of each run, Pallas kernels for 32% -> 33%
where the time goes in v6:
time: 609 us
  Pallas kernels  495 us (81%)
  waiting for transfers between devices  94.1 us (15%)
  between operations  13.8 us (2%)
    pallas_call x1, Pallas kernels, mlp(): pl.pallas_call(functools.partial(mlp_kernel, n, pieces), out_shape=(jax.S...  171 us
    pallas_call x1, Pallas kernels, attend(): pl.pallas_call(functools.partial(attend_kernel, n, dp, heads, block, piec...  120 us
    pallas_call x1, Pallas kernels, attend_back(): pl.pallas_call(functools.partial(attend_back_kernel, n, heads, block, pie...  119 us
    reduce_scatter x1, waiting for transfers between devices, local(): mlp_grad = lax.psum_scatter(mlp_grad, 'dp', scatter_dimension=0, tiled=True)  93.3 us
    pallas_call x1, Pallas kernels, sum_input_grad(): pl.pallas_call(functools.partial(last_kernel, n, dp, pieces), out_shape=(...  79.1 us
  transfers between devices with their start and end apart: 3, of which 1 were waited for; matrix products, arithmetic and copies ran while one was open for 0% of the time, Pallas kernels for 33%

profile of v6, /device:TPU:0, one launch (start us, length us, event | category | flops | bytes accessed | tf_op | source)
XLA Modules:
  0.0 609.0 jit_solution(2166650699282526625)
XLA Ops:
  7.2 0.0 all-gather.2.cloned.1.call-start
  7.2 1.4 copy.22
  8.7 0.0 copy-start
  8.7 0.0 copy-start.1
  8.7 2.8 pad_maximum_fusion
  11.5 0.0 all-gather.2.cloned.1.call-update
  11.6 0.0 reduce-scatter.5.cloned.1.call-start
  11.6 0.0 copy-done
  11.6 0.0 copy-done.1
  11.7 0.6 maximum_bitcast_fusion.gain_ref
  12.2 1.2 fusion
  13.5 120.0 %attend.1 = (f32[1,2048]{1,0:T(1,128)}, f32[1,2048]{1,0:T(1,128)}, bf16[1024,128]{1,0:T(8,128)(2,1)}, bf16[512,1024]{1,0:T(8,128)(2,1)}, f32[8,1024]{1,0:T(8,128...) custom-call(bf16[256,2048]{1,0:T(8,128)(2,1)} %x_hbm.3, ...), custom_call_target="tpu_custom_call" | custom-call | flops 4831838208 | bytes 367001600 | tf_op jit(solution)/shard_map/attend/pallas_call | solution.py:1201
  133.5 0.0 all-gather.2.cloned.1.call-done.w_hbm.w_mlp_hbm
  133.5 170.6 %mlp.1 = (f32[1,2048]{1,0:T(1,128)}, f32[256,2048]{1,0:T(8,128)}, f32[256,2048]{1,0:T(8,128)}, bf16[4,256,1408]{2,1,0:T(8,128)(2,1)}, bf16[2048,4224]{1,0:T(8,128)(2,1)}, /*index=5*/bf16[256,2048]{1,0:T(8,128)(2,1)}) custom-call(f32[1,2048]{1,0:T(1,128)} %get-tuple-element.45.gain_ref, bf16[4,256,2048]{2,1,0:T(8,128)(2,1)} %bitcast.19, ...), custom_call_target="tpu_custom_call" | custom-call | flops 53150220288 | bytes 524288000 | tf_op jit(solution)/shard_map/mlp/pallas_call | solution.py:644
  304.1 119.2 %attend_back.1 = (bf16[256,2048]{1,0:T(8,128)(2,1)}, bf16[1024,2048]{1,0:T(8,128)(2,1)}, bf16[2048,1152]{1,0:T(8,128)(2,1)}) custom-call(bf16[1024,128]{1,0:T(8,128)(2,1)} %get-tuple-element.49.kv_ref, f32[8,1024]{1,0:T(8,128)} %get-tuple-element.50.log_ref, f32[32,1024]{1,0:T(8,128)} %get-tuple-element.80.cos_ref, f32[32,1024]{1,0:T(8,128)} %get-tuple-element.79.sin_ref, ...), custom_call_target="tpu_custom_call" | custom-call | flops 14495514624 | bytes 367001600 | tf_op jit(solution)/shard_map/attend_back/pallas_call | solution.py:1429
  423.3 0.0 reduce-scatter.5.cloned.1.call-update
  423.3 0.0 reduce-scatter.3.cloned.1.call-start
  423.4 0.7 reduce-scatter.3.cloned.1.call-update
  424.1 79.1 %sum_input_grad.1 = (bf16[256,2048]{1,0:T(8,128)(2,1)}, f32[1,128]{1,0:T(1,128)}) custom-call(f32[1,2048]{1,0:T(1,128)} %get-tuple-element.60.gain_ref, f32[1,2048]{1,0:T(1,128)} %get-tuple-element.61.dgain_mlp_ref, bf16[4,256,2048]{2,1,0:T(8,128)(2,1)} %bitcast.11, bf16[256,2048]{1,0:T(8,128)(2,1)} %x_hbm.3, f32[256,2048]{1,0:T(8,128)} %get-tuple-element.63.grad_mid_hbm, ...), custom_call_target="tpu_custom_call" | custom-call | bytes 262144000 | tf_op jit(solution)/shard_map/sum_input_grad/pallas_call | solution.py:777
  503.2 0.0 reduce-scatter.5.cloned.1.call-done.attn_ref
  503.2 93.3 %reduce-scatter.3.cloned.1.call-done.mlp_ref = bf16[256,4224]{1,0:T(8,128)(2,1)} async-done(((bf16[2048,4224]{1,0:T(8,128)(2,1)}), bf16[256,4224]{1,0:T(8,128)(2,1)}) %reduce-scatter.3.cloned.1.call-update) | async-done | bytes 2162704 | tf_op jit(solution)/shard_map/reduce_scatter | solution.py:1497
  596.6 5.9 widen.1
  (1 shorter events, 0.0 us)
Async XLA Ops:
  7.2 126.3 %all-gather.2.cloned.1.call-start = ((), (), s32[]{:S(2)}) async-start(), calls=%async_computation.2 | async-start | bytes 19464192 | tf_op jit(solution)/shard_map/all_gather | solution.py:1477
  8.7 3.0 copy-start
  8.7 3.0 copy-start.1
  11.6 491.6 %reduce-scatter.5.cloned.1.call-start = ((), (), s32[]{:S(2)}) async-start(), calls=%async_computation.4 | async-start | bytes 5308416 | tf_op jit(solution)/shard_map/reduce_scatter | solution.py:1501
  423.3 173.2 %reduce-scatter.3.cloned.1.call-start = ((), (), s32[]{:S(2)}) async-start(), calls=%async_computation.3 | async-start | bytes 19464192 | tf_op jit(solution)/shard_map/reduce_scatter | solution.py:1497
Sparse Core Ops, SparseCore 0:
  11.7 115.2 all-gather.1
  423.5 50.5 reduce-scatter.4
  477.7 118.7 reduce-scatter.2

commit v7 on v6

--- a/solution.py
+++ b/solution.py
@@ -18,7 +18,7 @@
 F32 = jnp.float32
 BF16 = jnp.bfloat16
 VMEM_SPEC = pl.BlockSpec(memory_space=pltpu.VMEM)
-FAR_DONE = 3
+FAR_DONE = 2
 
 
 def tables(sequence_length):
@@ -451,7 +451,7 @@
             def _():
                 cot_gather.message(False, hop, piece, me + hop).wait_recv()
 
-    for piece in range(min(3, pieces)):
+    for piece in range(min(2, pieces)):
         far_start(jnp.int32(piece))
 
     def norm(piece):
@@ -579,9 +579,9 @@
         def _():
             scatter.middle(step)
 
-            @pl.when(step + 3 < pieces)
+            @pl.when(step + 2 < pieces)
             def _():
-                far_start(step + 3)
+                far_start(step + 2)
 
         for hop in range(n - 2, 1, -1):
             receive_rows(hop, step - hop)

time: 609 us -> 605 us (level)
    pallas_call x1, Pallas kernels: 119 us -> 112 us  [attend_back(): pl.pallas_call(functools.partial(attend_back_kernel, n, heads, block, pie...]
    pallas_call x1, Pallas kernels: 171 us -> 177 us  [mlp(): pl.pallas_call(functools.partial(mlp_kernel, n, pieces), out_shape=(jax.S...]
  transfers between devices with their start and end apart: 3 -> 3, of which waited for: 1 -> 1; matrix products, arithmetic and copies ran while one was open for 0% -> 0% of each run, Pallas kernels for 33% -> 32%
where the time goes in v7:
time: 605 us
  Pallas kernels  490 us (81%)
  waiting for transfers between devices  95.1 us (16%)
  between operations  13.8 us (2%)
    pallas_call x1, Pallas kernels, mlp(): pl.pallas_call(functools.partial(mlp_kernel, n, pieces), out_shape=(jax.S...  177 us
    pallas_call x1, Pallas kernels, attend(): pl.pallas_call(functools.partial(attend_kernel, n, dp, heads, block, piec...  114 us
    pallas_call x1, Pallas kernels, attend_back(): pl.pallas_call(functools.partial(attend_back_kernel, n, heads, block, pie...  112 us
    reduce_scatter x1, waiting for transfers between devices, local(): mlp_grad = lax.psum_scatter(mlp_grad, 'dp', scatter_dimension=0, tiled=True)  94.4 us
    pallas_call x1, Pallas kernels, sum_input_grad(): pl.pallas_call(functools.partial(last_kernel, n, dp, pieces), out_shape=(...  80.2 us
  transfers between devices with their start and end apart: 3, of which 1 were waited for; matrix products, arithmetic and copies ran while one was open for 0% of the time, Pallas kernels for 32%

profile of v7, /device:TPU:0, one launch (start us, length us, event | category | flops | bytes accessed | tf_op | source)
XLA Modules:
  0.0 605.0 jit_solution(12585827237495181054)
XLA Ops:
  7.2 0.0 all-gather.2.cloned.1.call-start
  7.2 1.4 copy.22
  8.7 0.0 copy-start
  8.7 0.0 copy-start.1
  8.7 2.8 pad_maximum_fusion
  11.5 0.0 all-gather.2.cloned.1.call-update
  11.6 0.0 reduce-scatter.5.cloned.1.call-start
  11.6 0.0 copy-done
  11.6 0.0 copy-done.1
  11.7 0.6 maximum_bitcast_fusion.gain_ref
  12.2 1.2 fusion
  13.5 114.4 %attend.1 = (f32[1,2048]{1,0:T(1,128)}, f32[1,2048]{1,0:T(1,128)}, bf16[1024,128]{1,0:T(8,128)(2,1)}, bf16[512,1024]{1,0:T(8,128)(2,1)}, f32[8,1024]{1,0:T(8,128...) custom-call(bf16[256,2048]{1,0:T(8,128)(2,1)} %x_hbm.3, ...), custom_call_target="tpu_custom_call" | custom-call | flops 4831838208 | bytes 367001600 | tf_op jit(solution)/shard_map/attend/pallas_call | solution.py:1201
  127.9 0.0 all-gather.2.cloned.1.call-done.w_hbm.w_mlp_hbm
  127.9 177.0 %mlp.1 = (f32[1,2048]{1,0:T(1,128)}, f32[256,2048]{1,0:T(8,128)}, f32[256,2048]{1,0:T(8,128)}, bf16[4,256,1408]{2,1,0:T(8,128)(2,1)}, bf16[2048,4224]{1,0:T(8,128)(2,1)}, /*index=5*/bf16[256,2048]{1,0:T(8,128)(2,1)}) custom-call(f32[1,2048]{1,0:T(1,128)} %get-tuple-element.45.gain_ref, bf16[4,256,2048]{2,1,0:T(8,128)(2,1)} %bitcast.19, ...), custom_call_target="tpu_custom_call" | custom-call | flops 53150220288 | bytes 524288000 | tf_op jit(solution)/shard_map/mlp/pallas_call | solution.py:644
  304.9 112.3 %attend_back.1 = (bf16[256,2048]{1,0:T(8,128)(2,1)}, bf16[1024,2048]{1,0:T(8,128)(2,1)}, bf16[2048,1152]{1,0:T(8,128)(2,1)}) custom-call(bf16[1024,128]{1,0:T(8,128)(2,1)} %get-tuple-element.49.kv_ref, f32[8,1024]{1,0:T(8,128)} %get-tuple-element.50.log_ref, f32[32,1024]{1,0:T(8,128)} %get-tuple-element.80.cos_ref, f32[32,1024]{1,0:T(8,128)} %get-tuple-element.79.sin_ref, ...), custom_call_target="tpu_custom_call" | custom-call | flops 14495514624 | bytes 367001600 | tf_op jit(solution)/shard_map/attend_back/pallas_call | solution.py:1429
  417.2 0.0 reduce-scatter.5.cloned.1.call-update
  417.3 0.0 reduce-scatter.3.cloned.1.call-start
  417.3 0.7 reduce-scatter.3.cloned.1.call-update
  418.0 80.2 %sum_input_grad.1 = (bf16[256,2048]{1,0:T(8,128)(2,1)}, f32[1,128]{1,0:T(1,128)}) custom-call(f32[1,2048]{1,0:T(1,128)} %get-tuple-element.60.gain_ref, f32[1,2048]{1,0:T(1,128)} %get-tuple-element.61.dgain_mlp_ref, bf16[4,256,2048]{2,1,0:T(8,128)(2,1)} %bitcast.11, bf16[256,2048]{1,0:T(8,128)(2,1)} %x_hbm.3, f32[256,2048]{1,0:T(8,128)} %get-tuple-element.63.grad_mid_hbm, ...), custom_call_target="tpu_custom_call" | custom-call | bytes 262144000 | tf_op jit(solution)/shard_map/sum_input_grad/pallas_call | solution.py:777
  498.2 0.0 reduce-scatter.5.cloned.1.call-done.attn_ref
  498.2 94.4 %reduce-scatter.3.cloned.1.call-done.mlp_ref = bf16[256,4224]{1,0:T(8,128)(2,1)} async-done(((bf16[2048,4224]{1,0:T(8,128)(2,1)}), bf16[256,4224]{1,0:T(8,128)(2,1)}) %reduce-scatter.3.cloned.1.call-update) | async-done | bytes 2162704 | tf_op jit(solution)/shard_map/reduce_scatter | solution.py:1497
  592.6 5.9 widen.1
  (1 shorter events, 0.0 us)
Async XLA Ops:
  7.2 120.7 %all-gather.2.cloned.1.call-start = ((), (), s32[]{:S(2)}) async-start(), calls=%async_computation.2 | async-start | bytes 19464192 | tf_op jit(solution)/shard_map/all_gather | solution.py:1477
  8.7 3.0 copy-start
  8.7 3.0 copy-start.1
  11.6 486.6 %reduce-scatter.5.cloned.1.call-start = ((), (), s32[]{:S(2)}) async-start(), calls=%async_computation.4 | async-start | bytes 5308416 | tf_op jit(solution)/shard_map/reduce_scatter | solution.py:1501
  417.3 175.3 %reduce-scatter.3.cloned.1.call-start = ((), (), s32[]{:S(2)}) async-start(), calls=%async_computation.3 | async-start | bytes 19464192 | tf_op jit(solution)/shard_map/reduce_scatter | solution.py:1497
Sparse Core Ops, SparseCore 0:
  11.7 115.2 all-gather.1
  417.4 52.6 reduce-scatter.4
  473.7 118.8 reduce-scatter.2
